TPU v7x, 8 devices: a whole 2x2x1 slice. The times are simulated.
8 devices in a mesh: dp: 1 (over z), sp: 8 (over y, x, core).
Axes of the slice: x: 2, y: 2, z: 1, core: 2. Of those that a mesh axis runs over, the one named last changes fastest.
Arguments:
- hidden: bfloat16 [16, 512, 4096], P('dp', 'sp')
- positions: int32 [512], P(('dp', 'sp'))
- long_factor: float32 [64], replicated
- norm_weight: float32 [4096], replicated
- w_qkv: bfloat16 [4096, 6144], replicated
- w_out: bfloat16 [4096, 4096], replicated
- grad_out: bfloat16 [16, 512, 4096], P('dp', 'sp')
Outputs:
- output 1: bfloat16 [16, 512, 4096], P('dp', 'sp')
- output 2: bfloat16 [16, 512, 4096], P('dp', 'sp')
- output 3: float32 [4096], P('dp')
- output 4: float32 [4096, 6144], P('dp')
- output 5: float32 [4096, 4096], P('dp')
All inputs are finite; a program needn't handle non-finite values.
Results may differ from a plain program's by a relative error of at most 0.0115151.
Values are sent between devices in bfloat16 or wider.
A program may use at most 1.25 GiB of HBM per device.

v0:
```python
import math
import jax
import jax.numpy as jnp
from jax import lax
from jax.sharding import PartitionSpec as P, NamedSharding

NORM_EPS = 1e-5
ROPE_BASE = 10000.0
ROPE_SCALE = math.sqrt(1.0 + math.log(32.0) / math.log(4096.0))


def rotate_half(head_vals):
    half_dim = head_vals.shape[-1] // 2
    return jnp.concatenate([-head_vals[..., half_dim:], head_vals[..., :half_dim]], axis=-1)


def rope_tables(positions, long_factor):
    head_dim = 2 * long_factor.shape[0]
    exponents = jnp.arange(0, head_dim, 2).astype(jnp.float32) / head_dim
    inv_freq = 1.0 / (long_factor * ROPE_BASE ** exponents)
    angles = positions.astype(jnp.float32)[..., None] * inv_freq
    cos_half = jnp.cos(angles) * ROPE_SCALE
    sin_half = jnp.sin(angles) * ROPE_SCALE
    return jnp.concatenate([cos_half, cos_half], axis=-1), jnp.concatenate([sin_half, sin_half], axis=-1)


def apply_rope(head_vals, cos_full, sin_full):
    vals_wide = head_vals.astype(jnp.float32)
    return (vals_wide * cos_full + rotate_half(vals_wide) * sin_full).astype(jnp.bfloat16)


def rope_back(grad_vals, cos_full, sin_full):
    grad_wide = grad_vals.astype(jnp.float32)
    return (grad_wide * cos_full - rotate_half(grad_wide * sin_full)).astype(jnp.bfloat16)


def norm_forward(hidden, norm_weight):
    hidden_wide = hidden.astype(jnp.float32)
    inv_rms = lax.rsqrt(jnp.mean(hidden_wide * hidden_wide, axis=-1, keepdims=True) + NORM_EPS)
    unit_hidden = hidden_wide * inv_rms
    return hidden_wide, inv_rms, unit_hidden, (unit_hidden * norm_weight).astype(jnp.bfloat16)


def norm_backward(grad_normed, grad_out, norm_weight, inv_rms, unit_hidden):
    grad_unit = grad_normed * norm_weight
    grad_inner = inv_rms * (grad_unit - unit_hidden * jnp.mean(grad_unit * unit_hidden, axis=-1, keepdims=True))
    return (grad_out.astype(jnp.float32) + grad_inner).astype(jnp.bfloat16)


def attention_forward(query_grp, key_all, value_all, causal):
    score_scale = query_grp.shape[-1] ** -0.5
    scores = jnp.einsum('bqkgd,bskd->bkgqs', query_grp, key_all, preferred_element_type=jnp.float32) * score_scale
    attn_probs = jax.nn.softmax(jnp.where(causal, scores, -jnp.inf), axis=-1)
    probs_low = attn_probs.astype(jnp.bfloat16)
    attn_grp = jnp.einsum('bkgqs,bskd->bqkgd', probs_low, value_all, preferred_element_type=jnp.float32).astype(jnp.bfloat16)
    return attn_grp, attn_probs, probs_low


def attention_backward(grad_grp, query_grp, key_all, value_all, attn_probs, probs_low):
    score_scale = query_grp.shape[-1] ** -0.5
    grad_probs = jnp.einsum('bqkgd,bskd->bkgqs', grad_grp, value_all, preferred_element_type=jnp.float32).astype(jnp.bfloat16)
    row_dot = jnp.sum(grad_probs * attn_probs, axis=-1, keepdims=True)
    grad_scores = (attn_probs * (grad_probs - row_dot) * score_scale).astype(jnp.bfloat16)
    grad_value = jnp.einsum('bkgqs,bqkgd->bskd', probs_low, grad_grp, preferred_element_type=jnp.float32)
    grad_key = jnp.einsum('bkgqs,bqkgd->bskd', grad_scores, query_grp, preferred_element_type=jnp.float32)
    grad_query = jnp.einsum('bkgqs,bskd->bqkgd', grad_scores, key_all, preferred_element_type=jnp.float32).astype(jnp.bfloat16)
    return grad_query, grad_key, grad_value


def block_body(hidden, positions, long_factor, norm_weight, w_qkv, w_out, grad_out):
    batch_size, seq_local, model_dim = hidden.shape
    head_dim = 2 * long_factor.shape[0]
    query_dim = w_out.shape[0]
    kv_dim = (w_qkv.shape[1] - query_dim) // 2
    num_heads = query_dim // head_dim
    kv_heads = kv_dim // head_dim
    group_size = num_heads // kv_heads
    cos_full, sin_full = rope_tables(positions, long_factor)
    cos_full = cos_full[:, None, :]
    sin_full = sin_full[:, None, :]
    hidden_wide, inv_rms, unit_hidden, normed = norm_forward(hidden, norm_weight)
    qkv_proj = jnp.einsum('bsd,de->bse', normed, w_qkv, preferred_element_type=jnp.float32).astype(jnp.bfloat16)
    query_rot = apply_rope(qkv_proj[..., :query_dim].reshape(batch_size, seq_local, num_heads, head_dim), cos_full, sin_full)
    key_rot = apply_rope(qkv_proj[..., query_dim:query_dim + kv_dim].reshape(batch_size, seq_local, kv_heads, head_dim), cos_full, sin_full)
    value_loc = qkv_proj[..., query_dim + kv_dim:].reshape(batch_size, seq_local, kv_heads, head_dim)
    query_heads = lax.all_to_all(query_rot, 'sp', 2, 1, tiled=True)
    key_heads = lax.all_to_all(key_rot, 'sp', 2, 1, tiled=True)
    value_heads = lax.all_to_all(value_loc, 'sp', 2, 1, tiled=True)
    seq_len = query_heads.shape[1]
    kv_local = key_heads.shape[2]
    query_grp = query_heads.reshape(batch_size, seq_len, kv_local, group_size, head_dim)
    row_ids = lax.broadcasted_iota(jnp.int32, (seq_len, seq_len), 0)
    col_ids = lax.broadcasted_iota(jnp.int32, (seq_len, seq_len), 1)
    attn_grp, attn_probs, probs_low = attention_forward(query_grp, key_heads, value_heads, row_ids >= col_ids)
    attn_back = lax.all_to_all(attn_grp.reshape(batch_size, seq_len, kv_local * group_size, head_dim), 'sp', 1, 2, tiled=True)
    attn_flat = attn_back.reshape(batch_size, seq_local, query_dim)
    mixed_out = jnp.einsum('bse,ed->bsd', attn_flat, w_out, preferred_element_type=jnp.float32)
    out_hidden = (hidden_wide + mixed_out).astype(jnp.bfloat16)

    grad_wout = jnp.einsum('bse,bsd->ed', attn_flat, grad_out, preferred_element_type=jnp.float32)
    grad_attn = jnp.einsum('bsd,ed->bse', grad_out, w_out, preferred_element_type=jnp.float32).astype(jnp.bfloat16)
    grad_heads = lax.all_to_all(grad_attn.reshape(batch_size, seq_local, num_heads, head_dim), 'sp', 2, 1, tiled=True)
    grad_grp = grad_heads.reshape(batch_size, seq_len, kv_local, group_size, head_dim)
    grad_query, grad_key, grad_value = attention_backward(grad_grp, query_grp, key_heads, value_heads, attn_probs, probs_low)
    grad_query_loc = lax.all_to_all(grad_query.reshape(batch_size, seq_len, kv_local * group_size, head_dim), 'sp', 1, 2, tiled=True)
    grad_key_loc = lax.all_to_all(grad_key.astype(jnp.bfloat16), 'sp', 1, 2, tiled=True)
    grad_value_loc = lax.all_to_all(grad_value.astype(jnp.bfloat16), 'sp', 1, 2, tiled=True)
    grad_qkv = jnp.concatenate([
        rope_back(grad_query_loc, cos_full, sin_full).reshape(batch_size, seq_local, query_dim),
        rope_back(grad_key_loc, cos_full, sin_full).reshape(batch_size, seq_local, kv_dim),
        grad_value_loc.reshape(batch_size, seq_local, kv_dim)], axis=-1)
    grad_wqkv = jnp.einsum('bsd,bse->de', normed, grad_qkv, preferred_element_type=jnp.float32)
    grad_normed = jnp.einsum('bse,de->bsd', grad_qkv, w_qkv, preferred_element_type=jnp.float32).astype(jnp.bfloat16)
    grad_norm = jnp.sum(grad_normed * unit_hidden, axis=(0, 1))
    grad_hidden = norm_backward(grad_normed, grad_out, norm_weight, inv_rms, unit_hidden)
    return out_hidden, grad_hidden, lax.psum(grad_norm, 'sp'), lax.psum(grad_wqkv, 'sp'), lax.psum(grad_wout, 'sp')


def solution(mesh):
    token_spec = P('dp', 'sp', None)
    return jax.shard_map(block_body, mesh=mesh,
                         in_specs=(token_spec, P(('dp', 'sp')), P(), P(), P(), P(), token_spec),
                         out_specs=(token_spec, token_spec, P('dp'), P('dp', None), P('dp', None)),
                         check_vma=False)
```

profile of v0, /device:TPU:0, one launch (start us, length us, event | category | flops | bytes accessed | tf_op | source)
XLA Modules:
  0.0 2638.9 jit_solution(17220510569803555934)
XLA Ops:
  7.2 5.1 fusion.34
  12.3 60.4 %fusion.39 = bf16[16,64,6144]{2,1,0:T(8,128)(2,1)} fusion(bf16[4096,6144]{1,0:T(8,128)(2,1)} %param.11, bf16[16,64,4096]{2,1,0:T(8,128)(2,1)} %param.7, f32[4096]{0:T(1024)} %param.10, f32[16,64]{1,0:T(8,128)S(1)} %add_rsqrt_fusion), kind=kOutput, calls=%fused_computation.58 | convolution fusion | flops 51562676224 | bytes 71323648 | tf_op jit(solution)/shard_map/bsd,de->bse/dot_general | solution.py:82
  72.6 5.1 convert_bitcast_fusion.8
  92.0 11.8 copy_bitcast_fusion
  103.8 7.0 all-to-all-done
  113.9 20.1 slice_negate_fusion.1
  134.0 13.3 fusion.38
  147.3 9.8 copy.90
  161.0 42.5 %convert_bitcast_fusion.4 = bf16[16,8,32,8,128]{4,3,2,1,0:T(8,128)(2,1)} fusion(bf16[16,64,4096]{2,1,0:T(8,128)(2,1)} %param.13, bf16[4096,4096]{1,0:T(8,128)(2,1)} %param.12), kind=kOutput, calls=%fused_computation.61 | convolution fusion | flops 34363932672 | bytes 50331648 | tf_op jit(solution)/shard_map/bsd,ed->bse/dot_general | solution.py:101
  203.5 9.4 copy.153
  216.5 38.5 %all-to-all-done.2 = bf16[16,64,32,128]{3,1,0,2:T(8,128)(2,1)} async-done(((bf16[16,64,32,128]{3,1,0,2:T(8,128)(2,1)}), bf16[16,64,32,128]{3,1,0,2:T(8,128)(2,1)}, u32[]{:S(2)}, u32[]{:S(2)}) %all-to-all-start.2) | async-done | bytes 8388640 | tf_op jit(solution)/shard_map/all_to_all | solution.py:86
  259.1 9.8 copy.91
  268.9 27.0 %fusion.8 = (f32[16,4,512]{2,1,0:T(4,128)S(1)}, f32[16,512,512,4]{2,1,3,0:T(8,128)}) fusion(pred[512,512]{0,1:T(8,128)(4,1)S(1)} %iota_compare_fusion, bf16[16,512,128,1]{2,1,3,0:T(8,128)(2,1)S(1)} %bitcast.240, bf16[16,512,4,128]{3,1,2,0:T(8,128)(2,1)} %bitcast.233), kind=kOutput, calls=%fused_computation.12 | convolution fusion | flops 4345266176 | bytes 77987840 | tf_op jit(solution)/shard_map/bqkgd,bskd->bkgqs/dot_general | solution.py:52
  296.0 21.8 fusion.7
  317.8 28.5 %convert_bitcast_fusion.5 = bf16[16,512,4,128]{1,3,2,0:T(8,128)(2,1)} fusion(bf16[16,512,128,1]{2,1,3,0:T(8,128)(2,1)S(1)} %bitcast.250, f32[16,4,512]{2,1,0:T(4,128)S(1)} %fusion.7, f32[16,4,512]{2,1,0:T(4,128)S(1)} %get-tuple-element.19, f32[16,512,512,4]{2,1,3,0:T(8,128)} %get-tuple-element.20, pred[512,512]{0,1:T(8,128)(4,1)S(1)} %iota_compare_fusion), kind=kOutput, calls=%fused_computation.62 | convolution fusion | flops 4383047680 | bytes 78118912 | tf_op jit(solution)/shard_map/bkgqs,bskd->bqkgd/dot_general | solution.py:55
  346.2 14.6 copy.94
  364.7 9.8 copy.98
  374.5 29.9 %fusion.60 = bf16[16,512,1,128]{1,3,0,2:T(8,128)(2,1)} fusion(bf16[16,512,4,128]{3,1,2,0:T(8,128)(2,1)} %bitcast.244, f32[16,4,512]{2,1,0:T(4,128)S(1)} %fusion.7, f32[16,4,512]{2,1,0:T(4,128)S(1)} %get-tuple-element.19, f32[16,512,512,4]{2,1,3,0:T(8,128)} %get-tuple-element.20, pred[512,512]{0,1:T(8,128)(4,1)S(1)} %iota_compare_fusion), kind=kOutput, calls=%fused_computation.83 | convolution fusion | flops 4379901952 | bytes 78118912 | tf_op jit(solution)/shard_map/bkgqs,bqkgd->bskd/dot_general | solution.py:64
  409.0 42.8 %fusion.2 = (f32[16,4,512]{2,1,0:T(4,128)}, bf16[16,512,512,4]{2,1,3,0:T(8,128)(2,1)}) fusion(f32[16,4,512]{2,1,0:T(4,128)S(1)} %fusion.7, f32[16,4,512]{2,1,0:T(4,128)S(1)} %get-tuple-element.19, f32[16,512,512,4]{2,1,3,0:T(8,128)} %get-tuple-element.20, pred[512,512]{0,1:T(8,128)(4,1)S(1)} %iota_compare_fusion, ...), kind=kOutput, calls=%fused_computation.4 | convolution fusion | flops 4429152256 | bytes 111804416 | tf_op jit(solution)/shard_map/bqkgd,bskd->bkgqs/dot_general | solution.py:61
  451.8 6.9 all-to-all-done.3
  461.9 12.2 copy.95
  474.1 11.5 copy.96
  485.6 14.4 reshape.149
  500.0 46.0 %convolution_bitcast_fusion.1 = f32[4096,4096]{1,0:T(8,128)} fusion(bf16[16,64,4096]{2,1,0:T(8,128)(2,1)} %reshape.149, bf16[16,64,4096]{2,1,0:T(8,128)(2,1)} %param.13), kind=kOutput, calls=%fused_computation.17 | convolution fusion | flops 34359738368 | bytes 83886080 | tf_op jit(solution)/shard_map/bse,bsd->ed/dot_general | solution.py:100
  547.2 44.1 %fusion.13 = bf16[16,4,512,512]{2,3,1,0:T(8,128)(2,1)} fusion(bf16[16,512,512,4]{2,1,3,0:T(8,128)(2,1)} %get-tuple-element.22, f32[16,4,512]{2,1,0:T(4,128)S(1)} %copy-done.20, f32[16,4,512]{2,1,0:T(4,128)S(1)} %copy-done.19, f32[16,4,512]{2,1,0:T(4,128)S(1)} %copy-done.13, f32[16,512,512,4]{2,1,3,0:T(8,128)} %get-tuple-element.20, ...), kind=kLoop, calls=%fused_computation.18 | loop fusion | flops 150994944 | bytes 134873088 | tf_op jit(solution)/shard_map/reshape.28
  591.3 18.7 fusion.59
  617.5 16.6 convert_bitcast_fusion.3
  634.1 14.5 copy.101
  648.6 18.0 all-to-all-done.6
  680.0 5.3 copy.110
  694.2 134.9 %all-to-all-done.5 = bf16[16,512,4,128]{3,2,0,1:T(4,128)(2,1)} async-done(((bf16[16,512,4,128]{3,2,0,1:T(4,128)(2,1)}), bf16[16,512,4,128]{3,2,0,1:T(4,128)(2,1)}, u32[]{:S(2)}, u32[]{:S(2)}) %all-to-all-start.5) | async-done | bytes 8388640 | tf_op jit(solution)/shard_map/all_to_all | solution.py:105
  829.1 12.2 copy.102
  841.3 11.8 convert_bitcast_fusion.1
  853.0 22.1 copy.103
  875.2 6.0 copy.104
  881.2 19.9 reshape.157
  901.2 7.1 broadcast_multiply_fusion
  908.3 12.3 slice_negate_fusion
  920.6 20.5 fusion.36
  941.1 71.1 %convolution_bitcast_fusion = f32[4096,6144]{1,0:T(8,128)} fusion(bf16[16,64,4096]{2,1,0:T(8,128)(2,1)} %param.7, f32[4096]{0:T(1024)S(1)} %copy-done.23, f32[16,64]{1,0:T(8,128)S(1)} %copy-done.22, bf16[16,64,1024]{2,1,0:T(8,128)(2,1)} %reshape.154, bf16[16,64,1024]{2,1,0:T(8,128)(2,1)S(1)} %fusion.54, bf16[16,64,4096]{2,1,0:T(8,128)(2,1)} %fusion.36), kind=kOutput, calls=%fused_computation.11 | convolution fusion | flops 51594133504 | bytes 121655296 | tf_op jit(solution)/shard_map/bsd,bse->de/dot_general | solution.py:112
  1012.2 75.6 %fusion.33 = (f32[4096]{0:T(1024)S(1)}, f32[16,64]{1,0:T(8,128)S(1)}, bf16[16,64,4096]{2,1,0:T(8,128)(2,1)}) fusion(bf16[16,64,4096]{2,1,0:T(8,128)(2,1)} %param.7, f32[16,64]{1,0:T(8,128)S(1)} %copy-done.22, f32[4096]{0:T(1024)S(1)} %copy-done.23, bf16[4096,6144]{1,0:T(8,128)(2,1)} %param.11, bf16[16,64,1024]{2,1,0:T(8,128)(2,1)} %reshape.154, ...), kind=kOutput, calls=%fused_computation.43 | convolution fusion | flops 51615100928 | bytes 79732736 | tf_op jit(solution)/shard_map/bse,de->bsd/dot_general | solution.py:113
  1087.8 26.3 psum.21
  1114.2 14.5 fusion.30
  1130.2 40.2 %fusion.35 = bf16[16,64,4096]{2,1,0:T(8,128)(2,1)} fusion(bf16[16,64,4096]{2,1,0:T(8,128)(2,1)S(1)} %copy-done.2, bf16[16,64,4096]{2,1,0:T(8,128)(2,1)S(1)} %copy-done.8, bf16[4096,4096]{1,0:T(8,128)(2,1)} %param.12), kind=kOutput, calls=%fused_computation.45 | convolution fusion | flops 34372321280 | bytes 58720256 | tf_op jit(solution)/shard_map/bse,ed->bsd/dot_general | solution.py:97
  1170.5 237.6 %all-reduce.5.cloned.1.call-done = f32[4096,4096]{1,0:T(8,128)} async-done(((f32[4096,4096]{1,0:T(8,128)}), f32[4096,4096]{1,0:T(8,128)}) %all-reduce.5.cloned.1.call-update) | async-done | bytes 67108880 | tf_op jit(solution)/shard_map/psum | solution.py:116
  1408.0 1114.9 %all-reduce.3.cloned.1.call-done = f32[4096,6144]{1,0:T(8,128)} async-done(((f32[4096,6144]{1,0:T(8,128)}), f32[4096,6144]{1,0:T(8,128)}) %all-reduce.3.cloned.1.call-update) | async-done | bytes 100663312 | tf_op jit(solution)/shard_map/psum | solution.py:116
  2522.9 64.8 %copy.160 = f32[4096,6144]{1,0:T(8,128)} copy(f32[4096,6144]{1,0:T(8,128)} %all-reduce.3.cloned.1.call-done) | data formatting | bytes 201326592
  2587.7 44.1 %copy.161 = f32[4096,4096]{1,0:T(8,128)} copy(f32[4096,4096]{1,0:T(8,128)} %all-reduce.5.cloned.1.call-done) | data formatting | bytes 134217728
  (96 shorter events, 73.0 us)
Async XLA Ops:
  12.3 60.4 %copy-start.21 = (f32[16,64]{1,0:T(8,128)}, f32[16,64]{1,0:T(8,128)S(1)}, u32[]{:S(2)}) copy-start(f32[16,64]{1,0:T(8,128)S(1)} %add_rsqrt_fusion) | copy-start | bytes 12292
  77.7 11.1 copy-start.24
  77.7 11.1 copy-start.25
  79.7 31.1 %all-to-all-start = ((bf16[16,64,8,128]{3,1,0,2:T(8,128)(2,1)}), bf16[16,64,8,128]{3,1,0,2:T(8,128)(2,1)S(1)}, u32[]{:S(2)}, u32[]{:S(2)}) async-start(bf16[16,64,8,128]{3,1,0,2:T(8,128)(2,1)} %bitcast.246), calls=%async_computation | async-start | bytes 4194304 | tf_op jit(solution)/shard_map/all_to_all | solution.py:88
  84.2 5.0 copy-start.1
  89.1 44.9 %copy-start.14 = (f32[64,128]{1,0:T(8,128)}, f32[64,128]{1,0:T(8,128)S(1)}, u32[]{:S(2)}) copy-start(f32[64,128]{1,0:T(8,128)S(1)} %get-tuple-element.25) | copy-start | bytes 98308
  89.2 44.9 %copy-start.16 = (f32[64,128]{1,0:T(8,128)}, f32[64,128]{1,0:T(8,128)S(1)}, u32[]{:S(2)}) copy-start(f32[64,128]{1,0:T(8,128)S(1)} %get-tuple-element.24) | copy-start | bytes 98308
  110.7 23.3 copy-start.9
  110.7 46.3 %all-to-all-start.1 = ((bf16[16,64,8,128]{3,1,0,2:T(8,128)(2,1)}), bf16[16,64,8,128]{3,1,0,2:T(8,128)(2,1)}, u32[]{:S(2)}, u32[]{:S(2)}) async-start(bf16[16,64,8,128]{3,1,0,2:T(8,128)(2,1)} %copy.85), calls=%async_computation.1 | async-start | bytes 4194304 | tf_op jit(solution)/shard_map/all_to_all | solution.py:87
  157.1 97.9 %all-to-all-start.2 = ((bf16[16,64,32,128]{3,1,0,2:T(8,128)(2,1)}), bf16[16,64,32,128]{3,1,0,2:T(8,128)(2,1)}, u32[]{:S(2)}, u32[]{:S(2)}) async-start(bf16[16,64,32,128]{3,1,0,2:T(8,128)(2,1)} %copy.90), calls=%async_computation.2 | async-start | bytes 16777216 | tf_op jit(solution)/shard_map/all_to_all | solution.py:86
  203.5 11.4 copy-start.10
  212.9 196.1 %copy-start.6 = (pred[512,512]{0,1:T(8,128)(4,1)}, pred[512,512]{0,1:T(8,128)(4,1)S(1)}, u32[]{:S(2)}) copy-start(pred[512,512]{0,1:T(8,128)(4,1)S(1)} %iota_compare_fusion) | copy-start | bytes 786436
  214.9 54.0 %copy-start.3 = (bf16[16,8,64,1,128]{4,2,1,0,3:T(8,128)(2,1)}, bf16[16,8,64,1,128]{4,2,1,0,3:T(8,128)(2,1)S(1)}, u32[]{:S(2)}) copy-start(bf16[16,8,64,1,128]{4,2,1,0,3:T(8,128)(2,1)S(1)} %copy.86) | copy-start | bytes 6291460
  255.0 105.9 %all-to-all-start.4 = ((bf16[16,64,32,128]{3,1,0,2:T(8,128)(2,1)}), bf16[16,64,32,128]{3,1,0,2:T(8,128)(2,1)}, u32[]{:S(2)}, u32[]{:S(2)}) async-start(bf16[16,64,32,128]{3,1,0,2:T(8,128)(2,1)} %bitcast.238), calls=%async_computation.4 | async-start | bytes 16777216 | tf_op jit(solution)/shard_map/all_to_all | solution.py:102
  295.9 113.1 %copy-start.12 = (f32[16,4,512]{2,1,0:T(4,128)}, f32[16,4,512]{2,1,0:T(4,128)S(1)}, u32[]{:S(2)}) copy-start(f32[16,4,512]{2,1,0:T(4,128)S(1)} %get-tuple-element.19) | copy-start | bytes 393220
  296.0 21.8 copy-start.11
  317.7 91.3 %copy-start.18 = (f32[16,4,512]{2,1,0:T(4,128)}, f32[16,4,512]{2,1,0:T(4,128)S(1)}, u32[]{:S(2)}) copy-start(f32[16,4,512]{2,1,0:T(4,128)S(1)} %fusion.7) | copy-start | bytes 393220
  360.9 97.9 %all-to-all-start.3 = ((bf16[16,512,4,128]{3,2,0,1:T(4,128)(2,1)}), bf16[16,512,4,128]{3,2,0,1:T(4,128)(2,1)}, u32[]{:S(2)}, u32[]{:S(2)}) async-start(bf16[16,512,4,128]{3,2,0,1:T(4,128)(2,1)} %copy.94), calls=%async_computation.3 | async-start | bytes 16777216 | tf_op jit(solution)/shard_map/all_to_all | solution.py:95
  458.8 155.7 %all-to-all-start.7 = ((bf16[16,512,1,128]{3,0,2,1:T(8,128)(2,1)}), bf16[16,512,1,128]{3,0,2,1:T(8,128)(2,1)}, u32[]{:S(2)}, u32[]{:S(2)}) async-start(bf16[16,512,1,128]{3,0,2,1:T(8,128)(2,1)} %copy.114), calls=%async_computation.7 | async-start | bytes 4194304 | tf_op jit(solution)/shard_map/all_to_all | solution.py:107
  461.9 946.2 %all-reduce.5.cloned.1.call-start = ((), (), s32[]{:S(2)}) async-start(), calls=%async_computation.9 | async-start | bytes 134217728 | tf_op jit(solution)/shard_map/psum | solution.py:116
  546.0 0.9 copy-start.7
  546.0 1.0 copy-start.13
  546.0 1.0 copy-start.19
  546.1 1.1 copy-start.20
  591.3 26.3 copy-start.4
  614.4 52.2 %all-to-all-start.6 = ((bf16[16,512,1,128]{3,0,2,1:T(8,128)(2,1)}), bf16[16,512,1,128]{3,0,2,1:T(8,128)(2,1)}, u32[]{:S(2)}, u32[]{:S(2)}) async-start(bf16[16,512,1,128]{3,0,2,1:T(8,128)(2,1)} %copy.108), calls=%async_computation.6 | async-start | bytes 4194304 | tf_op jit(solution)/shard_map/all_to_all | solution.py:106
  634.1 36.3 %copy-start.17 = (f32[64,128]{1,0:T(8,128)S(1)}, f32[64,128]{1,0:T(8,128)}, u32[]{:S(2)}) copy-start(f32[64,128]{1,0:T(8,128)} %copy-done.16) | copy-start | bytes 98308
  666.6 162.5 %all-to-all-start.5 = ((bf16[16,512,4,128]{3,2,0,1:T(4,128)(2,1)}), bf16[16,512,4,128]{3,2,0,1:T(4,128)(2,1)}, u32[]{:S(2)}, u32[]{:S(2)}) async-start(bf16[16,512,4,128]{3,2,0,1:T(4,128)(2,1)} %copy.101), calls=%async_computation.5 | async-start | bytes 16777216 | tf_op jit(solution)/shard_map/all_to_all | solution.py:105
  670.3 1852.6 %all-reduce.3.cloned.1.call-start = ((), (), s32[]{:S(2)}) async-start(), calls=%async_computation.8 | async-start | bytes 201326592 | tf_op jit(solution)/shard_map/psum | solution.py:116
  675.1 15.3 copy-start.15
  690.4 2.3 copy-start.5
  853.0 22.2 copy-start
  920.6 20.5 copy-start.22
  920.6 20.5 copy-start.23
  1114.1 14.5 copy-start.2
  1114.1 16.1 copy-start.8
Sparse Core Ops, SparseCore 0:
  546.2 861.7 all-reduce.4
  1412.4 1110.4 all-reduce.2
where the time goes:
time: 2650 us; the launch traced here: 2640 us
  waiting for transfers between devices  1560 us (59%)
  matrix products  499 us (19%)
  local copies, waits for them, and re-layouts  316 us (12%)
  other arithmetic  195 us (7%)
  starting transfers between devices  29.6 us (1%)
    psum x1, waiting for transfers between devices, block_body(): lax.psum(grad_wqkv, 'sp')  1110 us
    psum x1, waiting for transfers between devices, block_body(): lax.psum(grad_wout, 'sp')  238 us
    all_to_all x1, waiting for transfers between devices, block_body(): lax.all_to_all(grad_query.reshape(batch_size, seq_len, kv_local * group_s...  135 us
    unnamed x56, local copies, waits for them, and re-layouts  112 us
    dot_general x1, matrix products, block_body(): jnp.einsum('bse,de->bsd', grad_qkv, w_qkv, preferred_element_type=jnp.flo...  75.6 us
    dot_general x1, matrix products, block_body(): jnp.einsum('bsd,bse->de', normed, grad_qkv, preferred_element_type=jnp.fl...  71.1 us
    dot_general x1, matrix products, block_body(): jnp.einsum('bsd,de->bse', normed, w_qkv, preferred_element_type=jnp.float32)  60.4 us
    convert_element_type x5, local copies, waits for them, and re-layouts, rope_back(): grad_wide = grad_vals.astype(jnp.float32)  58.5 us
  transfers between devices with their start and end apart: 10, of which 7 were waited for; matrix products, arithmetic and copies ran while one was open for 31% of the time, Pallas kernels for 0%

commit v1 on v0

v1 whole, which is shorter than its diff:
```python
import functools
import math
import jax
import jax.numpy as jnp
from jax import lax
from jax.experimental import pallas as pl
from jax.experimental.pallas import tpu as pltpu
from jax.sharding import PartitionSpec as P

NORM_EPS = 1e-5
ROPE_BASE = 10000.0
ROPE_SCALE = math.sqrt(1.0 + math.log(32.0) / math.log(4096.0))
LOG2_E = math.log2(math.e)
CHUNKS = (2, 4, 4, 6)


def rope_tables(positions, long_factor):
    head_dim = 2 * long_factor.shape[0]
    exponents = jnp.arange(0, head_dim, 2).astype(jnp.float32) / head_dim
    inv_freq = 1.0 / (long_factor * ROPE_BASE ** exponents)
    angles = positions.astype(jnp.float32)[:, None] * inv_freq[None, :]
    cos_half = jnp.cos(angles) * ROPE_SCALE
    sin_half = jnp.sin(angles) * ROPE_SCALE
    return jnp.concatenate([cos_half, cos_half], axis=-1), jnp.concatenate([-sin_half, sin_half], axis=-1)


def attention_kernel(qkv_ref, grad_ref, cos_ref, sin_ref, out_ref, dqkv_ref, query_s, dkey_s, dvalue_s):
    devs, _, sub, width = qkv_ref.shape
    dim = cos_ref.shape[1]
    seq = devs * sub
    group = width // dim - 2
    block = 128
    per = block // sub
    scale = dim ** -0.5
    cols = group * block

    def rope(vals, cos, sin):
        wide = vals.astype(jnp.float32)
        return (wide * cos + pltpu.roll(wide, dim // 2, 1) * sin).astype(jnp.bfloat16)

    def rope_back(vals, cos, sin):
        wide = vals.astype(jnp.float32)
        return (wide * cos - pltpu.roll(wide, dim // 2, 1) * sin).astype(jnp.bfloat16)

    def nt(lhs, rhs):
        return lax.dot_general(lhs, rhs, (((1,), (1,)), ((), ())), preferred_element_type=jnp.float32)

    def nn(lhs, rhs):
        return jnp.dot(lhs, rhs, preferred_element_type=jnp.float32)

    key_raw = qkv_ref[:, 0, :, group * dim:(group + 1) * dim].reshape(seq, dim)
    value = qkv_ref[:, 0, :, (group + 1) * dim:].reshape(seq, dim)
    key = rope(key_raw, cos_ref[...], sin_ref[...])
    key_t = key.T
    value_t = value.T
    row_ids = lax.broadcasted_iota(jnp.int32, (block, cols), 0)
    col_ids = lax.broadcasted_iota(jnp.int32, (block, cols), 1)
    allowed = row_ids <= lax.rem(col_ids, block)

    for step in reversed(range(seq // block)):
        rows = pl.ds(step * block, block)
        cos = cos_ref[rows, :]
        sin = sin_ref[rows, :]
        span = (step + 1) * block
        grads = []
        for head in range(group):
            lanes = pl.ds(head * dim, dim)
            raw = qkv_ref[step * per:(step + 1) * per, 0, :, lanes].reshape(block, dim)
            query_s[head * block:(head + 1) * block, :] = rope(raw, cos, sin)
            grads.append(grad_ref[step * per:(step + 1) * per, 0, :, lanes].reshape(block, dim))
        query = query_s[...]
        grad = jnp.concatenate(grads, axis=0)
        scores = nt(key[:span], query)
        last = jnp.where(allowed, scores[span - block:], -jnp.inf)
        scores = last if step == 0 else jnp.concatenate([scores[:span - block], last], axis=0)
        peak = jnp.max(scores, axis=0, keepdims=True)
        weights = jnp.exp2((scores - peak) * (scale * LOG2_E))
        probs = weights * (1.0 / jnp.sum(weights, axis=0, keepdims=True))
        probs_low = probs.astype(jnp.bfloat16)
        attn = nn(value_t[:, :span], probs_low).astype(jnp.bfloat16).T
        grad_probs = nt(value[:span], grad).astype(jnp.bfloat16).astype(jnp.float32)
        row_dot = jnp.sum(grad_probs * probs, axis=0, keepdims=True)
        grad_scores = (probs * (grad_probs - row_dot)).astype(jnp.bfloat16)
        grad_query = (nn(key_t[:, :span], grad_scores) * scale).astype(jnp.bfloat16).T
        part_value = nn(probs_low, grad)
        part_key = nn(grad_scores, query)
        if span == seq:
            dvalue_s[...] = part_value
            dkey_s[...] = part_key
        else:
            dvalue_s[:span, :] += part_value
            dkey_s[:span, :] += part_key
        for head in range(group):
            lanes = pl.ds(head * dim, dim)
            part = slice(head * block, (head + 1) * block)
            out_ref[step * per:(step + 1) * per, 0, :, lanes] = attn[part].reshape(per, sub, dim)
            back = rope_back(grad_query[part], cos, sin)
            dqkv_ref[step * per:(step + 1) * per, 0, :, lanes] = back.reshape(per, sub, dim)

    grad_key = (dkey_s[...] * scale).astype(jnp.bfloat16)
    back = rope_back(grad_key, cos_ref[...], sin_ref[...])
    dqkv_ref[:, 0, :, group * dim:(group + 1) * dim] = back.reshape(devs, sub, dim)
    dqkv_ref[:, 0, :, (group + 1) * dim:] = dvalue_s[...].astype(jnp.bfloat16).reshape(devs, sub, dim)


def attention(qkv, grad, cos, sin, heads, name):
    devs, count, sub, width = qkv.shape
    dim = cos.shape[1]
    seq = devs * sub
    per_head = width // heads
    group = per_head // dim - 2

    def head_spec(cols):
        return pl.BlockSpec((devs, 1, sub, cols), lambda b, a: (0, b, 0, a))

    table_spec = pl.BlockSpec((seq, dim), lambda b, a: (0, 0))
    return pl.pallas_call(
        attention_kernel,
        name=name,
        grid=(count, heads),
        in_specs=[head_spec(per_head), head_spec(group * dim), table_spec, table_spec],
        out_specs=[head_spec(group * dim), head_spec(per_head)],
        out_shape=[jax.ShapeDtypeStruct(grad.shape, jnp.bfloat16), jax.ShapeDtypeStruct(qkv.shape, jnp.bfloat16)],
        scratch_shapes=[pltpu.VMEM((group * 128, dim), jnp.bfloat16),
                        pltpu.VMEM((seq, dim), jnp.float32), pltpu.VMEM((seq, dim), jnp.float32)],
        compiler_params=pltpu.CompilerParams(vmem_limit_bytes=56 * 1024 * 1024),
        cost_estimate=pl.CostEstimate(flops=count * heads * group * 6 * 2 * seq * seq * dim,
                                      bytes_accessed=4 * (qkv.size + grad.size),
                                      transcendentals=count * heads * group * seq * seq // 2),
    )(qkv, grad, cos, sin)


def join_kernel(parts, heads, core_ref, mine_ref, other_ref, out_ref):
    first = core_ref[0] == 0
    width = sum(parts)
    start = 0
    base = 0
    for cols in parts:
        for head in range(heads):
            lanes = slice(head * width + start, head * width + start + cols)
            mine = mine_ref[:, lanes]
            other = other_ref[:, lanes]
            at = base + 2 * head * cols
            out_ref[:, at:at + cols] = jnp.where(first, mine, other)
            out_ref[:, at + cols:at + 2 * cols] = jnp.where(first, other, mine)
        start += cols
        base += 2 * heads * cols


def join_columns(core, mine, other, parts, heads, name):
    rows, half = mine.shape
    tile = 128
    spec = pl.BlockSpec((tile, half), lambda t, core_ref: (t, 0))
    return pl.pallas_call(
        functools.partial(join_kernel, parts, heads),
        name=name,
        grid_spec=pltpu.PrefetchScalarGridSpec(
            num_scalar_prefetch=1, grid=(rows // tile,), in_specs=[spec, spec],
            out_specs=pl.BlockSpec((tile, 2 * half), lambda t, core_ref: (t, 0))),
        out_shape=jax.ShapeDtypeStruct((rows, 2 * half), mine.dtype),
        compiler_params=pltpu.CompilerParams(vmem_limit_bytes=40 * 1024 * 1024),
        cost_estimate=pl.CostEstimate(flops=rows * half * 64, bytes_accessed=4 * rows * half * mine.dtype.itemsize,
                                      transcendentals=0),
    )(core, mine, other)


def pick_columns_kernel(core_ref, query_ref, key_ref, value_ref, out_ref):
    query = query_ref.shape[1]
    small = key_ref.shape[1]
    out_ref[:, :query] = query_ref[...]
    out_ref[:, query:query + small] = key_ref[...]
    out_ref[:, query + small:] = value_ref[...]


def pick_columns(core, w_qkv, heads, group, dim):
    rows = w_qkv.shape[0]
    tile = 1024
    width = (group + 2) * dim
    kv_base = 2 * heads * group
    return pl.pallas_call(
        pick_columns_kernel,
        name='pick_columns',
        grid_spec=pltpu.PrefetchScalarGridSpec(
            num_scalar_prefetch=1, grid=(rows // tile, heads),
            in_specs=[pl.BlockSpec((tile, group * dim), lambda t, a, core_ref: (t, 2 * a + core_ref[0])),
                      pl.BlockSpec((tile, dim), lambda t, a, core_ref: (t, kv_base + 2 * a + core_ref[0])),
                      pl.BlockSpec((tile, dim), lambda t, a, core_ref: (t, kv_base + 2 * heads + 2 * a + core_ref[0]))],
            out_specs=pl.BlockSpec((tile, width), lambda t, a, core_ref: (t, a))),
        out_shape=jax.ShapeDtypeStruct((rows, heads * width), w_qkv.dtype),
        compiler_params=pltpu.CompilerParams(vmem_limit_bytes=32 * 1024 * 1024),
        cost_estimate=pl.CostEstimate(flops=rows * heads * width * 32, bytes_accessed=4 * rows * heads * width,
                                      transcendentals=0),
    )(core, w_qkv, w_qkv, w_qkv)


def pick_rows_kernel(core_ref, in_ref, out_ref):
    out_ref[...] = in_ref[...]


def pick_rows(core, w_out, heads, rows):
    cols = w_out.shape[1]
    return pl.pallas_call(
        pick_rows_kernel,
        name='pick_rows',
        grid_spec=pltpu.PrefetchScalarGridSpec(
            num_scalar_prefetch=1, grid=(heads, 2),
            in_specs=[pl.BlockSpec((rows // 2, cols), lambda a, h, core_ref: (4 * a + 2 * core_ref[0] + h, 0))],
            out_specs=pl.BlockSpec((rows // 2, cols), lambda a, h, core_ref: (2 * a + h, 0))),
        out_shape=jax.ShapeDtypeStruct((heads * rows, cols), w_out.dtype),
        compiler_params=pltpu.CompilerParams(vmem_limit_bytes=32 * 1024 * 1024),
        cost_estimate=pl.CostEstimate(flops=heads * rows * cols * 32, bytes_accessed=4 * heads * rows * cols,
                                      transcendentals=0),
    )(core, w_out)


def pick_tokens_kernel(count, devs_ref, *refs):
    inputs, outputs = refs[:2 * count], refs[2 * count:]
    for side in range(2):
        start = 0
        for index in range(count):
            part = inputs[side * count + index]
            outputs[side][start:start + part.shape[1]] = part[0]
            start += part.shape[1]


def pick_tokens(devs, chunks, name):
    sub, width = chunks[0].shape[2:]
    batch = sum(chunk.shape[1] for chunk in chunks)

    def token_spec(chunk, side):
        return pl.BlockSpec((1,) + chunk.shape[1:], lambda g, devs_ref: (devs_ref[side], 0, 0, 0))

    out = jax.ShapeDtypeStruct((batch, sub, width), chunks[0].dtype)
    out_spec = pl.BlockSpec((batch, sub, width), lambda g, devs_ref: (0, 0, 0))
    return pl.pallas_call(
        functools.partial(pick_tokens_kernel, len(chunks)),
        name=name,
        grid_spec=pltpu.PrefetchScalarGridSpec(
            num_scalar_prefetch=1, grid=(1,),
            in_specs=[token_spec(chunk, side) for side in range(2) for chunk in chunks],
            out_specs=[out_spec, out_spec]),
        out_shape=[out, out],
        compiler_params=pltpu.CompilerParams(vmem_limit_bytes=60 * 1024 * 1024),
        cost_estimate=pl.CostEstimate(flops=batch * sub * width * 64, bytes_accessed=8 * batch * sub * width,
                                      transcendentals=0),
    )(devs, *chunks, *chunks)


def block_body(hidden, positions, long_factor, norm_weight, w_qkv, w_out, grad_out):
    batch, sub, model = hidden.shape
    dim = 2 * long_factor.shape[0]
    query_dim = w_out.shape[0]
    kv_dim = (w_qkv.shape[1] - query_dim) // 2
    kv_heads = kv_dim // dim
    group = query_dim // kv_dim
    devs = lax.axis_size('sp')
    mine_heads = kv_heads // 2
    me = lax.axis_index('sp')
    core = lax.rem(me, 2)
    chip = lax.div(me, 2)
    partner = me + 1 - 2 * core
    pairs = [(d, d ^ 1) for d in range(devs)]

    hidden_wide = hidden.astype(jnp.float32)
    inv_rms = lax.rsqrt(jnp.mean(hidden_wide * hidden_wide, axis=-1, keepdims=True) + NORM_EPS)
    normed = (hidden_wide * inv_rms * norm_weight).astype(jnp.bfloat16)

    core_ref = core.reshape(1)
    w_own = pick_columns(core_ref, w_qkv, mine_heads, group, dim)
    wo_own = pick_rows(core_ref, w_out, mine_heads, group * dim)
    cos, sin = rope_tables(lax.all_gather(positions, 'sp', axis=0, tiled=True), long_factor)

    gathered = []
    start = 0
    for count in CHUNKS:
        gathered.append((lax.all_gather(normed[start:start + count], 'sp', axis=0),
                         lax.all_gather(grad_out[start:start + count], 'sp', axis=0)))
        start += count

    grad_wqkv = None
    grad_wout = None
    tokens = []
    for index, (normed_all, grad_all) in enumerate(gathered):
        qkv = jnp.einsum('tbsd,de->tbse', normed_all, w_own, preferred_element_type=jnp.float32).astype(jnp.bfloat16)
        grad_attn = jnp.einsum('tbsd,ed->tbse', grad_all, wo_own, preferred_element_type=jnp.float32).astype(jnp.bfloat16)
        attn, grad_qkv = attention(qkv, grad_attn, cos, sin, mine_heads, f'attention_{index}')
        attn_slice = lax.dynamic_slice_in_dim(attn, chip * group * dim, group * dim, axis=3)
        part_out = jnp.einsum('tbse,tbsd->ed', attn_slice, grad_all, preferred_element_type=jnp.float32)
        part_qkv = jnp.einsum('tbsd,tbse->de', normed_all, grad_qkv, preferred_element_type=jnp.float32)
        grad_wout = part_out if grad_wout is None else grad_wout + part_out
        grad_wqkv = part_qkv if grad_wqkv is None else grad_wqkv + part_qkv
        tokens.append((attn, grad_qkv))

    grad_wout = lax.all_gather(grad_wout, 'sp', axis=0, tiled=True)
    grad_wqkv_other = lax.ppermute(grad_wqkv, 'sp', pairs)

    ends = jnp.stack([me, partner])
    attn_mine, attn_send = pick_tokens(ends, [pair[0] for pair in tokens], 'pick_attention')
    dqkv_mine, dqkv_send = pick_tokens(ends, [pair[1] for pair in tokens], 'pick_gradient')
    attn_other = lax.ppermute(attn_send, 'sp', pairs)
    dqkv_other = lax.ppermute(dqkv_send, 'sp', pairs)

    def natural(mine, other, parts, name):
        rows = (batch * sub, -1)
        joined = join_columns(core_ref, mine.reshape(rows), other.reshape(rows), parts, mine_heads, name)
        return joined.reshape(batch, sub, -1)

    parts = (group * dim, dim, dim)
    attn_flat = natural(attn_mine, attn_other, parts[:1], 'join_attention')
    mixed_out = jnp.einsum('bse,ed->bsd', attn_flat, w_out, preferred_element_type=jnp.float32)
    out_hidden = (hidden_wide + mixed_out).astype(jnp.bfloat16)

    grad_qkv = natural(dqkv_mine, dqkv_other, parts, 'join_gradient')
    grad_normed = jnp.einsum('bse,de->bsd', grad_qkv, w_qkv, preferred_element_type=jnp.float32)
    grad_normed = grad_normed.astype(jnp.bfloat16).astype(jnp.float32)
    unit_hidden = hidden_wide * inv_rms
    grad_norm = jnp.sum(grad_normed * unit_hidden, axis=(0, 1))
    grad_unit = grad_normed * norm_weight
    grad_inner = inv_rms * (grad_unit - unit_hidden * jnp.mean(grad_unit * unit_hidden, axis=-1, keepdims=True))
    grad_hidden = (grad_out.astype(jnp.float32) + grad_inner).astype(jnp.bfloat16)

    grad_wqkv = join_columns(core_ref, grad_wqkv, grad_wqkv_other, parts, mine_heads, 'join_weights')
    return out_hidden, grad_hidden, lax.psum(grad_norm, 'sp'), grad_wqkv, grad_wout


def solution(mesh):
    token_spec = P('dp', 'sp', None)
    return jax.shard_map(block_body, mesh=mesh,
                         in_specs=(token_spec, P(('dp', 'sp')), P(), P(), P(), P(), token_spec),
                         out_specs=(token_spec, token_spec, P('dp'), P('dp', None), P('dp', None)),
                         check_vma=False)
```

time: 2650 us -> 1590 us (0.60)
  waiting for transfers between devices: 1560 us -> 125 us
  Pallas kernels: 0 us -> 415 us
  matrix products: 499 us -> 872 us
  local copies, waits for them, and re-layouts: 316 us -> 75.3 us
  other arithmetic: 195 us -> 31.6 us
  starting transfers between devices: 29.6 us -> 1.12 us
    psum x2 -> x0, waiting for transfers between devices: 1350 us -> none  [the longest x1 1110 us: block_body(): lax.psum(grad_wqkv, 'sp')]
    pallas_call x0 -> x11, Pallas kernels: none -> 415 us  [the longest x4 277 us: attention(): pl.pallas_call(attention_kernel, name=name, grid=(count, heads), in_specs...]
    dot_general x10 -> x16, matrix products: 383 us -> 766 us  [the longest x4 282 us: block_body(): jnp.einsum('tbsd,tbse->de', normed_all, grad_qkv, preferred_element_type=...]
    all_to_all x8 -> x0, waiting for transfers between devices: 205 us -> none  [the longest x1 135 us: block_body(): lax.all_to_all(grad_query.reshape(batch_size, seq_len, kv_local * group_s...]
    convert_element_type x10 -> x0, local copies, waits for them, and re-layouts: 81.8 us -> none  [the longest x5 58.5 us: rope_back(): grad_wide = grad_vals.astype(jnp.float32)]
    all_to_all x10 -> x0, local copies, waits for them, and re-layouts: 65 us -> none  [the longest x2 23.7 us: block_body(): lax.all_to_all(attn_grp.reshape(batch_size, seq_len, kv_local * group_siz...]
    ppermute x0 -> x3, waiting for transfers between devices: none -> 64.1 us  [the longest x1 64.1 us: block_body(): attn_other = lax.ppermute(attn_send, 'sp', pairs)]
    all_gather x0 -> x9, waiting for transfers between devices: none -> 59.3 us  [the longest x4 59.3 us: block_body(): lax.all_gather(normed[start:start + count], 'sp', axis=0)]
  transfers between devices with their start and end apart: 10 -> 12, of which waited for: 7 -> 4; matrix products, arithmetic and copies ran while one was open for 31% -> 50% of each run, Pallas kernels for 0% -> 20%
where the time goes in v1:
time: 1590 us; the launch traced here: 1580 us
  matrix products  872 us (55%)
  Pallas kernels  415 us (26%)
  waiting for transfers between devices  125 us (8%)
  local copies, waits for them, and re-layouts  75.3 us (5%)
  blocking collectives  48.1 us (3%)
  other arithmetic  31.6 us (2%)
    dot_general x4, matrix products, block_body(): jnp.einsum('tbsd,tbse->de', normed_all, grad_qkv, preferred_element_type=...  282 us
    pallas_call x4, Pallas kernels, attention(): pl.pallas_call(attention_kernel, name=name, grid=(count, heads), in_specs...  277 us
    dot_general x4, matrix products, block_body(): jnp.einsum('tbsd,de->tbse', normed_all, w_own, preferred_element_type=jnp...  245 us
    dot_general x4, matrix products, block_body(): jnp.einsum('tbsd,ed->tbse', grad_all, wo_own, preferred_element_type=jnp....  171 us
    pallas_call x3, Pallas kernels, join_columns(): pl.pallas_call(functools.partial(join_kernel, parts, heads), name=name, g...  90 us
    dot_general x4, matrix products, block_body(): jnp.einsum('tbse,tbsd->ed', attn_slice, grad_all, preferred_element_type=...  68.6 us
    ppermute x1, waiting for transfers between devices, block_body(): attn_other = lax.ppermute(attn_send, 'sp', pairs)  64.1 us
    dot_general x1, matrix products, block_body(): jnp.einsum('bse,de->bsd', grad_qkv, w_qkv, preferred_element_type=jnp.flo...  63.9 us
  transfers between devices with their start and end apart: 12, of which 4 were waited for; matrix products, arithmetic and copies ran while one was open for 50% of the time, Pallas kernels for 20%

profile of v1, /device:TPU:0, one launch (start us, length us, event | category | flops | bytes accessed | tf_op | source)
XLA Modules:
  0.0 1582.7 jit_solution(1957355364481869155)
XLA Ops:
  7.2 2.3 slice.25
  9.6 5.1 fusion.28
  15.3 10.2 fusion.25
  25.4 2.3 slice.32
  27.8 4.7 fusion.86
  32.6 4.8 fusion.87
  38.6 4.0 slice.31
  42.7 3.9 slice.35
  46.9 25.7 %all-reduce = s32[512]{0:T(512)S(1)} all-reduce(s32[512]{0:T(512)S(1)} %dynamic-update-slice), channel_id=1, replica_groups=mesh['dp'=1,'sp'=8] {'sp'}, use_global_device_ids=true, to_apply=%add | all-reduce | flops 512 | bytes 4096
  72.7 8.0 pick_rows.1
  80.7 6.2 copy-done
  86.8 22.4 %pick_columns.1 = bf16[4096,3072]{1,0:T(8,128)(2,1)} custom-call(s32[1]{0:T(128)} %bitcast.core_ref, bf16[4096,6144]{1,0:T(8,128)(2,1)} %value_ref.1, bf16[4096,6144]{1,0:T(8,128)(2,1)} %value_ref.1, bf16[4096,6144]{1,0:T(8,128)(2,1)} %value_ref.1), custom_call_target="tpu_custom_call" | custom-call | flops 402653184 | bytes 50331648 | tf_op jit(solution)/shard_map/pick_columns/pallas_call | solution.py:180
  110.2 1.0 pad_maximum_fusion
  111.3 23.7 %convert_bitcast_fusion.3.grad_ref = bf16[8,2,64,2048]{3,2,1,0:T(8,128)(2,1)} fusion(bf16[8,2,64,4096]{3,2,1,0:T(8,128)(2,1)} %bitcast.132, bf16[2048,4096]{1,0:T(8,128)(2,1)} %copy-done), kind=kOutput, calls=%fused_computation.70 | convolution fusion | flops 17181966336 | bytes 29360128 | tf_op jit(solution)/shard_map/tbsd,ed->tbse/dot_general | solution.py:285
  135.0 33.0 %fusion.70.qkv_ref = bf16[8,2,64,3072]{3,2,1,0:T(8,128)(2,1)} fusion(bf16[8,2,64,4096]{3,2,1,0:T(8,128)(2,1)} %bitcast.145, bf16[4096,3072]{1,0:T(8,128)(2,1)} %pick_columns.1), kind=kOutput, calls=%fused_computation.69 | convolution fusion | flops 25772949504 | bytes 39845888 | tf_op jit(solution)/shard_map/tbsd,de->tbse/dot_general | solution.py:284
  168.0 35.9 %attention_0.1 = (bf16[8,2,64,2048]{3,2,1,0:T(8,128)(2,1)}, bf16[8,2,64,3072]{3,2,1,0:T(8,128)(2,1)}) custom-call(bf16[8,2,64,3072]{3,2,1,0:T(8,128)(2,1)} %fusion.70.qkv_ref, bf16[8,2,64,2048]{3,2,1,0:T(8,128)(2,1)} %convert_bitcast_fusion.3.grad_ref, f32[512,128]{1,0:T(8,128)} %get-tuple-element.39.cos_ref, f32[512,128]{1,0:T(8,128)} %get-tuple-element.40.sin_ref), custom_call_target="tpu_custom_call" | custom-call | flops 12884901888 | bytes 20971520 | tf_op jit(solution)/shard_map/attention_0/pallas_call | solution.py:117
  203.9 11.5 fusion.51
  215.4 42.7 %convert_bitcast_fusion.1.grad_ref = bf16[8,4,64,2048]{3,2,1,0:T(8,128)(2,1)} fusion(bf16[8,4,64,4096]{3,2,1,0:T(8,128)(2,1)} %bitcast.143, bf16[2048,4096]{1,0:T(8,128)(2,1)} %copy-done), kind=kOutput, calls=%fused_computation.63 | convolution fusion | flops 34363932672 | bytes 41943040 | tf_op jit(solution)/shard_map/tbsd,ed->tbse/dot_general | solution.py:285
  258.1 26.0 %all-gather.24.cloned.1.call-done = bf16[32,64,4096]{2,1,0:T(8,128)(2,1)} async-done(((bf16[4,64,4096]{2,1,0:T(8,128)(2,1)}), bf16[32,64,4096]{2,1,0:T(8,128)(2,1)}) %all-gather.24.cloned.1.call-update) | async-done | bytes 16777232 | tf_op jit(solution)/shard_map/all_gather | solution.py:276
  284.2 61.5 %fusion.56.qkv_ref = bf16[8,4,64,3072]{3,2,1,0:T(8,128)(2,1)} fusion(bf16[8,4,64,4096]{3,2,1,0:T(8,128)(2,1)} %bitcast.139, bf16[4096,3072]{1,0:T(8,128)(2,1)} %pick_columns.1), kind=kOutput, calls=%fused_computation.65 | convolution fusion | flops 51545899008 | bytes 54525952 | tf_op jit(solution)/shard_map/tbsd,de->tbse/dot_general | solution.py:284
  345.7 24.3 %all-gather.28.cloned.1.call-done = bf16[32,64,4096]{2,1,0:T(8,128)(2,1)} async-done(((bf16[4,64,4096]{2,1,0:T(8,128)(2,1)}), bf16[32,64,4096]{2,1,0:T(8,128)(2,1)}) %all-gather.28.cloned.1.call-update) | async-done | bytes 16777232 | tf_op jit(solution)/shard_map/all_gather | solution.py:276
  370.0 61.7 %fusion.59.qkv_ref = bf16[8,4,64,3072]{3,2,1,0:T(8,128)(2,1)} fusion(bf16[8,4,64,4096]{3,2,1,0:T(8,128)(2,1)} %bitcast.141, bf16[4096,3072]{1,0:T(8,128)(2,1)} %pick_columns.1), kind=kOutput, calls=%fused_computation.66 | convolution fusion | flops 51545899008 | bytes 54525952 | tf_op jit(solution)/shard_map/tbsd,de->tbse/dot_general | solution.py:284
  431.7 69.1 %attention_2.1 = (bf16[8,4,64,2048]{3,2,1,0:T(8,128)(2,1)}, bf16[8,4,64,3072]{3,2,1,0:T(8,128)(2,1)}) custom-call(bf16[8,4,64,3072]{3,2,1,0:T(8,128)(2,1)} %fusion.59.qkv_ref, bf16[8,4,64,2048]{3,2,1,0:T(8,128)(2,1)} %convert_bitcast_fusion.1.grad_ref, f32[512,128]{1,0:T(8,128)} %get-tuple-element.39.cos_ref, f32[512,128]{1,0:T(8,128)} %get-tuple-element.40.sin_ref), custom_call_target="tpu_custom_call" | custom-call | flops 25769803776 | bytes 41943040 | tf_op jit(solution)/shard_map/attention_2/pallas_call | solution.py:117
  500.7 15.2 fusion.38
  516.0 42.5 %convert_bitcast_fusion.2.grad_ref = bf16[8,4,64,2048]{3,2,1,0:T(8,128)(2,1)} fusion(bf16[8,4,64,4096]{3,2,1,0:T(8,128)(2,1)} %bitcast.129, bf16[2048,4096]{1,0:T(8,128)(2,1)} %copy-done), kind=kOutput, calls=%fused_computation.64 | convolution fusion | flops 34363932672 | bytes 41943040 | tf_op jit(solution)/shard_map/tbsd,ed->tbse/dot_general | solution.py:285
  558.5 69.5 %attention_1.1 = (bf16[8,4,64,2048]{3,2,1,0:T(8,128)(2,1)}, bf16[8,4,64,3072]{3,2,1,0:T(8,128)(2,1)}) custom-call(bf16[8,4,64,3072]{3,2,1,0:T(8,128)(2,1)} %fusion.56.qkv_ref, bf16[8,4,64,2048]{3,2,1,0:T(8,128)(2,1)} %convert_bitcast_fusion.2.grad_ref, f32[512,128]{1,0:T(8,128)} %get-tuple-element.39.cos_ref, f32[512,128]{1,0:T(8,128)} %get-tuple-element.40.sin_ref), custom_call_target="tpu_custom_call" | custom-call | flops 25769803776 | bytes 41943040 | tf_op jit(solution)/shard_map/attention_1/pallas_call | solution.py:117
  628.0 61.8 %convert_bitcast_fusion.grad_ref = bf16[8,6,64,2048]{3,2,1,0:T(8,128)(2,1)} fusion(bf16[8,6,64,4096]{3,2,1,0:T(8,128)(2,1)} %bitcast.137, bf16[2048,4096]{1,0:T(8,128)(2,1)} %copy-done), kind=kOutput, calls=%fused_computation.55 | convolution fusion | flops 51545899008 | bytes 54525952 | tf_op jit(solution)/shard_map/tbsd,ed->tbse/dot_general | solution.py:285
  689.8 9.0 all-gather.32.cloned.1.call-done
  698.7 88.4 %fusion.48.qkv_ref = bf16[8,6,64,3072]{3,2,1,0:T(8,128)(2,1)} fusion(bf16[8,6,64,4096]{3,2,1,0:T(8,128)(2,1)} %bitcast.135, bf16[4096,3072]{1,0:T(8,128)(2,1)} %pick_columns.1), kind=kOutput, calls=%fused_computation.56 | convolution fusion | flops 77318848512 | bytes 69206016 | tf_op jit(solution)/shard_map/tbsd,de->tbse/dot_general | solution.py:284
  787.1 102.5 %attention_3.1 = (bf16[8,6,64,2048]{3,2,1,0:T(8,128)(2,1)}, bf16[8,6,64,3072]{3,2,1,0:T(8,128)(2,1)}) custom-call(bf16[8,6,64,3072]{3,2,1,0:T(8,128)(2,1)} %fusion.48.qkv_ref, bf16[8,6,64,2048]{3,2,1,0:T(8,128)(2,1)} %convert_bitcast_fusion.grad_ref, f32[512,128]{1,0:T(8,128)} %get-tuple-element.39.cos_ref, f32[512,128]{1,0:T(8,128)} %get-tuple-element.40.sin_ref), custom_call_target="tpu_custom_call" | custom-call | flops 38654705664 | bytes 62914560 | tf_op jit(solution)/shard_map/attention_3/pallas_call | solution.py:117
  889.6 21.0 %fusion.12 = f32[512,4096,1,1]{1,0,3,2:T(8,128)} fusion(bf16[8,6,64,4096]{3,2,1,0:T(8,128)(2,1)} %bitcast.138, bf16[8,6,64,2048]{3,2,1,0:T(8,128)(2,1)} %get-tuple-element.20.refs_3_.refs_7_, s32[]{:T(128)S(6)} %select_n.2), kind=kOutput, calls=%fused_computation.15 | convolution fusion | flops 12884901888 | bytes 36700164 | tf_op jit(solution)/shard_map/tbse,tbsd->ed/dot_general | solution.py:288
  910.7 20.9 %bitcast_add_fusion.3 = f32[512,4096]{1,0:T(8,128)} fusion(f32[512,4096,1,1]{1,0,3,2:T(8,128)} %fusion.12, f32[512,4096,1,1]{1,0,3,2:T(8,128)} %fusion.38, f32[512,4096,1,1]{1,0,3,2:T(8,128)} %fusion.51, bf16[8,4,64,4096]{3,2,1,0:T(8,128)(2,1)} %bitcast.130, bf16[8,4,64,2048]{3,2,1,0:T(8,128)(2,1)} %get-tuple-element.18.refs_1_.refs_5_, s32[]{:T(128)S(6)} %select_n.2), kind=kOutput, calls=%fused_computation.57 | convolution fusion | flops 8596226048 | bytes 52428804 | tf_op jit(solution)/shard_map/tbse,tbsd->ed/dot_general | solution.py:288
  931.6 61.9 %fusion.42 = f32[4096,3072,1,1]{1,0,3,2:T(8,128)} fusion(bf16[8,4,64,4096]{3,2,1,0:T(8,128)(2,1)} %bitcast.142, bf16[8,4,64,3072]{3,2,1,0:T(8,128)(2,1)} %get-tuple-element.25.refs_2_.refs_6_), kind=kOutput, calls=%fused_computation.49 | convolution fusion | flops 51539607552 | bytes 79691776 | tf_op jit(solution)/shard_map/tbsd,tbse->de/dot_general | solution.py:289
  993.4 62.0 %fusion.44 = f32[4096,3072,1,1]{1,0,3,2:T(8,128)} fusion(bf16[8,4,64,4096]{3,2,1,0:T(8,128)(2,1)} %bitcast.140, bf16[8,4,64,3072]{3,2,1,0:T(8,128)(2,1)} %get-tuple-element.24.refs_1_.refs_5_), kind=kOutput, calls=%fused_computation.51 | convolution fusion | flops 51539607552 | bytes 79691776 | tf_op jit(solution)/shard_map/tbsd,tbse->de/dot_general | solution.py:289
  1055.4 88.8 %fusion.14 = f32[4096,3072,1,1]{1,0,3,2:T(8,128)} fusion(bf16[8,6,64,4096]{3,2,1,0:T(8,128)(2,1)} %bitcast.136, bf16[8,6,64,3072]{3,2,1,0:T(8,128)(2,1)} %get-tuple-element.26.refs_3_.refs_7_), kind=kOutput, calls=%fused_computation.17 | convolution fusion | flops 77309411328 | bytes 94371840 | tf_op jit(solution)/shard_map/tbsd,tbse->de/dot_general | solution.py:289
  1144.2 69.4 %bitcast_add_fusion.mine_ref = f32[4096,3072]{1,0:T(8,128)} fusion(f32[4096,3072,1,1]{1,0,3,2:T(8,128)} %fusion.14, f32[4096,3072,1,1]{1,0,3,2:T(8,128)} %fusion.42, f32[4096,3072,1,1]{1,0,3,2:T(8,128)} %fusion.44, bf16[8,2,64,4096]{3,2,1,0:T(8,128)(2,1)} %bitcast.146, bf16[8,2,64,3072]{3,2,1,0:T(8,128)(2,1)} %get-tuple-element.23.refs_0_.refs_4_), kind=kOutput, calls=%fused_computation | convolution fusion | flops 25807552512 | bytes 216006656 | tf_op jit(solution)/shard_map/tbsd,tbse->de/dot_general | solution.py:289
  1214.5 7.8 pick_attention.1
  1222.5 10.4 pick_gradient.1
  1233.2 64.1 %collective-permute-done = bf16[16,64,2048]{2,1,0:T(8,128)(2,1)} collective-permute-done((bf16[16,64,2048]{2,1,0:T(8,128)(2,1)}, bf16[16,64,2048]{2,1,0:T(8,128)(2,1)}, u32[]{:S(2)}, u32[]{:S(2)}) %collective-permute-start) | collective-permute-done | bytes 4194336 | tf_op jit(solution)/shard_map/ppermute | solution.py:300
  1297.2 2.2 copy-done.1
  1299.4 8.1 join_attention.1
  1307.5 42.2 %fusion.29 = bf16[16,64,4096]{2,1,0:T(8,128)(2,1)} fusion(bf16[16,64,4096]{2,1,0:T(8,128)(2,1)} %param.7, bf16[16,64,4096]{2,1,0:T(8,128)(2,1)} %bitcast.134, bf16[4096,4096]{1,0:T(8,128)(2,1)} %in_ref.1), kind=kOutput, calls=%fused_computation.36 | convolution fusion | flops 34372321280 | bytes 58720256 | tf_op jit(solution)/shard_map/bse,ed->bsd/dot_general | solution.py:310
  1349.8 9.0 join_gradient.1
  1358.7 63.9 %fusion.27 = (f32[4096]{0:T(1024)S(1)}, f32[16,64]{1,0:T(8,128)S(1)}, bf16[16,64,4096]{2,1,0:T(8,128)(2,1)}) fusion(bf16[16,64,4096]{2,1,0:T(8,128)(2,1)} %param.7, f32[16,64]{1,0:T(8,128)S(1)} %copy-done.3, f32[4096]{0:T(1024)S(1)} %copy-done.4, bf16[16,64,6144]{2,1,0:T(8,128)(2,1)} %bitcast.131, bf16[4096,6144]{1,0:T(8,128)(2,1)} %value_ref.1), kind=kOutput, calls=%fused_computation.34 | convolution fusion | flops 51577352192 | bytes 79732736 | tf_op jit(solution)/shard_map/bse,de->bsd/dot_general | solution.py:314
  1422.6 22.4 %psum.7 = f32[4096]{0:T(1024)} all-reduce(f32[4096]{0:T(1024)S(1)} %get-tuple-element.29), channel_id=1, replica_groups=mesh['dp'=1,'sp'=8] {'sp'}, use_global_device_ids=true, to_apply=%region_3.0 | all-reduce | flops 4096 | bytes 32768 | tf_op jit(solution)/shard_map/psum | solution.py:323
  1445.0 13.7 fusion.24
  1458.7 72.9 %join_weights.1 = f32[4096,6144]{1,0:T(8,128)} custom-call(s32[1]{0:T(128)} %bitcast.core_ref, f32[4096,3072]{1,0:T(8,128)} %bitcast_add_fusion.mine_ref, f32[4096,3072]{1,0:T(8,128)} %collective-permute-done.2.other_ref), custom_call_target="tpu_custom_call" | custom-call | flops 805306368 | bytes 201326592 | tf_op jit(solution)/shard_map/join_weights/pallas_call | solution.py:154
  1531.6 44.1 %copy.90 = f32[4096,4096]{1,0:T(8,128)} copy(f32[4096,4096]{1,0:T(8,128)} %all-gather.18.cloned.1.call-done) | data formatting | bytes 134217728
  (54 shorter events, 4.8 us)
Async XLA Ops:
  7.2 104.1 %all-gather.22.cloned.1.call-start = ((), (), s32[]{:S(2)}) async-start(), calls=%async_computation.2 | async-start | bytes 9437184 | tf_op jit(solution)/shard_map/all_gather | solution.py:277
  9.5 125.5 %all-gather.20.cloned.1.call-start = ((), (), s32[]{:S(2)}) async-start(), calls=%async_computation.1 | async-start | bytes 9437184 | tf_op jit(solution)/shard_map/all_gather | solution.py:276
  14.7 0.6 copy-start.2
  27.7 187.7 %all-gather.30.cloned.1.call-start = ((), (), s32[]{:S(2)}) async-start(), calls=%async_computation.6 | async-start | bytes 18874368 | tf_op jit(solution)/shard_map/all_gather | solution.py:277
  32.5 14.2 copy-start.5
  32.5 14.2 copy-start.6
  32.5 251.7 %all-gather.24.cloned.1.call-start = ((), (), s32[]{:S(2)}) async-start(), calls=%async_computation.3 | async-start | bytes 18874368 | tf_op jit(solution)/shard_map/all_gather | solution.py:276
  37.4 332.6 %all-gather.28.cloned.1.call-start = ((), (), s32[]{:S(2)}) async-start(), calls=%async_computation.5 | async-start | bytes 18874368 | tf_op jit(solution)/shard_map/all_gather | solution.py:276
  38.0 478.0 %all-gather.26.cloned.1.call-start = ((), (), s32[]{:S(2)}) async-start(), calls=%async_computation.4 | async-start | bytes 18874368 | tf_op jit(solution)/shard_map/all_gather | solution.py:277
  38.6 589.4 %all-gather.34.cloned.1.call-start = ((), (), s32[]{:S(2)}) async-start(), calls=%async_computation.8 | async-start | bytes 28311552 | tf_op jit(solution)/shard_map/all_gather | solution.py:277
  42.6 656.1 %all-gather.32.cloned.1.call-start = ((), (), s32[]{:S(2)}) async-start(), calls=%async_computation.7 | async-start | bytes 28311552 | tf_op jit(solution)/shard_map/all_gather | solution.py:276
  46.6 1485.0 %all-gather.18.cloned.1.call-start = ((), (), s32[]{:S(2)}) async-start(), calls=%async_computation | async-start | bytes 75497472 | tf_op jit(solution)/shard_map/all_gather | solution.py:294
  80.7 6.2 copy-start
  1213.7 245.0 %collective-permute-start.2 = (f32[4096,3072]{1,0:T(8,128)}, f32[4096,3072]{1,0:T(8,128)}, u32[]{:S(2)}, u32[]{:S(2)}) collective-permute-start(f32[4096,3072]{1,0:T(8,128)} %bitcast_add_fusion.mine_ref), channel_id=1, source_target_pairs={{0,1},{1,0},{2,3},{3,2},{4,5},{5,4},{6,7},{7,6}} | collective-permute-start | bytes 150994944 | tf_op jit(solution)/shard_map/ppermute | solution.py:295
  1222.3 75.0 %collective-permute-start = (bf16[16,64,2048]{2,1,0:T(8,128)(2,1)}, bf16[16,64,2048]{2,1,0:T(8,128)(2,1)}, u32[]{:S(2)}, u32[]{:S(2)}) collective-permute-start(bf16[16,64,2048]{2,1,0:T(8,128)(2,1)} %get-tuple-element.22), channel_id=1, source_target_pairs={{0,1},{1,0},{2,3},{3,2},{4,5},{5,4},{6,7},{7,6}} | collective-permute-start | bytes 12582920 | tf_op jit(solution)/shard_map/ppermute | solution.py:300
  1232.9 116.8 %collective-permute-start.1 = (bf16[16,64,3072]{2,1,0:T(8,128)(2,1)}, bf16[16,64,3072]{2,1,0:T(8,128)(2,1)}, u32[]{:S(2)}, u32[]{:S(2)}) collective-permute-start(bf16[16,64,3072]{2,1,0:T(8,128)(2,1)} %get-tuple-element.28), channel_id=1, source_target_pairs={{0,1},{1,0},{2,3},{3,2},{4,5},{5,4},{6,7},{7,6}} | collective-permute-start | bytes 18874376 | tf_op jit(solution)/shard_map/ppermute | solution.py:301
  1297.2 2.2 copy-start.1
  1299.4 50.3 %slice-start = ((s8[6291456]{0:T(1024)(128)(4,1)}), s8[4194304]{0:T(1024)(128)(4,1)S(1)}, s32[]{:S(2)}) async-start(s8[6291456]{0:T(1024)(128)(4,1)} %bitcast.125), calls=%async_computation.9 | async-start | bytes 8388608
  1307.5 42.2 %slice-start.1 = ((s8[6291456]{0:T(1024)(128)(4,1)}), s8[2097152]{0:T(1024)(128)(4,1)S(1)}, s32[]{:S(2)}) async-start(s8[6291456]{0:T(1024)(128)(4,1)} %bitcast.125), calls=%async_computation.10 | async-start | bytes 4194304
  1349.7 9.0 copy-start.3
  1349.7 9.0 copy-start.4
Sparse Core Ops, SparseCore 0:
  10.4 51.6 all-gather.21
  63.9 48.4 all-gather.19
  114.3 84.0 all-gather.29
  200.1 84.0 all-gather.23
  285.8 84.0 all-gather.27
  371.6 84.0 all-gather.25
  457.5 119.6 all-gather.33
  579.0 119.6 all-gather.31
  931.7 301.8 all-gather.17

commit v2 on v1

--- a/solution.py
+++ b/solution.py
@@ -11,7 +11,7 @@
 ROPE_BASE = 10000.0
 ROPE_SCALE = math.sqrt(1.0 + math.log(32.0) / math.log(4096.0))
 LOG2_E = math.log2(math.e)
-CHUNKS = (2, 4, 4, 6)
+CHUNKS = (2, 5, 5, 4)
 
 
 def rope_tables(positions, long_factor):
@@ -24,7 +24,7 @@
     return jnp.concatenate([cos_half, cos_half], axis=-1), jnp.concatenate([-sin_half, sin_half], axis=-1)
 
 
-def attention_kernel(qkv_ref, grad_ref, cos_ref, sin_ref, out_ref, dqkv_ref, query_s, dkey_s, dvalue_s):
+def attention_kernel(qkv_ref, grad_ref, cos_ref, sin_ref, out_ref, dquery_ref, dkv_ref, dkey_s, dvalue_s):
     devs, _, sub, width = qkv_ref.shape
     dim = cos_ref.shape[1]
     seq = devs * sub
@@ -32,7 +32,6 @@
     block = 128
     per = block // sub
     scale = dim ** -0.5
-    cols = group * block
 
     def rope(vals, cos, sin):
         wide = vals.astype(jnp.float32)
@@ -53,54 +52,85 @@
     key = rope(key_raw, cos_ref[...], sin_ref[...])
     key_t = key.T
     value_t = value.T
+    heads_unit = 2
+    cols = heads_unit * block
     row_ids = lax.broadcasted_iota(jnp.int32, (block, cols), 0)
     col_ids = lax.broadcasted_iota(jnp.int32, (block, cols), 1)
     allowed = row_ids <= lax.rem(col_ids, block)
-
-    for step in reversed(range(seq // block)):
+    units = [(step, first) for step in reversed(range(seq // block)) for first in range(0, group, heads_unit)]
+    state = {}
+
+    def load(unit):
+        step, first = units[unit]
         rows = pl.ds(step * block, block)
         cos = cos_ref[rows, :]
         sin = sin_ref[rows, :]
         span = (step + 1) * block
+        queries = []
         grads = []
-        for head in range(group):
+        for head in range(first, first + heads_unit):
             lanes = pl.ds(head * dim, dim)
             raw = qkv_ref[step * per:(step + 1) * per, 0, :, lanes].reshape(block, dim)
-            query_s[head * block:(head + 1) * block, :] = rope(raw, cos, sin)
+            queries.append(rope(raw, cos, sin))
             grads.append(grad_ref[step * per:(step + 1) * per, 0, :, lanes].reshape(block, dim))
-        query = query_s[...]
+        query = jnp.concatenate(queries, axis=0)
         grad = jnp.concatenate(grads, axis=0)
         scores = nt(key[:span], query)
+        grad_probs = nt(value[:span], grad).astype(jnp.bfloat16)
+        state[unit] = (query, grad, scores, grad_probs)
+
+    def soften(unit):
+        step, first = units[unit]
+        span = (step + 1) * block
+        query, grad, scores, grad_probs = state[unit]
         last = jnp.where(allowed, scores[span - block:], -jnp.inf)
         scores = last if step == 0 else jnp.concatenate([scores[:span - block], last], axis=0)
         peak = jnp.max(scores, axis=0, keepdims=True)
         weights = jnp.exp2((scores - peak) * (scale * LOG2_E))
         probs = weights * (1.0 / jnp.sum(weights, axis=0, keepdims=True))
-        probs_low = probs.astype(jnp.bfloat16)
-        attn = nn(value_t[:, :span], probs_low).astype(jnp.bfloat16).T
-        grad_probs = nt(value[:span], grad).astype(jnp.bfloat16).astype(jnp.float32)
+        grad_probs = grad_probs.astype(jnp.float32)
         row_dot = jnp.sum(grad_probs * probs, axis=0, keepdims=True)
         grad_scores = (probs * (grad_probs - row_dot)).astype(jnp.bfloat16)
+        state[unit] = (query, grad, probs.astype(jnp.bfloat16), grad_scores)
+
+    def finish(unit):
+        step, first = units[unit]
+        rows = pl.ds(step * block, block)
+        cos = cos_ref[rows, :]
+        sin = sin_ref[rows, :]
+        span = (step + 1) * block
+        query, grad, probs_low, grad_scores = state.pop(unit)
+        attn = nn(value_t[:, :span], probs_low).astype(jnp.bfloat16).T
         grad_query = (nn(key_t[:, :span], grad_scores) * scale).astype(jnp.bfloat16).T
         part_value = nn(probs_low, grad)
         part_key = nn(grad_scores, query)
-        if span == seq:
+        if unit == 0:
             dvalue_s[...] = part_value
             dkey_s[...] = part_key
         else:
             dvalue_s[:span, :] += part_value
             dkey_s[:span, :] += part_key
-        for head in range(group):
-            lanes = pl.ds(head * dim, dim)
+        for head in range(heads_unit):
+            lanes = pl.ds((first + head) * dim, dim)
             part = slice(head * block, (head + 1) * block)
             out_ref[step * per:(step + 1) * per, 0, :, lanes] = attn[part].reshape(per, sub, dim)
             back = rope_back(grad_query[part], cos, sin)
-            dqkv_ref[step * per:(step + 1) * per, 0, :, lanes] = back.reshape(per, sub, dim)
+            dquery_ref[step * per:(step + 1) * per, 0, :, lanes] = back.reshape(per, sub, dim)
+
+    count = len(units)
+    load(0)
+    for unit in range(count + 1):
+        if unit < count:
+            soften(unit)
+        if unit + 1 < count:
+            load(unit + 1)
+        if unit > 0:
+            finish(unit - 1)
 
     grad_key = (dkey_s[...] * scale).astype(jnp.bfloat16)
     back = rope_back(grad_key, cos_ref[...], sin_ref[...])
-    dqkv_ref[:, 0, :, group * dim:(group + 1) * dim] = back.reshape(devs, sub, dim)
-    dqkv_ref[:, 0, :, (group + 1) * dim:] = dvalue_s[...].astype(jnp.bfloat16).reshape(devs, sub, dim)
+    dkv_ref[:, 0, :, :dim] = back.reshape(devs, sub, dim)
+    dkv_ref[:, 0, :, dim:] = dvalue_s[...].astype(jnp.bfloat16).reshape(devs, sub, dim)
 
 
 def attention(qkv, grad, cos, sin, heads, name):
@@ -119,10 +149,10 @@
         name=name,
         grid=(count, heads),
         in_specs=[head_spec(per_head), head_spec(group * dim), table_spec, table_spec],
-        out_specs=[head_spec(group * dim), head_spec(per_head)],
-        out_shape=[jax.ShapeDtypeStruct(grad.shape, jnp.bfloat16), jax.ShapeDtypeStruct(qkv.shape, jnp.bfloat16)],
-        scratch_shapes=[pltpu.VMEM((group * 128, dim), jnp.bfloat16),
-                        pltpu.VMEM((seq, dim), jnp.float32), pltpu.VMEM((seq, dim), jnp.float32)],
+        out_specs=[head_spec(group * dim), head_spec(group * dim), head_spec(2 * dim)],
+        out_shape=[jax.ShapeDtypeStruct((devs, count, sub, heads * cols), jnp.bfloat16)
+                   for cols in (group * dim, group * dim, 2 * dim)],
+        scratch_shapes=[pltpu.VMEM((seq, dim), jnp.float32), pltpu.VMEM((seq, dim), jnp.float32)],
         compiler_params=pltpu.CompilerParams(vmem_limit_bytes=56 * 1024 * 1024),
         cost_estimate=pl.CostEstimate(flops=count * heads * group * 6 * 2 * seq * seq * dim,
                                       bytes_accessed=4 * (qkv.size + grad.size),
@@ -130,38 +160,80 @@
     )(qkv, grad, cos, sin)
 
 
-def join_kernel(parts, heads, core_ref, mine_ref, other_ref, out_ref):
+def join_kernel(parts, heads, core_ref, *refs):
     first = core_ref[0] == 0
-    width = sum(parts)
-    start = 0
+    out_ref = refs[-1]
     base = 0
-    for cols in parts:
-        for head in range(heads):
-            lanes = slice(head * width + start, head * width + start + cols)
-            mine = mine_ref[:, lanes]
-            other = other_ref[:, lanes]
-            at = base + 2 * head * cols
-            out_ref[:, at:at + cols] = jnp.where(first, mine, other)
-            out_ref[:, at + cols:at + 2 * cols] = jnp.where(first, other, mine)
-        start += cols
-        base += 2 * heads * cols
-
-
-def join_columns(core, mine, other, parts, heads, name):
-    rows, half = mine.shape
+    for index, group_parts in enumerate(parts):
+        mine_ref, other_ref = refs[2 * index], refs[2 * index + 1]
+        width = sum(group_parts)
+        start = 0
+        for cols in group_parts:
+            for head in range(heads):
+                lanes = slice(head * width + start, head * width + start + cols)
+                mine = mine_ref[:, lanes]
+                other = other_ref[:, lanes]
+                at = base + 2 * head * cols
+                out_ref[:, at:at + cols] = jnp.where(first, mine, other)
+                out_ref[:, at + cols:at + 2 * cols] = jnp.where(first, other, mine)
+            start += cols
+            base += 2 * heads * cols
+
+
+def join_columns(core, pairs, parts, heads, name):
+    arrays = [array for pair in pairs for array in pair]
+    rows = arrays[0].shape[0]
+    total = sum(array.shape[1] for array in arrays)
     tile = 128
-    spec = pl.BlockSpec((tile, half), lambda t, core_ref: (t, 0))
     return pl.pallas_call(
         functools.partial(join_kernel, parts, heads),
         name=name,
         grid_spec=pltpu.PrefetchScalarGridSpec(
-            num_scalar_prefetch=1, grid=(rows // tile,), in_specs=[spec, spec],
-            out_specs=pl.BlockSpec((tile, 2 * half), lambda t, core_ref: (t, 0))),
-        out_shape=jax.ShapeDtypeStruct((rows, 2 * half), mine.dtype),
+            num_scalar_prefetch=1, grid=(rows // tile,),
+            in_specs=[pl.BlockSpec((tile, array.shape[1]), lambda t, core_ref: (t, 0)) for array in arrays],
+            out_specs=pl.BlockSpec((tile, total), lambda t, core_ref: (t, 0))),
+        out_shape=jax.ShapeDtypeStruct((rows, total), arrays[0].dtype),
         compiler_params=pltpu.CompilerParams(vmem_limit_bytes=40 * 1024 * 1024),
-        cost_estimate=pl.CostEstimate(flops=rows * half * 64, bytes_accessed=4 * rows * half * mine.dtype.itemsize,
+        cost_estimate=pl.CostEstimate(flops=rows * total * 32, bytes_accessed=2 * rows * total * arrays[0].dtype.itemsize,
                                       transcendentals=0),
-    )(core, mine, other)
+    )(core, *arrays)
+
+
+def join_weights_kernel(heads, core_ref, mine_ref, other_ref, kv_ref, out_ref):
+    first = core_ref[0] == 0
+    cols = mine_ref.shape[1] // heads
+    dim = kv_ref.shape[2] // 2
+    for head in range(heads):
+        lanes = slice(head * cols, (head + 1) * cols)
+        mine = mine_ref[:, lanes]
+        other = other_ref[:, lanes]
+        at = 2 * head * cols
+        out_ref[:, at:at + cols] = jnp.where(first, mine, other)
+        out_ref[:, at + cols:at + 2 * cols] = jnp.where(first, other, mine)
+    base = 2 * heads * cols
+    for head in range(2 * heads):
+        out_ref[:, base + head * dim:base + (head + 1) * dim] = kv_ref[head, :, :dim]
+        at = base + (2 * heads + head) * dim
+        out_ref[:, at:at + dim] = kv_ref[head, :, dim:]
+
+
+def join_weights(core, mine, other, kv_all, heads):
+    rows, half = mine.shape
+    total = 2 * half + kv_all.shape[0] * kv_all.shape[2]
+    tile = 128
+    spec = pl.BlockSpec((tile, half), lambda t, core_ref: (t, 0))
+    return pl.pallas_call(
+        functools.partial(join_weights_kernel, heads),
+        name='join_weights',
+        grid_spec=pltpu.PrefetchScalarGridSpec(
+            num_scalar_prefetch=1, grid=(rows // tile,),
+            in_specs=[spec, spec,
+                      pl.BlockSpec((kv_all.shape[0], tile, kv_all.shape[2]), lambda t, core_ref: (0, t, 0))],
+            out_specs=pl.BlockSpec((tile, total), lambda t, core_ref: (t, 0))),
+        out_shape=jax.ShapeDtypeStruct((rows, total), mine.dtype),
+        compiler_params=pltpu.CompilerParams(vmem_limit_bytes=40 * 1024 * 1024),
+        cost_estimate=pl.CostEstimate(flops=rows * total * 32, bytes_accessed=8 * rows * total, transcendentals=0),
+    )(core, mine, other, kv_all)
 
 
 def pick_columns_kernel(core_ref, query_ref, key_ref, value_ref, out_ref):
@@ -244,6 +316,14 @@
         cost_estimate=pl.CostEstimate(flops=batch * sub * width * 64, bytes_accessed=8 * batch * sub * width,
                                       transcendentals=0),
     )(devs, *chunks, *chunks)
+
+
+def exchange_sum(part, devs):
+    bit = 1
+    while bit < devs:
+        part = part + lax.ppermute(part, 'sp', [(d, d ^ bit) for d in range(devs)])
+        bit *= 2
+    return part
 
 
 def block_body(hidden, positions, long_factor, norm_weight, w_qkv, w_out, grad_out):
@@ -268,7 +348,8 @@
     core_ref = core.reshape(1)
     w_own = pick_columns(core_ref, w_qkv, mine_heads, group, dim)
     wo_own = pick_rows(core_ref, w_out, mine_heads, group * dim)
-    cos, sin = rope_tables(lax.all_gather(positions, 'sp', axis=0, tiled=True), long_factor)
+    spread = lax.dynamic_update_slice(jnp.zeros((devs * sub,), positions.dtype), positions, (me * sub,))
+    cos, sin = rope_tables(exchange_sum(spread, devs), long_factor)
 
     gathered = []
     start = 0
@@ -277,40 +358,55 @@
                          lax.all_gather(grad_out[start:start + count], 'sp', axis=0)))
         start += count
 
-    grad_wqkv = None
+    grad_wq = []
+    grad_wkv = None
     grad_wout = None
     tokens = []
+    last = len(CHUNKS) - 1
     for index, (normed_all, grad_all) in enumerate(gathered):
+        if index > 0:
+            attn, grad_all = lax.optimization_barrier((tokens[-1][0], grad_all))
+            tokens[-1] = (attn,) + tokens[-1][1:]
+        grad_attn = jnp.einsum('tbsd,ed->tbse', grad_all, wo_own, preferred_element_type=jnp.float32).astype(jnp.bfloat16)
+        grad_attn, normed_all = lax.optimization_barrier((grad_attn, normed_all))
+        if index == 1:
+            grad_wq[-1], grad_wkv, grad_wout, normed_all = lax.optimization_barrier(
+                (grad_wq[-1], grad_wkv, grad_wout, normed_all))
         qkv = jnp.einsum('tbsd,de->tbse', normed_all, w_own, preferred_element_type=jnp.float32).astype(jnp.bfloat16)
-        grad_attn = jnp.einsum('tbsd,ed->tbse', grad_all, wo_own, preferred_element_type=jnp.float32).astype(jnp.bfloat16)
-        attn, grad_qkv = attention(qkv, grad_attn, cos, sin, mine_heads, f'attention_{index}')
+        attn, grad_query, grad_kv = attention(qkv, grad_attn, cos, sin, mine_heads, f'attention_{index}')
+        tokens.append((attn, grad_query, grad_kv))
+        kv_slice = lax.dynamic_slice_in_dim(grad_kv, chip * 2 * dim, 2 * dim, axis=3)
+        part_kv = jnp.einsum('tbsd,tbse->de', normed_all, kv_slice, preferred_element_type=jnp.float32)
+        grad_wkv = part_kv if grad_wkv is None else grad_wkv + part_kv
         attn_slice = lax.dynamic_slice_in_dim(attn, chip * group * dim, group * dim, axis=3)
+        if index == last:
+            grad_wkv, attn_slice = lax.optimization_barrier((grad_wkv, attn_slice))
         part_out = jnp.einsum('tbse,tbsd->ed', attn_slice, grad_all, preferred_element_type=jnp.float32)
-        part_qkv = jnp.einsum('tbsd,tbse->de', normed_all, grad_qkv, preferred_element_type=jnp.float32)
         grad_wout = part_out if grad_wout is None else grad_wout + part_out
-        grad_wqkv = part_qkv if grad_wqkv is None else grad_wqkv + part_qkv
-        tokens.append((attn, grad_qkv))
-
+        if index == last:
+            ends = jnp.stack([me, partner])
+            picked = [pick_tokens(ends, list(parts), name) for parts, name in
+                      zip(zip(*tokens), ('pick_attention', 'pick_query', 'pick_kv'))]
+            others = [lax.ppermute(pair[1], 'sp', pairs) for pair in picked]
+            *others, grad_query = lax.optimization_barrier((*others, grad_query))
+        part_q = jnp.einsum('tbsd,tbse->de', normed_all, grad_query, preferred_element_type=jnp.float32)
+        grad_wq.append(part_q if not grad_wq else grad_wq[-1] + part_q)
+
+    grad_wq_other = lax.ppermute(grad_wq[-1], 'sp', pairs)
+    grad_wkv_all = lax.all_gather(grad_wkv, 'sp', axis=0)
     grad_wout = lax.all_gather(grad_wout, 'sp', axis=0, tiled=True)
-    grad_wqkv_other = lax.ppermute(grad_wqkv, 'sp', pairs)
-
-    ends = jnp.stack([me, partner])
-    attn_mine, attn_send = pick_tokens(ends, [pair[0] for pair in tokens], 'pick_attention')
-    dqkv_mine, dqkv_send = pick_tokens(ends, [pair[1] for pair in tokens], 'pick_gradient')
-    attn_other = lax.ppermute(attn_send, 'sp', pairs)
-    dqkv_other = lax.ppermute(dqkv_send, 'sp', pairs)
-
-    def natural(mine, other, parts, name):
+
+    def natural(indices, parts, name):
         rows = (batch * sub, -1)
-        joined = join_columns(core_ref, mine.reshape(rows), other.reshape(rows), parts, mine_heads, name)
+        joined = join_columns(core_ref, [(picked[i][0].reshape(rows), others[i].reshape(rows)) for i in indices],
+                              parts, mine_heads, name)
         return joined.reshape(batch, sub, -1)
 
-    parts = (group * dim, dim, dim)
-    attn_flat = natural(attn_mine, attn_other, parts[:1], 'join_attention')
+    attn_flat = natural((0,), ((group * dim,),), 'join_attention')
     mixed_out = jnp.einsum('bse,ed->bsd', attn_flat, w_out, preferred_element_type=jnp.float32)
     out_hidden = (hidden_wide + mixed_out).astype(jnp.bfloat16)
 
-    grad_qkv = natural(dqkv_mine, dqkv_other, parts, 'join_gradient')
+    grad_qkv = natural((1, 2), ((group * dim,), (dim, dim)), 'join_gradient')
     grad_normed = jnp.einsum('bse,de->bsd', grad_qkv, w_qkv, preferred_element_type=jnp.float32)
     grad_normed = grad_normed.astype(jnp.bfloat16).astype(jnp.float32)
     unit_hidden = hidden_wide * inv_rms
@@ -319,8 +415,8 @@
     grad_inner = inv_rms * (grad_unit - unit_hidden * jnp.mean(grad_unit * unit_hidden, axis=-1, keepdims=True))
     grad_hidden = (grad_out.astype(jnp.float32) + grad_inner).astype(jnp.bfloat16)
 
-    grad_wqkv = join_columns(core_ref, grad_wqkv, grad_wqkv_other, parts, mine_heads, 'join_weights')
-    return out_hidden, grad_hidden, lax.psum(grad_norm, 'sp'), grad_wqkv, grad_wout
+    grad_wqkv = join_weights(core_ref, grad_wq[-1], grad_wq_other, grad_wkv_all, mine_heads)
+    return out_hidden, grad_hidden, exchange_sum(grad_norm, devs), grad_wqkv, grad_wout
 
 
 def solution(mesh):

time: 1590 us -> 1370 us (0.86)
  Pallas kernels: 415 us -> 337 us
  waiting for transfers between devices: 125 us -> 75.1 us
  blocking collectives: 48.1 us -> 0 us
  matrix products: 872 us -> 826 us
    pallas_call x4, Pallas kernels: 277 us -> 195 us  [attention(): pl.pallas_call(attention_kernel, name=name, grid=(count, heads), in_specs...]
    pallas_call x0 -> x1, Pallas kernels: none -> 73 us  [join_weights(): pl.pallas_call(functools.partial(join_weights_kernel, heads), name='join_...]
    pallas_call x3 -> x2, Pallas kernels: 90 us -> 18.5 us  [join_columns(): pl.pallas_call(functools.partial(join_kernel, parts, heads), name=name, g...]
    ppermute x3 -> x10, waiting for transfers between devices: 64.1 us -> 2.7 us  [the longest x6 2.69 us: exchange_sum(): part = part + lax.ppermute(part, 'sp', [(d, d ^ bit) for d in range(devs)])]
    dot_general x4 -> x8, matrix products: 282 us -> 239 us  [the longest x4 194 us: block_body(): jnp.einsum('tbsd,tbse->de', normed_all, grad_query, preferred_element_typ...]
    unnamed x1 -> x0, blocking collectives: 25.7 us -> none
    psum x1 -> x0, blocking collectives: 22.4 us -> none  [block_body(): lax.psum(grad_norm, 'sp')]
    unnamed x21 -> x35, local copies, waits for them, and re-layouts: 53.3 us -> 52.7 us
  transfers between devices with their start and end apart: 12 -> 20, of which waited for: 4 -> 4; matrix products, arithmetic and copies ran while one was open for 50% -> 57% of each run, Pallas kernels for 20% -> 21%
where the time goes in v2:
time: 1370 us
  matrix products  826 us (60%)
  Pallas kernels  337 us (25%)
  local copies, waits for them, and re-layouts  76.6 us (6%)
  waiting for transfers between devices  75.1 us (5%)
  other arithmetic  29.4 us (2%)
  between operations  14.7 us (1%)
    dot_general x4, matrix products, block_body(): jnp.einsum('tbsd,de->tbse', normed_all, w_own, preferred_element_type=jnp...  243 us
    pallas_call x4, Pallas kernels, attention(): pl.pallas_call(attention_kernel, name=name, grid=(count, heads), in_specs...  195 us
    dot_general x4, matrix products, block_body(): jnp.einsum('tbsd,tbse->de', normed_all, grad_query, preferred_element_typ...  194 us
    dot_general x4, matrix products, block_body(): jnp.einsum('tbsd,ed->tbse', grad_all, wo_own, preferred_element_type=jnp....  172 us
    pallas_call x1, Pallas kernels, join_weights(): pl.pallas_call(functools.partial(join_weights_kernel, heads), name='join_...  73 us
    all_gather x4, waiting for transfers between devices, block_body(): lax.all_gather(normed[start:start + count], 'sp', axis=0)  70.8 us
    dot_general x4, matrix products, block_body(): jnp.einsum('tbse,tbsd->ed', attn_slice, grad_all, preferred_element_type=...  65 us
    dot_general x1, matrix products, block_body(): jnp.einsum('bse,de->bsd', grad_qkv, w_qkv, preferred_element_type=jnp.flo...  63.8 us
  transfers between devices with their start and end apart: 20, of which 4 were waited for; matrix products, arithmetic and copies ran while one was open for 57% of the time, Pallas kernels for 21%

profile of v2, /device:TPU:0, one launch (start us, length us, event | category | flops | bytes accessed | tf_op | source)
XLA Modules:
  0.0 1366.8 jit_solution(1055539498419914335)
XLA Ops:
  7.2 2.3 slice.24
  9.6 5.1 fusion.35
  15.3 10.5 fusion.32
  28.2 5.5 fusion.125
  33.7 5.6 fusion.124
  40.5 3.1 slice.30
  44.9 3.1 slice.35
  48.4 2.5 collective-permute-start.1
  51.0 22.4 %pick_columns.1 = bf16[4096,3072]{1,0:T(8,128)(2,1)} custom-call(s32[1]{0:T(128)} %bitcast.core_ref, bf16[4096,6144]{1,0:T(8,128)(2,1)} %value_ref.1, bf16[4096,6144]{1,0:T(8,128)(2,1)} %value_ref.1, bf16[4096,6144]{1,0:T(8,128)(2,1)} %value_ref.1), custom_call_target="tpu_custom_call" | custom-call | flops 402653184 | bytes 50331648 | tf_op jit(solution)/shard_map/pick_columns/pallas_call | solution.py:252
  74.9 8.0 pick_rows.1
  82.9 5.8 copy-done
  90.7 23.7 %convert_bitcast_fusion.grad_ref = bf16[8,2,64,2048]{3,2,1,0:T(8,128)(2,1)} fusion(bf16[8,2,64,4096]{3,2,1,0:T(8,128)(2,1)} %bitcast.155, bf16[2048,4096]{1,0:T(8,128)(2,1)} %copy-done), kind=kOutput, calls=%fused_computation.86 | convolution fusion | flops 17181966336 | bytes 29360128 | tf_op jit(solution)/shard_map/tbsd,ed->tbse/dot_general | solution.py:370
  114.5 33.0 %fusion.83.qkv_ref = bf16[8,2,64,3072]{3,2,1,0:T(8,128)(2,1)} fusion(bf16[8,2,64,4096]{3,2,1,0:T(8,128)(2,1)} %bitcast.173, bf16[4096,3072]{1,0:T(8,128)(2,1)} %pick_columns.1), kind=kOutput, calls=%fused_computation.76 | convolution fusion | flops 25772949504 | bytes 39845888 | tf_op jit(solution)/shard_map/tbsd,de->tbse/dot_general | solution.py:375
  147.5 25.9 %attention_0.1 = (bf16[8,2,64,2048]{3,2,1,0:T(8,128)(2,1)}, bf16[8,2,64,2048]{3,2,1,0:T(8,128)(2,1)}, bf16[8,2,64,1024]{3,2,1,0:T(8,128)(2,1)}) custom-call(bf16[8,2,64,3072]{3,2,1,0:T(8,128)(2,1)} %fusion.83.qkv_ref, bf16[8,2,64,2048]{3,2,1,0:T(8,128)(2,1)} %convert_bitcast_fusion.grad_ref, f32[512,128]{1,0:T(8,128)} %get-tuple-element.99.cos_ref, ...), custom_call_target="tpu_custom_call" | custom-call | flops 12884901888 | bytes 20971520 | tf_op jit(solution)/shard_map/attention_0/pallas_call | solution.py:147
  173.3 25.9 %convolution_bitcast_fusion = f32[4096,2048]{1,0:T(8,128)} fusion(bf16[8,2,64,4096]{3,2,1,0:T(8,128)(2,1)} %bitcast.174, bf16[8,2,64,2048]{3,2,1,0:T(8,128)(2,1)} %get-tuple-element.51.refs_0_.refs_4_), kind=kOutput, calls=%fused_computation.36 | convolution fusion | flops 17179869184 | bytes 46137344 | tf_op jit(solution)/shard_map/tbsd,tbse->de/dot_general | solution.py:392
  199.3 7.9 fusion.86
  207.2 8.5 fusion.72
  216.1 52.7 %fusion.77.grad_ref = bf16[8,5,64,2048]{3,2,1,0:T(8,128)(2,1)} fusion(bf16[8,5,64,4096]{3,2,1,0:T(8,128)(2,1)} %bitcast.166, bf16[2048,4096]{1,0:T(8,128)(2,1)} %copy-done), kind=kOutput, calls=%fused_computation.74 | convolution fusion | flops 42954915840 | bytes 48234496 | tf_op jit(solution)/shard_map/tbsd,ed->tbse/dot_general | solution.py:370
  268.8 50.9 %all-gather.28.cloned.1.call-done = bf16[40,64,4096]{2,1,0:T(8,128)(2,1)} async-done(((bf16[5,64,4096]{2,1,0:T(8,128)(2,1)}), bf16[40,64,4096]{2,1,0:T(8,128)(2,1)}) %all-gather.28.cloned.1.call-update) | async-done | bytes 20971536 | tf_op jit(solution)/shard_map/all_gather | solution.py:357
  319.6 74.4 %fusion.52.qkv_ref = bf16[8,5,64,3072]{3,2,1,0:T(8,128)(2,1)} fusion(bf16[8,5,64,4096]{3,2,1,0:T(8,128)(2,1)} %bitcast.160, bf16[4096,3072]{1,0:T(8,128)(2,1)} %pick_columns.1), kind=kOutput, calls=%fused_computation.60 | convolution fusion | flops 64432373760 | bytes 61865984 | tf_op jit(solution)/shard_map/tbsd,de->tbse/dot_general | solution.py:375
  394.0 59.9 %attention_1.1 = (bf16[8,5,64,2048]{3,2,1,0:T(8,128)(2,1)}, bf16[8,5,64,2048]{3,2,1,0:T(8,128)(2,1)}, bf16[8,5,64,1024]{3,2,1,0:T(8,128)(2,1)}) custom-call(bf16[8,5,64,3072]{3,2,1,0:T(8,128)(2,1)} %fusion.52.qkv_ref, bf16[8,5,64,2048]{3,2,1,0:T(8,128)(2,1)} %fusion.77.grad_ref, f32[512,128]{1,0:T(8,128)} %get-tuple-element.99.cos_ref, ...), custom_call_target="tpu_custom_call" | custom-call | flops 32212254720 | bytes 52428800 | tf_op jit(solution)/shard_map/attention_1/pallas_call | solution.py:147
  454.0 52.9 %fusion.80.grad_ref = bf16[8,5,64,2048]{3,2,1,0:T(8,128)(2,1)} fusion(bf16[8,5,64,4096]{3,2,1,0:T(8,128)(2,1)} %bitcast.168, bf16[2048,4096]{1,0:T(8,128)(2,1)} %copy-done), kind=kOutput, calls=%fused_computation.75 | convolution fusion | flops 42954915840 | bytes 48234496 | tf_op jit(solution)/shard_map/tbsd,ed->tbse/dot_general | solution.py:370
  506.8 19.9 %all-gather.32.cloned.1.call-done = bf16[40,64,4096]{2,1,0:T(8,128)(2,1)} async-done(((bf16[5,64,4096]{2,1,0:T(8,128)(2,1)}), bf16[40,64,4096]{2,1,0:T(8,128)(2,1)}) %all-gather.32.cloned.1.call-update) | async-done | bytes 20971536 | tf_op jit(solution)/shard_map/all_gather | solution.py:357
  526.7 74.2 %fusion.55.qkv_ref = bf16[8,5,64,3072]{3,2,1,0:T(8,128)(2,1)} fusion(bf16[8,5,64,4096]{3,2,1,0:T(8,128)(2,1)} %bitcast.163, bf16[4096,3072]{1,0:T(8,128)(2,1)} %pick_columns.1), kind=kOutput, calls=%fused_computation.61 | convolution fusion | flops 64432373760 | bytes 61865984 | tf_op jit(solution)/shard_map/tbsd,de->tbse/dot_general | solution.py:375
  601.0 60.0 %attention_2.1 = (bf16[8,5,64,2048]{3,2,1,0:T(8,128)(2,1)}, bf16[8,5,64,2048]{3,2,1,0:T(8,128)(2,1)}, bf16[8,5,64,1024]{3,2,1,0:T(8,128)(2,1)}) custom-call(bf16[8,5,64,3072]{3,2,1,0:T(8,128)(2,1)} %fusion.55.qkv_ref, bf16[8,5,64,2048]{3,2,1,0:T(8,128)(2,1)} %fusion.80.grad_ref, f32[512,128]{1,0:T(8,128)} %get-tuple-element.99.cos_ref, ...), custom_call_target="tpu_custom_call" | custom-call | flops 32212254720 | bytes 52428800 | tf_op jit(solution)/shard_map/attention_2/pallas_call | solution.py:147
  661.0 43.0 %fusion.107.grad_ref = bf16[8,4,64,2048]{3,2,1,0:T(8,128)(2,1)} fusion(bf16[8,4,64,4096]{3,2,1,0:T(8,128)(2,1)} %bitcast.152, bf16[2048,4096]{1,0:T(8,128)(2,1)} %copy-done), kind=kOutput, calls=%fused_computation.84 | convolution fusion | flops 34363932672 | bytes 41943040 | tf_op jit(solution)/shard_map/tbsd,ed->tbse/dot_general | solution.py:370
  704.0 61.4 %fusion.63.qkv_ref = bf16[8,4,64,3072]{3,2,1,0:T(8,128)(2,1)} fusion(bf16[8,4,64,4096]{3,2,1,0:T(8,128)(2,1)} %bitcast.170, bf16[4096,3072]{1,0:T(8,128)(2,1)} %pick_columns.1), kind=kOutput, calls=%fused_computation.68 | convolution fusion | flops 51545899008 | bytes 54525952 | tf_op jit(solution)/shard_map/tbsd,de->tbse/dot_general | solution.py:375
  765.3 48.8 %attention_3.1 = (bf16[8,4,64,2048]{3,2,1,0:T(8,128)(2,1)}, bf16[8,4,64,2048]{3,2,1,0:T(8,128)(2,1)}, bf16[8,4,64,1024]{3,2,1,0:T(8,128)(2,1)}) custom-call(bf16[8,4,64,3072]{3,2,1,0:T(8,128)(2,1)} %fusion.63.qkv_ref, bf16[8,4,64,2048]{3,2,1,0:T(8,128)(2,1)} %fusion.107.grad_ref, f32[512,128]{1,0:T(8,128)} %get-tuple-element.99.cos_ref, ...), custom_call_target="tpu_custom_call" | custom-call | flops 25769803776 | bytes 41943040 | tf_op jit(solution)/shard_map/attention_3/pallas_call | solution.py:147
  814.1 13.1 fusion.89
  829.0 11.0 fusion.104
  840.0 13.4 fusion.101
  853.5 18.3 %fusion.16 = f32[512,4096,1,1]{1,0,3,2:T(8,128)} fusion(bf16[8,5,64,4096]{3,2,1,0:T(8,128)(2,1)} %bitcast.169, bf16[8,5,64,2048]{3,2,1,0:T(8,128)(2,1)} %get-tuple-element.63.refs_2_.refs_6_, s32[]{:T(128)S(6)} %select_n.8), kind=kOutput, calls=%fused_computation.23 | convolution fusion | flops 10737418240 | bytes 31981572 | tf_op jit(solution)/shard_map/tbse,tbsd->ed/dot_general | solution.py:384
  871.9 18.1 %fusion.18 = f32[512,4096,1,1]{1,0,3,2:T(8,128)} fusion(bf16[8,5,64,4096]{3,2,1,0:T(8,128)(2,1)} %bitcast.167, bf16[8,5,64,2048]{3,2,1,0:T(8,128)(2,1)} %get-tuple-element.58.refs_1_.refs_5_, s32[]{:T(128)S(6)} %select_n.8), kind=kOutput, calls=%fused_computation.25 | convolution fusion | flops 10737418240 | bytes 31981572 | tf_op jit(solution)/shard_map/tbse,tbsd->ed/dot_general | solution.py:384
  890.0 20.1 %bitcast_add_fusion.3 = f32[512,4096]{1,0:T(8,128)} fusion(f32[512,4096,1,1]{1,0,3,2:T(8,128)} %fusion.16, f32[512,4096]{1,0:T(8,128)} %fusion.72, f32[512,4096,1,1]{1,0,3,2:T(8,128)} %fusion.18, bf16[8,4,64,4096]{3,2,1,0:T(8,128)(2,1)} %bitcast.153, bf16[8,4,64,512]{3,2,1,0:T(8,128)(2,1)S(1)} %constant_dynamic-slice_fusion.2), kind=kOutput, calls=%fused_computation.62 | convolution fusion | flops 8596226048 | bytes 52428800 | tf_op jit(solution)/shard_map/tbse,tbsd->ed/dot_general | solution.py:384
  910.7 7.7 pick_attention.1
  918.8 7.8 pick_query.1
  926.6 4.9 pick_kv.1
  932.0 53.9 %fusion.23 = f32[4096,2048,1,1]{1,0,3,2:T(8,128)} fusion(bf16[8,5,64,4096]{3,2,1,0:T(8,128)(2,1)} %bitcast.165, bf16[8,5,64,2048]{3,2,1,0:T(8,128)(2,1)} %get-tuple-element.71.refs_2_.refs_6_), kind=kOutput, calls=%fused_computation.30 | convolution fusion | flops 42949672960 | bytes 65011712 | tf_op jit(solution)/shard_map/tbsd,tbse->de/dot_general | solution.py:392
  985.9 53.5 %fusion.27 = f32[4096,2048,1,1]{1,0,3,2:T(8,128)} fusion(bf16[8,5,64,4096]{3,2,1,0:T(8,128)(2,1)} %bitcast.162, bf16[8,5,64,2048]{3,2,1,0:T(8,128)(2,1)} %get-tuple-element.70.refs_1_.refs_5_), kind=kOutput, calls=%fused_computation.34 | convolution fusion | flops 42949672960 | bytes 65011712 | tf_op jit(solution)/shard_map/tbsd,tbse->de/dot_general | solution.py:392
  1039.4 60.5 %bitcast_add_fusion.mine_ref = f32[4096,2048]{1,0:T(8,128)} fusion(f32[4096,2048,1,1]{1,0,3,2:T(8,128)} %fusion.23, f32[4096,2048]{1,0:T(8,128)} %convolution_bitcast_fusion, f32[4096,2048,1,1]{1,0,3,2:T(8,128)} %fusion.27, bf16[8,4,64,4096]{3,2,1,0:T(8,128)(2,1)} %bitcast.172, bf16[8,4,64,2048]{3,2,1,0:T(8,128)(2,1)} %get-tuple-element.84.refs_3_.refs_7_), kind=kOutput, calls=%fused_computation.2 | convolution fusion | flops 34384904192 | bytes 159383552 | tf_op jit(solution)/shard_map/tbsd,tbse->de/dot_general | solution.py:392
  1102.3 8.9 join_gradient.1
  1111.2 63.8 %fusion.34 = (f32[4096]{0:T(1024)S(1)}, f32[16,64]{1,0:T(8,128)S(1)}, bf16[16,64,4096]{2,1,0:T(8,128)(2,1)}) fusion(bf16[16,64,4096]{2,1,0:T(8,128)(2,1)} %param.7, f32[16,64]{1,0:T(8,128)S(1)} %copy-done.5, f32[4096]{0:T(1024)S(1)} %copy-done.7, bf16[16,64,6144]{2,1,0:T(8,128)(2,1)} %bitcast.154, bf16[4096,6144]{1,0:T(8,128)(2,1)} %value_ref.1), kind=kOutput, calls=%fused_computation.42 | convolution fusion | flops 51577352192 | bytes 79732736 | tf_op jit(solution)/shard_map/bse,de->bsd/dot_general | solution.py:410
  1175.4 9.6 join_attention.1
  1185.1 42.1 %fusion.36 = bf16[16,64,4096]{2,1,0:T(8,128)(2,1)} fusion(bf16[16,64,4096]{2,1,0:T(8,128)(2,1)S(1)} %bitcast.148, bf16[16,64,4096]{2,1,0:T(8,128)(2,1)} %bitcast.159, bf16[4096,4096]{1,0:T(8,128)(2,1)} %in_ref.1), kind=kOutput, calls=%fused_computation.44 | convolution fusion | flops 34372321280 | bytes 58720256 | tf_op jit(solution)/shard_map/bse,ed->bsd/dot_general | solution.py:406
  1228.7 2.7 collective-permute-done.7
  1231.7 10.3 fusion.31
  1242.6 73.0 %join_weights.1 = f32[4096,6144]{1,0:T(8,128)} custom-call(s32[1]{0:T(128)} %bitcast.core_ref, f32[4096,2048]{1,0:T(8,128)} %bitcast_add_fusion.mine_ref, f32[4096,2048]{1,0:T(8,128)} %collective-permute-done.9.other_ref, f32[8,4096,256]{2,1,0:T(8,128)} %bitcast.151), custom_call_target="tpu_custom_call" | custom-call | flops 805306368 | bytes 201326592 | tf_op jit(solution)/shard_map/join_weights/pallas_call | solution.py:225
  1315.6 44.1 %copy.143 = f32[4096,4096]{1,0:T(8,128)} copy(f32[4096,4096]{1,0:T(8,128)} %all-gather.20.cloned.1.call-done) | data formatting | bytes 134217728
  (98 shorter events, 18.4 us)
Async XLA Ops:
  7.2 8.1 copy-start.6
  7.2 83.5 %all-gather.22.cloned.1.call-start = ((), (), s32[]{:S(2)}) async-start(), calls=%async_computation.1 | async-start | bytes 9437184 | tf_op jit(solution)/shard_map/all_gather | solution.py:358
  9.5 104.9 %all-gather.24.cloned.1.call-start = ((), (), s32[]{:S(2)}) async-start(), calls=%async_computation.2 | async-start | bytes 9437184 | tf_op jit(solution)/shard_map/all_gather | solution.py:357
  14.7 0.6 copy-start.4
  28.1 188.0 %all-gather.26.cloned.1.call-start = ((), (), s32[]{:S(2)}) async-start(), calls=%async_computation.3 | async-start | bytes 23592960 | tf_op jit(solution)/shard_map/all_gather | solution.py:358
  33.7 10.1 copy-start.8
  33.7 286.0 %all-gather.28.cloned.1.call-start = ((), (), s32[]{:S(2)}) async-start(), calls=%async_computation.4 | async-start | bytes 23592960 | tf_op jit(solution)/shard_map/all_gather | solution.py:357
  39.3 8.8 copy-start.9
  39.3 414.6 %all-gather.30.cloned.1.call-start = ((), (), s32[]{:S(2)}) async-start(), calls=%async_computation.5 | async-start | bytes 23592960 | tf_op jit(solution)/shard_map/all_gather | solution.py:358
  39.9 486.8 %all-gather.32.cloned.1.call-start = ((), (), s32[]{:S(2)}) async-start(), calls=%async_computation.6 | async-start | bytes 23592960 | tf_op jit(solution)/shard_map/all_gather | solution.py:357
  40.5 620.5 %all-gather.34.cloned.1.call-start = ((), (), s32[]{:S(2)}) async-start(), calls=%async_computation.7 | async-start | bytes 18874368 | tf_op jit(solution)/shard_map/all_gather | solution.py:358
  43.7 660.3 %all-gather.36.cloned.1.call-start = ((), (), s32[]{:S(2)}) async-start(), calls=%async_computation.8 | async-start | bytes 18874368 | tf_op jit(solution)/shard_map/all_gather | solution.py:357
  44.0 4.1 collective-permute-start
  48.0 1194.6 %all-gather.38.cloned.1.call-start = ((), (), s32[]{:S(2)}) async-start(), calls=%async_computation.9 | async-start | bytes 37748736 | tf_op jit(solution)/shard_map/all_gather | solution.py:396
  48.4 24.9 %collective-permute-start.1 = (s32[512]{0:T(512)S(1)}, s32[512]{0:T(512)S(1)}, u32[]{:S(2)}, u32[]{:S(2)}) collective-permute-start(s32[512]{0:T(512)S(1)} %add_dynamic-update-slice_fusion), channel_id=1, source_target_pairs={{0,2},{1,3},{2,0},{3,1},{4,6},{5,7},{6,4},{7,5}} | collective-permute-start | bytes 6152 | tf_op jit(solution)/shard_map/ppermute | solution.py:324
  73.3 15.4 %collective-permute-start.2 = (s32[512]{0:T(512)S(1)}, s32[512]{0:T(512)S(1)}, u32[]{:S(2)}, u32[]{:S(2)}) collective-permute-start(s32[512]{0:T(512)S(1)} %add.86), channel_id=1, source_target_pairs={{0,4},{1,5},{2,6},{3,7},{4,0},{5,1},{6,2},{7,3}} | collective-permute-start | bytes 6152 | tf_op jit(solution)/shard_map/ppermute | solution.py:324
  82.9 5.8 copy-start
  147.5 59.7 %slice-start.4 = ((s8[8388608]{0:T(1024)(128)(4,1)}), s8[4194304]{0:T(1024)(128)(4,1)S(1)}, s32[]{:S(2)}) async-start(s8[8388608]{0:T(1024)(128)(4,1)} %bitcast.156), calls=%async_computation.14 | async-start | bytes 8388608
  173.3 33.8 %slice-start.5 = ((s8[8388608]{0:T(1024)(128)(4,1)}), s8[4194304]{0:T(1024)(128)(4,1)S(1)}, s32[]{:S(2)}) async-start(s8[8388608]{0:T(1024)(128)(4,1)} %bitcast.156), calls=%async_computation.15 | async-start | bytes 8388608
  814.1 14.9 %copy-start.10 = (f32[4096,256]{1,0:T(8,128)S(1)}, f32[4096,256]{1,0:T(8,128)}, u32[]{:S(2)}) copy-start(f32[4096,256]{1,0:T(8,128)} %fusion.86) | copy-start | bytes 12582916
  853.5 462.2 %all-gather.20.cloned.1.call-start = ((), (), s32[]{:S(2)}) async-start(), calls=%async_computation | async-start | bytes 75497472 | tf_op jit(solution)/shard_map/all_gather | solution.py:397
  918.4 121.1 %collective-permute-start.3 = (bf16[16,64,2048]{2,1,0:T(8,128)(2,1)}, bf16[16,64,2048]{2,1,0:T(8,128)(2,1)}, u32[]{:S(2)}, u32[]{:S(2)}) collective-permute-start(bf16[16,64,2048]{2,1,0:T(8,128)(2,1)} %get-tuple-element.69), channel_id=1, source_target_pairs={{0,1},{1,0},{2,3},{3,2},{4,5},{5,4},{6,7},{7,6}} | collective-permute-start | bytes 12582920 | tf_op jit(solution)/shard_map/ppermute | solution.py:390
  926.5 112.9 %collective-permute-start.4 = (bf16[16,64,2048]{2,1,0:T(8,128)(2,1)}, bf16[16,64,2048]{2,1,0:T(8,128)(2,1)}, u32[]{:S(2)}, u32[]{:S(2)}) collective-permute-start(bf16[16,64,2048]{2,1,0:T(8,128)(2,1)} %get-tuple-element.73), channel_id=1, source_target_pairs={{0,1},{1,0},{2,3},{3,2},{4,5},{5,4},{6,7},{7,6}} | collective-permute-start | bytes 12582920 | tf_op jit(solution)/shard_map/ppermute | solution.py:390
  931.6 107.9 %collective-permute-start.5 = (bf16[16,64,1024]{2,1,0:T(8,128)(2,1)}, bf16[16,64,1024]{2,1,0:T(8,128)(2,1)}, u32[]{:S(2)}, u32[]{:S(2)}) collective-permute-start(bf16[16,64,1024]{2,1,0:T(8,128)(2,1)} %get-tuple-element.77), channel_id=1, source_target_pairs={{0,1},{1,0},{2,3},{3,2},{4,5},{5,4},{6,7},{7,6}} | collective-permute-start | bytes 6291464 | tf_op jit(solution)/shard_map/ppermute | solution.py:390
  1039.4 60.6 %copy-start.3 = (bf16[16,64,1024]{2,1,0:T(8,128)(2,1)S(1)}, bf16[16,64,1024]{2,1,0:T(8,128)(2,1)}, u32[]{:S(2)}) copy-start(bf16[16,64,1024]{2,1,0:T(8,128)(2,1)} %get-tuple-element.81) | copy-start | bytes 6291460
  1100.0 142.6 %collective-permute-start.9 = (f32[4096,2048]{1,0:T(8,128)}, f32[4096,2048]{1,0:T(8,128)}, u32[]{:S(2)}, u32[]{:S(2)}) collective-permute-start(f32[4096,2048]{1,0:T(8,128)} %bitcast_add_fusion.mine_ref), channel_id=1, source_target_pairs={{0,1},{1,0},{2,3},{3,2},{4,5},{5,4},{6,7},{7,6}} | collective-permute-start | bytes 100663304 | tf_op jit(solution)/shard_map/ppermute | solution.py:395
  1100.1 2.2 copy-start.2
  1102.3 8.9 copy-start.5
  1102.3 8.9 copy-start.7
  1111.2 64.3 %copy-start.1 = (bf16[16,64,2048]{2,1,0:T(8,128)(2,1)S(1)}, bf16[16,64,2048]{2,1,0:T(8,128)(2,1)}, u32[]{:S(2)}) copy-start(bf16[16,64,2048]{2,1,0:T(8,128)(2,1)} %get-tuple-element.68) | copy-start | bytes 12582916
  1175.0 10.0 slice-start
  1175.0 52.2 %collective-permute-start.6 = (f32[4096]{0:T(1024)S(1)}, f32[4096]{0:T(1024)S(1)}, u32[]{:S(2)}, u32[]{:S(2)}) collective-permute-start(f32[4096]{0:T(1024)S(1)} %get-tuple-element.89), channel_id=1, source_target_pairs={{0,1},{1,0},{2,3},{3,2},{4,5},{5,4},{6,7},{7,6}} | collective-permute-start | bytes 49160 | tf_op jit(solution)/shard_map/ppermute | solution.py:324
  1175.4 9.6 slice-start.1
  1175.4 56.3 %slice-start.2 = ((s8[8388608]{0:T(1024)(128)(4,1)}), s8[4194304]{0:T(1024)(128)(4,1)S(1)}, s32[]{:S(2)}) async-start(s8[8388608]{0:T(1024)(128)(4,1)} %bitcast.149), calls=%async_computation.12 | async-start | bytes 8388608
  1185.1 46.6 %slice-start.3 = ((s8[8388608]{0:T(1024)(128)(4,1)}), s8[4194304]{0:T(1024)(128)(4,1)S(1)}, s32[]{:S(2)}) async-start(s8[8388608]{0:T(1024)(128)(4,1)} %bitcast.149), calls=%async_computation.13 | async-start | bytes 8388608
  1227.2 4.1 collective-permute-start.7
  1231.3 10.6 collective-permute-start.8
Sparse Core Ops, SparseCore 0:
  10.4 51.1 all-gather.21
  64.0 48.3 all-gather.23
  114.2 101.8 all-gather.25
  217.8 101.8 all-gather.27
  321.3 101.8 all-gather.29
  424.9 101.8 all-gather.31
  528.6 84.0 all-gather.33
  614.5 84.0 all-gather.35
  853.6 155.2 all-gather.37
  1010.5 297.5 all-gather.19

commit v3 on v1

--- a/solution.py
+++ b/solution.py
@@ -11,7 +11,7 @@
 ROPE_BASE = 10000.0
 ROPE_SCALE = math.sqrt(1.0 + math.log(32.0) / math.log(4096.0))
 LOG2_E = math.log2(math.e)
-CHUNKS = (2, 4, 4, 6)
+CHUNKS = (2, 4, 5, 5)
 
 
 def rope_tables(positions, long_factor):
@@ -24,7 +24,7 @@
     return jnp.concatenate([cos_half, cos_half], axis=-1), jnp.concatenate([-sin_half, sin_half], axis=-1)
 
 
-def attention_kernel(qkv_ref, grad_ref, cos_ref, sin_ref, out_ref, dqkv_ref, query_s, dkey_s, dvalue_s):
+def attention_kernel(qkv_ref, grad_ref, cos_ref, sin_ref, out_ref, dqkv_ref, dkey_s, dvalue_s):
     devs, _, sub, width = qkv_ref.shape
     dim = cos_ref.shape[1]
     seq = devs * sub
@@ -32,7 +32,6 @@
     block = 128
     per = block // sub
     scale = dim ** -0.5
-    cols = group * block
 
     def rope(vals, cos, sin):
         wide = vals.astype(jnp.float32)
@@ -53,49 +52,80 @@
     key = rope(key_raw, cos_ref[...], sin_ref[...])
     key_t = key.T
     value_t = value.T
+    heads_unit = 2
+    cols = heads_unit * block
     row_ids = lax.broadcasted_iota(jnp.int32, (block, cols), 0)
     col_ids = lax.broadcasted_iota(jnp.int32, (block, cols), 1)
     allowed = row_ids <= lax.rem(col_ids, block)
-
-    for step in reversed(range(seq // block)):
+    units = [(step, first) for step in reversed(range(seq // block)) for first in range(0, group, heads_unit)]
+    state = {}
+
+    def load(unit):
+        step, first = units[unit]
         rows = pl.ds(step * block, block)
         cos = cos_ref[rows, :]
         sin = sin_ref[rows, :]
         span = (step + 1) * block
+        queries = []
         grads = []
-        for head in range(group):
+        for head in range(first, first + heads_unit):
             lanes = pl.ds(head * dim, dim)
             raw = qkv_ref[step * per:(step + 1) * per, 0, :, lanes].reshape(block, dim)
-            query_s[head * block:(head + 1) * block, :] = rope(raw, cos, sin)
+            queries.append(rope(raw, cos, sin))
             grads.append(grad_ref[step * per:(step + 1) * per, 0, :, lanes].reshape(block, dim))
-        query = query_s[...]
+        query = jnp.concatenate(queries, axis=0)
         grad = jnp.concatenate(grads, axis=0)
         scores = nt(key[:span], query)
+        grad_probs = nt(value[:span], grad).astype(jnp.bfloat16)
+        state[unit] = (query, grad, scores, grad_probs)
+
+    def soften(unit):
+        step, first = units[unit]
+        span = (step + 1) * block
+        query, grad, scores, grad_probs = state[unit]
         last = jnp.where(allowed, scores[span - block:], -jnp.inf)
         scores = last if step == 0 else jnp.concatenate([scores[:span - block], last], axis=0)
         peak = jnp.max(scores, axis=0, keepdims=True)
         weights = jnp.exp2((scores - peak) * (scale * LOG2_E))
         probs = weights * (1.0 / jnp.sum(weights, axis=0, keepdims=True))
-        probs_low = probs.astype(jnp.bfloat16)
-        attn = nn(value_t[:, :span], probs_low).astype(jnp.bfloat16).T
-        grad_probs = nt(value[:span], grad).astype(jnp.bfloat16).astype(jnp.float32)
+        grad_probs = grad_probs.astype(jnp.float32)
         row_dot = jnp.sum(grad_probs * probs, axis=0, keepdims=True)
         grad_scores = (probs * (grad_probs - row_dot)).astype(jnp.bfloat16)
+        state[unit] = (query, grad, probs.astype(jnp.bfloat16), grad_scores)
+
+    def finish(unit):
+        step, first = units[unit]
+        rows = pl.ds(step * block, block)
+        cos = cos_ref[rows, :]
+        sin = sin_ref[rows, :]
+        span = (step + 1) * block
+        query, grad, probs_low, grad_scores = state.pop(unit)
+        attn = nn(value_t[:, :span], probs_low).astype(jnp.bfloat16).T
         grad_query = (nn(key_t[:, :span], grad_scores) * scale).astype(jnp.bfloat16).T
         part_value = nn(probs_low, grad)
         part_key = nn(grad_scores, query)
-        if span == seq:
+        if unit == 0:
             dvalue_s[...] = part_value
             dkey_s[...] = part_key
         else:
             dvalue_s[:span, :] += part_value
             dkey_s[:span, :] += part_key
-        for head in range(group):
-            lanes = pl.ds(head * dim, dim)
+        for head in range(heads_unit):
+            lanes = pl.ds((first + head) * dim, dim)
             part = slice(head * block, (head + 1) * block)
             out_ref[step * per:(step + 1) * per, 0, :, lanes] = attn[part].reshape(per, sub, dim)
             back = rope_back(grad_query[part], cos, sin)
             dqkv_ref[step * per:(step + 1) * per, 0, :, lanes] = back.reshape(per, sub, dim)
+
+    count = len(units)
+    load(0)
+    for unit in range(count + 1):
+        if unit < count:
+            soften(unit)
+        if unit + 1 < count:
+            load(unit + 1)
+        if unit > 0:
+            finish(unit - 1)
 
     grad_key = (dkey_s[...] * scale).astype(jnp.bfloat16)
     back = rope_back(grad_key, cos_ref[...], sin_ref[...])
@@ -120,9 +150,9 @@
         grid=(count, heads),
         in_specs=[head_spec(per_head), head_spec(group * dim), table_spec, table_spec],
         out_specs=[head_spec(group * dim), head_spec(per_head)],
-        out_shape=[jax.ShapeDtypeStruct(grad.shape, jnp.bfloat16), jax.ShapeDtypeStruct(qkv.shape, jnp.bfloat16)],
-        scratch_shapes=[pltpu.VMEM((group * 128, dim), jnp.bfloat16),
-                        pltpu.VMEM((seq, dim), jnp.float32), pltpu.VMEM((seq, dim), jnp.float32)],
+        out_shape=[jax.ShapeDtypeStruct((devs, count, sub, heads * cols), jnp.bfloat16)
+                   for cols in (group * dim, per_head)],
+        scratch_shapes=[pltpu.VMEM((seq, dim), jnp.float32), pltpu.VMEM((seq, dim), jnp.float32)],
         compiler_params=pltpu.CompilerParams(vmem_limit_bytes=56 * 1024 * 1024),
         cost_estimate=pl.CostEstimate(flops=count * heads * group * 6 * 2 * seq * seq * dim,
                                       bytes_accessed=4 * (qkv.size + grad.size),
@@ -130,8 +160,7 @@
     )(qkv, grad, cos, sin)
 
 
-def join_kernel(parts, heads, core_ref, mine_ref, other_ref, out_ref):
-    first = core_ref[0] == 0
+def join_heads(first, mine_ref, other_ref, out_ref, parts, heads):
     width = sum(parts)
     start = 0
     base = 0
@@ -147,6 +176,10 @@
         base += 2 * heads * cols
 
 
+def join_kernel(parts, heads, core_ref, mine_ref, other_ref, out_ref):
+    join_heads(core_ref[0] == 0, mine_ref, other_ref, out_ref, parts, heads)
+
+
 def join_columns(core, mine, other, parts, heads, name):
     rows, half = mine.shape
     tile = 128
@@ -162,6 +195,37 @@
         cost_estimate=pl.CostEstimate(flops=rows * half * 64, bytes_accessed=4 * rows * half * mine.dtype.itemsize,
                                       transcendentals=0),
     )(core, mine, other)
+
+
+def project_join_kernel(parts, heads, core_ref, grad_ref, weight_ref, mine_ref, other_ref, out_ref, joined_ref):
+    join_heads(core_ref[0] == 0, mine_ref, other_ref, joined_ref, parts, heads)
+    out_ref[...] = lax.dot_general(grad_ref[...], weight_ref[...], (((1,), (1,)), ((), ())),
+                                   preferred_element_type=jnp.float32).astype(jnp.bfloat16)
+
+
+def project_and_join(core, grad, weight, mine, other, parts, heads):
+    rows, depth = grad.shape
+    model = weight.shape[0]
+    half = mine.shape[1]
+    tile = 256
+
+    def row_spec(cols):
+        return pl.BlockSpec((tile, cols), lambda t, core_ref: (t, 0))
+
+    return pl.pallas_call(
+        functools.partial(project_join_kernel, parts, heads),
+        name='project_and_join',
+        grid_spec=pltpu.PrefetchScalarGridSpec(
+            num_scalar_prefetch=1, grid=(model // tile,),
+            in_specs=[pl.BlockSpec((rows, depth), lambda t, core_ref: (0, 0), pipeline_mode=pl.Buffered(1)),
+                      row_spec(depth), row_spec(half), row_spec(half)],
+            out_specs=[pl.BlockSpec((rows, tile), lambda t, core_ref: (0, t)), row_spec(2 * half)]),
+        out_shape=[jax.ShapeDtypeStruct((rows, model), jnp.bfloat16),
+                   jax.ShapeDtypeStruct((model, 2 * half), jnp.float32)],
+        compiler_params=pltpu.CompilerParams(vmem_limit_bytes=62 * 1024 * 1024),
+        cost_estimate=pl.CostEstimate(flops=2 * rows * depth * model,
+                                      bytes_accessed=2 * depth * (rows + model) + 16 * model * half, transcendentals=0),
+    )(core, grad, weight, mine, other)
 
 
 def pick_columns_kernel(core_ref, query_ref, key_ref, value_ref, out_ref):
@@ -244,6 +308,14 @@
         cost_estimate=pl.CostEstimate(flops=batch * sub * width * 64, bytes_accessed=8 * batch * sub * width,
                                       transcendentals=0),
     )(devs, *chunks, *chunks)
+
+
+def exchange_sum(part, devs):
+    bit = 1
+    while bit < devs:
+        part = part + lax.ppermute(part, 'sp', [(d, d ^ bit) for d in range(devs)])
+        bit *= 2
+    return part
 
 
 def block_body(hidden, positions, long_factor, norm_weight, w_qkv, w_out, grad_out):
@@ -268,7 +340,8 @@
     core_ref = core.reshape(1)
     w_own = pick_columns(core_ref, w_qkv, mine_heads, group, dim)
     wo_own = pick_rows(core_ref, w_out, mine_heads, group * dim)
-    cos, sin = rope_tables(lax.all_gather(positions, 'sp', axis=0, tiled=True), long_factor)
+    spread = lax.dynamic_update_slice(jnp.zeros((devs * sub,), positions.dtype), positions, (me * sub,))
+    cos, sin = rope_tables(exchange_sum(spread, devs), long_factor)
 
     gathered = []
     start = 0
@@ -277,50 +350,72 @@
                          lax.all_gather(grad_out[start:start + count], 'sp', axis=0)))
         start += count
 
+    def project(normed_all):
+        return jnp.einsum('tbsd,de->tbse', normed_all, w_own, preferred_element_type=jnp.float32).astype(jnp.bfloat16)
+
+    def project_back(grad_all):
+        return jnp.einsum('tbsd,ed->tbse', grad_all, wo_own, preferred_element_type=jnp.float32).astype(jnp.bfloat16)
+
+    def after(value, *earlier):
+        *earlier, value = lax.optimization_barrier((*earlier, value))
+        return (value, *earlier)
+
     grad_wqkv = None
     grad_wout = None
     tokens = []
+    last = len(CHUNKS) - 1
     for index, (normed_all, grad_all) in enumerate(gathered):
-        qkv = jnp.einsum('tbsd,de->tbse', normed_all, w_own, preferred_element_type=jnp.float32).astype(jnp.bfloat16)
-        grad_attn = jnp.einsum('tbsd,ed->tbse', grad_all, wo_own, preferred_element_type=jnp.float32).astype(jnp.bfloat16)
+        if index == 0:
+            grad_attn = project_back(grad_all)
+            normed_all, grad_attn = after(normed_all, grad_attn)
+            qkv = project(normed_all)
+        else:
+            attn, grad_qkv = tokens[-1]
+            if index == 1:
+                normed_all, attn, grad_wqkv = after(normed_all, attn, grad_wqkv)
+            else:
+                normed_all, attn = after(normed_all, attn)
+            tokens[-1] = (attn, grad_qkv)
+            qkv = project(normed_all)
+            grad_all, qkv, grad_wout = after(grad_all, qkv, grad_wout)
+            grad_attn = project_back(grad_all)
         attn, grad_qkv = attention(qkv, grad_attn, cos, sin, mine_heads, f'attention_{index}')
+        tokens.append((attn, grad_qkv))
         attn_slice = lax.dynamic_slice_in_dim(attn, chip * group * dim, group * dim, axis=3)
         part_out = jnp.einsum('tbse,tbsd->ed', attn_slice, grad_all, preferred_element_type=jnp.float32)
+        grad_wout = part_out if grad_wout is None else grad_wout + part_out
+        if index == last:
+            ends = jnp.stack([me, partner])
+            picked = [pick_tokens(ends, list(arrays), name) for arrays, name in
+                      zip(zip(*tokens), ('pick_attention', 'pick_gradient'))]
+            others = [lax.ppermute(pair[1], 'sp', pairs) for pair in picked]
+            grad_qkv, *others = after(grad_qkv, *others)
         part_qkv = jnp.einsum('tbsd,tbse->de', normed_all, grad_qkv, preferred_element_type=jnp.float32)
-        grad_wout = part_out if grad_wout is None else grad_wout + part_out
         grad_wqkv = part_qkv if grad_wqkv is None else grad_wqkv + part_qkv
-        tokens.append((attn, grad_qkv))
-
+
+    grad_wqkv_other = lax.ppermute(grad_wqkv, 'sp', pairs)
     grad_wout = lax.all_gather(grad_wout, 'sp', axis=0, tiled=True)
-    grad_wqkv_other = lax.ppermute(grad_wqkv, 'sp', pairs)
-
-    ends = jnp.stack([me, partner])
-    attn_mine, attn_send = pick_tokens(ends, [pair[0] for pair in tokens], 'pick_attention')
-    dqkv_mine, dqkv_send = pick_tokens(ends, [pair[1] for pair in tokens], 'pick_gradient')
-    attn_other = lax.ppermute(attn_send, 'sp', pairs)
-    dqkv_other = lax.ppermute(dqkv_send, 'sp', pairs)
-
-    def natural(mine, other, parts, name):
+    parts = (group * dim, dim, dim)
+
+    def natural(index, parts, name):
         rows = (batch * sub, -1)
-        joined = join_columns(core_ref, mine.reshape(rows), other.reshape(rows), parts, mine_heads, name)
-        return joined.reshape(batch, sub, -1)
-
-    parts = (group * dim, dim, dim)
-    attn_flat = natural(attn_mine, attn_other, parts[:1], 'join_attention')
+        return join_columns(core_ref, picked[index][0].reshape(rows), others[index].reshape(rows), parts, mine_heads, name)
+
+    attn_flat = natural(0, parts[:1], 'join_attention').reshape(batch, sub, -1)
     mixed_out = jnp.einsum('bse,ed->bsd', attn_flat, w_out, preferred_element_type=jnp.float32)
     out_hidden = (hidden_wide + mixed_out).astype(jnp.bfloat16)
 
-    grad_qkv = natural(dqkv_mine, dqkv_other, parts, 'join_gradient')
-    grad_normed = jnp.einsum('bse,de->bsd', grad_qkv, w_qkv, preferred_element_type=jnp.float32)
-    grad_normed = grad_normed.astype(jnp.bfloat16).astype(jnp.float32)
+    grad_qkv = natural(1, parts, 'join_gradient')
+    grad_qkv, out_hidden = after(grad_qkv, out_hidden)
+    grad_normed, grad_wqkv = project_and_join(core_ref, grad_qkv, w_qkv, grad_wqkv, grad_wqkv_other, parts, mine_heads)
+    grad_normed = grad_normed.reshape(batch, sub, model).astype(jnp.float32)
     unit_hidden = hidden_wide * inv_rms
     grad_norm = jnp.sum(grad_normed * unit_hidden, axis=(0, 1))
     grad_unit = grad_normed * norm_weight
     grad_inner = inv_rms * (grad_unit - unit_hidden * jnp.mean(grad_unit * unit_hidden, axis=-1, keepdims=True))
     grad_hidden = (grad_out.astype(jnp.float32) + grad_inner).astype(jnp.bfloat16)
 
-    grad_wqkv = join_columns(core_ref, grad_wqkv, grad_wqkv_other, parts, mine_heads, 'join_weights')
-    return out_hidden, grad_hidden, lax.psum(grad_norm, 'sp'), grad_wqkv, grad_wout
+    return out_hidden, grad_hidden, exchange_sum(grad_norm, devs), grad_wqkv, grad_wout
 
 
 def solution(mesh):

time: 1590 us -> 1360 us (0.86)
  matrix products: 872 us -> 786 us
  waiting for transfers between devices: 125 us -> 53.9 us
  blocking collectives: 48.1 us -> 0 us
  Pallas kernels: 415 us -> 369 us
    pallas_call x0 -> x1, Pallas kernels: none -> 108 us  [project_and_join(): pl.pallas_call(functools.partial(project_join_kernel, parts, heads), name...]
    pallas_call x4, Pallas kernels: 277 us -> 194 us  [attention(): pl.pallas_call(attention_kernel, name=name, grid=(count, heads), in_specs...]
    pallas_call x3 -> x2, Pallas kernels: 90 us -> 18.2 us  [join_columns(): pl.pallas_call(functools.partial(join_kernel, parts, heads), name=name, g...]
    dot_general x9 -> x8, matrix products: 479 us -> 416 us  [the longest x4 243 us: project(): jnp.einsum('tbsd,de->tbse', normed_all, w_own, preferred_element_type=jnp...]
    ppermute x2 -> x8, waiting for transfers between devices: 64.1 us -> 3.31 us  [the longest x6 3.31 us: exchange_sum(): part = part + lax.ppermute(part, 'sp', [(d, d ^ bit) for d in range(devs)])]
    all_gather x4, waiting for transfers between devices: 59.3 us -> 0.01 us  [block_body(): lax.all_gather(normed[start:start + count], 'sp', axis=0)]
    all_gather x4, waiting for transfers between devices: 0.01 us -> 28.8 us  [block_body(): lax.all_gather(grad_out[start:start + count], 'sp', axis=0)]
    unnamed x1 -> x0, blocking collectives: 25.7 us -> none
  transfers between devices with their start and end apart: 12 -> 18, of which waited for: 4 -> 7; matrix products, arithmetic and copies ran while one was open for 50% -> 58% of each run, Pallas kernels for 20% -> 23%
where the time goes in v3:
time: 1360 us; the launch traced here: 1350 us
  matrix products  786 us (58%)
  Pallas kernels  369 us (27%)
  local copies, waits for them, and re-layouts  74.9 us (6%)
  waiting for transfers between devices  53.9 us (4%)
  other arithmetic  42.3 us (3%)
  between operations  14.5 us (1%)
    dot_general x4, matrix products, block_body(): jnp.einsum('tbsd,tbse->de', normed_all, grad_qkv, preferred_element_type=...  263 us
    dot_general x4, matrix products, project(): jnp.einsum('tbsd,de->tbse', normed_all, w_own, preferred_element_type=jnp...  243 us
    pallas_call x4, Pallas kernels, attention(): pl.pallas_call(attention_kernel, name=name, grid=(count, heads), in_specs...  194 us
    dot_general x4, matrix products, project_back(): jnp.einsum('tbsd,ed->tbse', grad_all, wo_own, preferred_element_type=jnp....  172 us
    pallas_call x1, Pallas kernels, project_and_join(): pl.pallas_call(functools.partial(project_join_kernel, parts, heads), name...  108 us
    dot_general x4, matrix products, block_body(): jnp.einsum('tbse,tbsd->ed', attn_slice, grad_all, preferred_element_type=...  66.1 us
    unnamed x35, local copies, waits for them, and re-layouts  52.8 us
    dot_general x1, matrix products, block_body(): jnp.einsum('bse,ed->bsd', attn_flat, w_out, preferred_element_type=jnp.fl...  41.8 us
  transfers between devices with their start and end apart: 18, of which 7 were waited for; matrix products, arithmetic and copies ran while one was open for 58% of the time, Pallas kernels for 23%

profile of v3, /device:TPU:0, one launch (start us, length us, event | category | flops | bytes accessed | tf_op | source)
XLA Modules:
  0.0 1349.4 jit_solution(2032855404396927377)
XLA Ops:
  7.2 2.3 slice.24
  9.6 5.1 fusion.28
  15.3 10.2 fusion.25
  25.4 2.3 slice.32
  27.8 3.2 slice.33
  31.0 3.1 slice.27
  34.2 5.5 fusion.91
  39.7 5.5 fusion.90
  48.4 2.9 collective-permute-start.1
  51.2 22.4 %pick_columns.1 = bf16[4096,3072]{1,0:T(8,128)(2,1)} custom-call(s32[1]{0:T(128)} %bitcast.core_ref, bf16[4096,6144]{1,0:T(8,128)(2,1)} %weight_ref.1, bf16[4096,6144]{1,0:T(8,128)(2,1)} %weight_ref.1, bf16[4096,6144]{1,0:T(8,128)(2,1)} %weight_ref.1), custom_call_target="tpu_custom_call" | custom-call | flops 402653184 | bytes 50331648 | tf_op jit(solution)/shard_map/pick_columns/pallas_call | solution.py:244
  73.6 1.5 collective-permute-start.2
  75.2 8.0 pick_rows.1
  83.2 5.7 copy-done
  91.0 23.7 %convert_bitcast_fusion.grad_ref = bf16[8,2,64,2048]{3,2,1,0:T(8,128)(2,1)} fusion(bf16[8,2,64,4096]{3,2,1,0:T(8,128)(2,1)} %bitcast.121, bf16[2048,4096]{1,0:T(8,128)(2,1)} %copy-done), kind=kOutput, calls=%fused_computation.68 | convolution fusion | flops 17181966336 | bytes 29360128 | tf_op jit(solution)/shard_map/tbsd,ed->tbse/dot_general | solution.py:357
  114.7 33.0 %fusion.75.qkv_ref = bf16[8,2,64,3072]{3,2,1,0:T(8,128)(2,1)} fusion(bf16[8,2,64,4096]{3,2,1,0:T(8,128)(2,1)} %bitcast.138, bf16[4096,3072]{1,0:T(8,128)(2,1)} %pick_columns.1), kind=kOutput, calls=%fused_computation.66 | convolution fusion | flops 25772949504 | bytes 39845888 | tf_op jit(solution)/shard_map/tbsd,de->tbse/dot_general | solution.py:354
  147.7 26.1 %attention_0.1 = (bf16[8,2,64,2048]{3,2,1,0:T(8,128)(2,1)}, bf16[8,2,64,3072]{3,2,1,0:T(8,128)(2,1)}) custom-call(bf16[8,2,64,3072]{3,2,1,0:T(8,128)(2,1)} %fusion.75.qkv_ref, bf16[8,2,64,2048]{3,2,1,0:T(8,128)(2,1)} %convert_bitcast_fusion.grad_ref, f32[512,128]{1,0:T(8,128)} %get-tuple-element.88.cos_ref, f32[512,128]{1,0:T(8,128)} %get-tuple-element.89.sin_ref), custom_call_target="tpu_custom_call" | custom-call | flops 12884901888 | bytes 20971520 | tf_op jit(solution)/shard_map/attention_0/pallas_call | solution.py:147
  173.8 35.4 %convolution_bitcast_fusion = f32[4096,3072]{1,0:T(8,128)} fusion(bf16[8,2,64,4096]{3,2,1,0:T(8,128)(2,1)} %bitcast.139, bf16[8,2,64,3072]{3,2,1,0:T(8,128)(2,1)} %get-tuple-element.45.refs_0_.refs_4_), kind=kOutput, calls=%fused_computation.5 | convolution fusion | flops 25769803776 | bytes 65011712 | tf_op jit(solution)/shard_map/tbsd,tbse->de/dot_general | solution.py:393
  209.2 8.1 fusion.59
  217.3 61.3 %fusion.56.qkv_ref = bf16[8,4,64,3072]{3,2,1,0:T(8,128)(2,1)} fusion(bf16[8,4,64,4096]{3,2,1,0:T(8,128)(2,1)} %bitcast.134, bf16[4096,3072]{1,0:T(8,128)(2,1)} %pick_columns.1), kind=kOutput, calls=%fused_computation.61 | convolution fusion | flops 51545899008 | bytes 54525952 | tf_op jit(solution)/shard_map/tbsd,de->tbse/dot_general | solution.py:354
  278.6 5.5 all-gather.26.cloned.1.call-done
  284.1 42.8 %fusion.78.grad_ref = bf16[8,4,64,2048]{3,2,1,0:T(8,128)(2,1)} fusion(bf16[8,4,64,4096]{3,2,1,0:T(8,128)(2,1)} %bitcast.136, bf16[2048,4096]{1,0:T(8,128)(2,1)} %copy-done), kind=kOutput, calls=%fused_computation.67 | convolution fusion | flops 34363932672 | bytes 41943040 | tf_op jit(solution)/shard_map/tbsd,ed->tbse/dot_general | solution.py:357
  326.9 48.3 %attention_1.1 = (bf16[8,4,64,2048]{3,2,1,0:T(8,128)(2,1)}, bf16[8,4,64,3072]{3,2,1,0:T(8,128)(2,1)}) custom-call(bf16[8,4,64,3072]{3,2,1,0:T(8,128)(2,1)} %fusion.56.qkv_ref, bf16[8,4,64,2048]{3,2,1,0:T(8,128)(2,1)} %fusion.78.grad_ref, f32[512,128]{1,0:T(8,128)} %get-tuple-element.88.cos_ref, f32[512,128]{1,0:T(8,128)} %get-tuple-element.89.sin_ref), custom_call_target="tpu_custom_call" | custom-call | flops 25769803776 | bytes 41943040 | tf_op jit(solution)/shard_map/attention_1/pallas_call | solution.py:147
  375.2 19.0 %bitcast_add_fusion.5 = f32[512,4096]{1,0:T(8,128)} fusion(f32[512,4096]{1,0:T(8,128)} %fusion.59, bf16[8,4,64,4096]{3,2,1,0:T(8,128)(2,1)} %bitcast.137, bf16[8,4,64,2048]{3,2,1,0:T(8,128)(2,1)} %get-tuple-element.51.refs_1_.refs_5_, s32[]{:T(128)S(6)} %select_n.10), kind=kOutput, calls=%fused_computation.57 | convolution fusion | flops 8592031744 | bytes 35651588 | tf_op jit(solution)/shard_map/tbse,tbsd->ed/dot_general | solution.py:385
  394.2 74.4 %fusion.45.qkv_ref = bf16[8,5,64,3072]{3,2,1,0:T(8,128)(2,1)} fusion(bf16[8,5,64,4096]{3,2,1,0:T(8,128)(2,1)} %bitcast.126, bf16[4096,3072]{1,0:T(8,128)(2,1)} %pick_columns.1), kind=kOutput, calls=%fused_computation.53 | convolution fusion | flops 64432373760 | bytes 61865984 | tf_op jit(solution)/shard_map/tbsd,de->tbse/dot_general | solution.py:354
  468.6 22.6 %all-gather.30.cloned.1.call-done = bf16[40,64,4096]{2,1,0:T(8,128)(2,1)} async-done(((bf16[5,64,4096]{2,1,0:T(8,128)(2,1)}), bf16[40,64,4096]{2,1,0:T(8,128)(2,1)}) %all-gather.30.cloned.1.call-update) | async-done | bytes 20971536 | tf_op jit(solution)/shard_map/all_gather | solution.py:350
  491.2 52.8 %fusion.69.grad_ref = bf16[8,5,64,2048]{3,2,1,0:T(8,128)(2,1)} fusion(bf16[8,5,64,4096]{3,2,1,0:T(8,128)(2,1)} %bitcast.130, bf16[2048,4096]{1,0:T(8,128)(2,1)} %copy-done), kind=kOutput, calls=%fused_computation.64 | convolution fusion | flops 42954915840 | bytes 48234496 | tf_op jit(solution)/shard_map/tbsd,ed->tbse/dot_general | solution.py:357
  544.0 59.8 %attention_2.1 = (bf16[8,5,64,2048]{3,2,1,0:T(8,128)(2,1)}, bf16[8,5,64,3072]{3,2,1,0:T(8,128)(2,1)}) custom-call(bf16[8,5,64,3072]{3,2,1,0:T(8,128)(2,1)} %fusion.45.qkv_ref, bf16[8,5,64,2048]{3,2,1,0:T(8,128)(2,1)} %fusion.69.grad_ref, f32[512,128]{1,0:T(8,128)} %get-tuple-element.88.cos_ref, f32[512,128]{1,0:T(8,128)} %get-tuple-element.89.sin_ref), custom_call_target="tpu_custom_call" | custom-call | flops 32212254720 | bytes 52428800 | tf_op jit(solution)/shard_map/attention_2/pallas_call | solution.py:147
  603.8 19.6 %bitcast_add_fusion.4 = f32[512,4096]{1,0:T(8,128)} fusion(f32[512,4096]{1,0:T(8,128)} %bitcast_add_fusion.5, bf16[8,5,64,4096]{3,2,1,0:T(8,128)(2,1)} %bitcast.131, bf16[8,5,64,2048]{3,2,1,0:T(8,128)(2,1)} %get-tuple-element.57.refs_2_.refs_6_, s32[]{:T(128)S(6)} %select_n.10), kind=kOutput, calls=%fused_computation.56 | convolution fusion | flops 10739515392 | bytes 40370180 | tf_op jit(solution)/shard_map/tbse,tbsd->ed/dot_general | solution.py:385
  623.4 74.5 %fusion.48.qkv_ref = bf16[8,5,64,3072]{3,2,1,0:T(8,128)(2,1)} fusion(bf16[8,5,64,4096]{3,2,1,0:T(8,128)(2,1)} %bitcast.128, bf16[4096,3072]{1,0:T(8,128)(2,1)} %pick_columns.1), kind=kOutput, calls=%fused_computation.54 | convolution fusion | flops 64432373760 | bytes 61865984 | tf_op jit(solution)/shard_map/tbsd,de->tbse/dot_general | solution.py:354
  698.6 53.1 %fusion.72.grad_ref = bf16[8,5,64,2048]{3,2,1,0:T(8,128)(2,1)} fusion(bf16[8,5,64,4096]{3,2,1,0:T(8,128)(2,1)} %bitcast.132, bf16[2048,4096]{1,0:T(8,128)(2,1)} %copy-done), kind=kOutput, calls=%fused_computation.65 | convolution fusion | flops 42954915840 | bytes 48234496 | tf_op jit(solution)/shard_map/tbsd,ed->tbse/dot_general | solution.py:357
  751.7 59.7 %attention_3.1 = (bf16[8,5,64,2048]{3,2,1,0:T(8,128)(2,1)}, bf16[8,5,64,3072]{3,2,1,0:T(8,128)(2,1)}) custom-call(bf16[8,5,64,3072]{3,2,1,0:T(8,128)(2,1)} %fusion.48.qkv_ref, bf16[8,5,64,2048]{3,2,1,0:T(8,128)(2,1)} %fusion.72.grad_ref, f32[512,128]{1,0:T(8,128)} %get-tuple-element.88.cos_ref, f32[512,128]{1,0:T(8,128)} %get-tuple-element.89.sin_ref), custom_call_target="tpu_custom_call" | custom-call | flops 32212254720 | bytes 52428800 | tf_op jit(solution)/shard_map/attention_3/pallas_call | solution.py:147
  811.4 19.3 %bitcast_add_fusion.3 = f32[512,4096]{1,0:T(8,128)} fusion(f32[512,4096]{1,0:T(8,128)} %bitcast_add_fusion.4, bf16[8,5,64,4096]{3,2,1,0:T(8,128)(2,1)} %bitcast.133, bf16[8,5,64,2048]{3,2,1,0:T(8,128)(2,1)} %get-tuple-element.62.refs_3_.refs_7_, s32[]{:T(128)S(6)} %select_n.10), kind=kOutput, calls=%fused_computation.55 | convolution fusion | flops 10739515392 | bytes 40370180 | tf_op jit(solution)/shard_map/tbse,tbsd->ed/dot_general | solution.py:385
  830.8 62.3 %fusion.38 = f32[4096,3072,1,1]{1,0,3,2:T(8,128)} fusion(bf16[8,4,64,4096]{3,2,1,0:T(8,128)(2,1)} %bitcast.135, bf16[8,4,64,3072]{3,2,1,0:T(8,128)(2,1)} %get-tuple-element.65.refs_1_.refs_5_), kind=kOutput, calls=%fused_computation.46 | convolution fusion | flops 51539607552 | bytes 79691776 | tf_op jit(solution)/shard_map/tbsd,tbse->de/dot_general | solution.py:393
  893.1 7.6 pick_attention.1
  900.9 10.5 pick_gradient.1
  911.7 75.0 %fusion.17 = f32[4096,3072,1,1]{1,0,3,2:T(8,128)} fusion(bf16[8,5,64,4096]{3,2,1,0:T(8,128)(2,1)} %bitcast.127, bf16[8,5,64,3072]{3,2,1,0:T(8,128)(2,1)} %get-tuple-element.66.refs_2_.refs_6_), kind=kOutput, calls=%fused_computation.25 | convolution fusion | flops 64424509440 | bytes 87031808 | tf_op jit(solution)/shard_map/tbsd,tbse->de/dot_general | solution.py:393
  986.7 90.2 %bitcast_add_fusion.mine_ref = f32[4096,3072]{1,0:T(8,128)} fusion(f32[4096,3072,1,1]{1,0,3,2:T(8,128)} %fusion.17, f32[4096,3072]{1,0:T(8,128)} %convolution_bitcast_fusion, f32[4096,3072,1,1]{1,0,3,2:T(8,128)} %fusion.38, bf16[8,5,64,4096]{3,2,1,0:T(8,128)(2,1)} %bitcast.129, bf16[8,5,64,3072]{3,2,1,0:T(8,128)(2,1)} %get-tuple-element.75.refs_3_.refs_7_), kind=kOutput, calls=%fused_computation | convolution fusion | flops 64462258176 | bytes 238026752 | tf_op jit(solution)/shard_map/tbsd,tbse->de/dot_general | solution.py:393
  1077.1 2.3 copy-done.1
  1079.4 7.5 join_attention.1
  1086.9 10.7 join_gradient.1.grad_ref
  1097.7 41.8 %fusion.29 = bf16[16,64,4096]{2,1,0:T(8,128)(2,1)} fusion(bf16[16,64,4096]{2,1,0:T(8,128)(2,1)S(1)} %bitcast.115, bf16[16,64,4096]{2,1,0:T(8,128)(2,1)} %bitcast.125, bf16[4096,4096]{1,0:T(8,128)(2,1)} %in_ref.1), kind=kOutput, calls=%fused_computation.37 | convolution fusion | flops 34372321280 | bytes 58720256 | tf_op jit(solution)/shard_map/bse,ed->bsd/dot_general | solution.py:405
  1139.4 20.9 %collective-permute-done.5.other_ref = f32[4096,3072]{1,0:T(8,128)} collective-permute-done((f32[4096,3072]{1,0:T(8,128)}, f32[4096,3072]{1,0:T(8,128)}, u32[]{:S(2)}, u32[]{:S(2)}) %collective-permute-start.5) | collective-permute-done | bytes 50331680 | tf_op jit(solution)/shard_map/ppermute | solution.py:396
  1160.4 108.2 %project_and_join.1 = (bf16[1024,4096]{1,0:T(8,128)(2,1)}, f32[4096,6144]{1,0:T(8,128)}) custom-call(s32[1]{0:T(128)} %bitcast.core_ref, bf16[1024,6144]{1,0:T(8,128)(2,1)} %join_gradient.1.grad_ref, bf16[4096,6144]{1,0:T(8,128)(2,1)} %weight_ref.1, f32[4096,3072]{1,0:T(8,128)} %bitcast_add_fusion.mine_ref, f32[4096,3072]{1,0:T(8,128)} %collective-permute-done.5.other_ref), custom_call_target="tpu_custom_call" | custom-call | flops 51539607552 | bytes 264241152 | tf_op jit(solution)/shard_map/project_and_join/pallas_call | solution.py:215
  1268.7 13.0 fusion.27
  1282.9 1.5 collective-permute-start.7
  1284.3 2.3 collective-permute-done.7
  1287.2 10.5 fusion.24
  1298.3 44.1 %copy.97 = f32[4096,4096]{1,0:T(8,128)} copy(f32[4096,4096]{1,0:T(8,128)} %all-gather.18.cloned.1.call-done) | data formatting | bytes 134217728
  (89 shorter events, 10.0 us)
Async XLA Ops:
  7.2 83.8 %all-gather.20.cloned.1.call-start = ((), (), s32[]{:S(2)}) async-start(), calls=%async_computation.1 | async-start | bytes 9437184 | tf_op jit(solution)/shard_map/all_gather | solution.py:350
  9.5 105.2 %all-gather.22.cloned.1.call-start = ((), (), s32[]{:S(2)}) async-start(), calls=%async_computation.2 | async-start | bytes 9437184 | tf_op jit(solution)/shard_map/all_gather | solution.py:349
  14.7 0.6 copy-start.3
  27.7 189.5 %all-gather.24.cloned.1.call-start = ((), (), s32[]{:S(2)}) async-start(), calls=%async_computation.3 | async-start | bytes 18874368 | tf_op jit(solution)/shard_map/all_gather | solution.py:349
  31.0 253.1 %all-gather.26.cloned.1.call-start = ((), (), s32[]{:S(2)}) async-start(), calls=%async_computation.4 | async-start | bytes 18874368 | tf_op jit(solution)/shard_map/all_gather | solution.py:350
  34.1 12.0 copy-start.5
  34.2 13.1 copy-start.6
  34.2 360.0 %all-gather.28.cloned.1.call-start = ((), (), s32[]{:S(2)}) async-start(), calls=%async_computation.5 | async-start | bytes 23592960 | tf_op jit(solution)/shard_map/all_gather | solution.py:349
  39.7 451.5 %all-gather.30.cloned.1.call-start = ((), (), s32[]{:S(2)}) async-start(), calls=%async_computation.6 | async-start | bytes 23592960 | tf_op jit(solution)/shard_map/all_gather | solution.py:350
  45.3 558.5 %all-gather.32.cloned.1.call-start = ((), (), s32[]{:S(2)}) async-start(), calls=%async_computation.7 | async-start | bytes 23592960 | tf_op jit(solution)/shard_map/all_gather | solution.py:349
  46.0 652.6 %all-gather.34.cloned.1.call-start = ((), (), s32[]{:S(2)}) async-start(), calls=%async_computation.8 | async-start | bytes 23592960 | tf_op jit(solution)/shard_map/all_gather | solution.py:350
  46.4 1.7 collective-permute-start
  47.2 1251.1 %all-gather.18.cloned.1.call-start = ((), (), s32[]{:S(2)}) async-start(), calls=%async_computation | async-start | bytes 75497472 | tf_op jit(solution)/shard_map/all_gather | solution.py:397
  48.4 25.2 %collective-permute-start.1 = (s32[512]{0:T(512)S(1)}, s32[512]{0:T(512)S(1)}, u32[]{:S(2)}, u32[]{:S(2)}) collective-permute-start(s32[512]{0:T(512)S(1)} %add_dynamic-update-slice_fusion), channel_id=1, source_target_pairs={{0,2},{1,3},{2,0},{3,1},{4,6},{5,7},{6,4},{7,5}} | collective-permute-start | bytes 6152 | tf_op jit(solution)/shard_map/ppermute | solution.py:316
  73.6 15.3 %collective-permute-start.2 = (s32[512]{0:T(512)S(1)}, s32[512]{0:T(512)S(1)}, u32[]{:S(2)}, u32[]{:S(2)}) collective-permute-start(s32[512]{0:T(512)S(1)} %add.71), channel_id=1, source_target_pairs={{0,4},{1,5},{2,6},{3,7},{4,0},{5,1},{6,2},{7,3}} | collective-permute-start | bytes 6152 | tf_op jit(solution)/shard_map/ppermute | solution.py:316
  83.2 5.8 copy-start
  147.7 61.5 %slice-start.8 = ((s8[8388608]{0:T(1024)(128)(4,1)}), s8[4194304]{0:T(1024)(128)(4,1)S(1)}, s32[]{:S(2)}) async-start(s8[8388608]{0:T(1024)(128)(4,1)} %bitcast.122), calls=%async_computation.17 | async-start | bytes 8388608
  173.8 35.5 %slice-start.9 = ((s8[8388608]{0:T(1024)(128)(4,1)}), s8[4194304]{0:T(1024)(128)(4,1)S(1)}, s32[]{:S(2)}) async-start(s8[8388608]{0:T(1024)(128)(4,1)} %bitcast.122), calls=%async_computation.18 | async-start | bytes 8388608
  900.7 86.0 %collective-permute-start.3 = (bf16[16,64,2048]{2,1,0:T(8,128)(2,1)}, bf16[16,64,2048]{2,1,0:T(8,128)(2,1)}, u32[]{:S(2)}, u32[]{:S(2)}) collective-permute-start(bf16[16,64,2048]{2,1,0:T(8,128)(2,1)} %get-tuple-element.64), channel_id=1, source_target_pairs={{0,1},{1,0},{2,3},{3,2},{4,5},{5,4},{6,7},{7,6}} | collective-permute-start | bytes 12582920 | tf_op jit(solution)/shard_map/ppermute | solution.py:391
  911.4 75.3 %collective-permute-start.4 = (bf16[16,64,3072]{2,1,0:T(8,128)(2,1)}, bf16[16,64,3072]{2,1,0:T(8,128)(2,1)}, u32[]{:S(2)}, u32[]{:S(2)}) collective-permute-start(bf16[16,64,3072]{2,1,0:T(8,128)(2,1)} %get-tuple-element.68), channel_id=1, source_target_pairs={{0,1},{1,0},{2,3},{3,2},{4,5},{5,4},{6,7},{7,6}} | collective-permute-start | bytes 18874376 | tf_op jit(solution)/shard_map/ppermute | solution.py:391
  1076.9 10.0 slice-start
  1076.9 83.5 %collective-permute-start.5 = (f32[4096,3072]{1,0:T(8,128)}, f32[4096,3072]{1,0:T(8,128)}, u32[]{:S(2)}, u32[]{:S(2)}) collective-permute-start(f32[4096,3072]{1,0:T(8,128)} %bitcast_add_fusion.mine_ref), channel_id=1, source_target_pairs={{0,1},{1,0},{2,3},{3,2},{4,5},{5,4},{6,7},{7,6}} | collective-permute-start | bytes 150994944 | tf_op jit(solution)/shard_map/ppermute | solution.py:396
  1077.1 2.3 copy-start.1
  1079.4 7.5 slice-start.1
  1086.9 10.7 slice-start.2
  1086.9 10.7 slice-start.3
  1139.4 129.2 %copy-start.2 = (f32[4096]{0:T(1024)S(1)}, f32[4096]{0:T(1024)}, u32[]{:S(2)}) copy-start(f32[4096]{0:T(1024)} %param.10) | copy-start | bytes 49156
  1139.4 129.2 %copy-start.4 = (f32[16,64]{1,0:T(8,128)S(1)}, f32[16,64]{1,0:T(8,128)}, u32[]{:S(2)}) copy-start(f32[16,64]{1,0:T(8,128)} %copy-done.3) | copy-start | bytes 12292
  1268.6 18.6 %slice-start.4 = ((s8[8388608]{0:T(1024)(128)(4,1)}), s8[4194304]{0:T(1024)(128)(4,1)S(1)}, s32[]{:S(2)}) async-start(s8[8388608]{0:T(1024)(128)(4,1)} %bitcast.116), calls=%async_computation.13 | async-start | bytes 8388608
  1268.6 18.6 %slice-start.6 = ((s8[8388608]{0:T(1024)(128)(4,1)}), s8[4194304]{0:T(1024)(128)(4,1)S(1)}, s32[]{:S(2)}) async-start(s8[8388608]{0:T(1024)(128)(4,1)} %bitcast.119), calls=%async_computation.15 | async-start | bytes 8388608
  1268.6 18.5 %slice-start.5 = ((s8[8388608]{0:T(1024)(128)(4,1)}), s8[4194304]{0:T(1024)(128)(4,1)S(1)}, s32[]{:S(2)}) async-start(s8[8388608]{0:T(1024)(128)(4,1)} %bitcast.116), calls=%async_computation.14 | async-start | bytes 8388608
  1268.6 18.5 %slice-start.7 = ((s8[8388608]{0:T(1024)(128)(4,1)}), s8[4194304]{0:T(1024)(128)(4,1)S(1)}, s32[]{:S(2)}) async-start(s8[8388608]{0:T(1024)(128)(4,1)} %bitcast.119), calls=%async_computation.16 | async-start | bytes 8388608
  1281.7 1.2 collective-permute-start.6
  1282.9 3.7 collective-permute-start.7
  1286.6 11.1 collective-permute-start.8
Sparse Core Ops, SparseCore 0:
  10.4 51.1 all-gather.19
  64.0 48.3 all-gather.21
  114.2 84.0 all-gather.23
  200.0 84.0 all-gather.25
  285.7 101.8 all-gather.27
  389.3 101.8 all-gather.29
  493.0 101.8 all-gather.31
  596.7 101.8 all-gather.33
  830.9 301.6 all-gather.17

commit v4 on v3

--- a/solution.py
+++ b/solution.py
@@ -12,6 +12,7 @@
 ROPE_SCALE = math.sqrt(1.0 + math.log(32.0) / math.log(4096.0))
 LOG2_E = math.log2(math.e)
 CHUNKS = (2, 4, 5, 5)
+SPLIT_ROWS = 768
 
 
 def rope_tables(positions, long_factor):
@@ -197,35 +198,80 @@
     )(core, mine, other)
 
 
-def project_join_kernel(parts, heads, core_ref, grad_ref, weight_ref, mine_ref, other_ref, out_ref, joined_ref):
-    join_heads(core_ref[0] == 0, mine_ref, other_ref, joined_ref, parts, heads)
+def project_join_kernel(parts, heads, limit, core_ref, grad_ref, weight_ref, mine_ref, other_ref, split_ref,
+                        out_ref, joined_ref, sem):
+    step = pl.program_id(0)
+    core = core_ref[0]
+    tile = mine_ref.shape[0]
+    rows = pl.ds(pl.multiple_of(step * tile, tile), tile)
+
+    def copies(halves):
+        start = 0
+        base = 0
+        for cols in parts:
+            for head in range(2 * heads):
+                if halves:
+                    half, at = divmod(head, heads)
+                    ref = other_ref if half else mine_ref
+                    src = ref.at[:, pl.ds(at * sum(parts) + start, cols)]
+                    spot = 2 * at + (1 - core if half else core)
+                else:
+                    src = split_ref.at[head, :, pl.ds(start, cols)]
+                    spot = head
+                dst = joined_ref.at[rows, pl.ds(pl.multiple_of(base + spot * cols, 128), cols)]
+                yield pltpu.make_async_copy(src, dst, sem)
+            start += cols
+            base += 2 * heads * cols
+
+    @pl.when(step < limit)
+    def _():
+        for copy in copies(True):
+            copy.start()
+
+    @pl.when(step >= limit)
+    def _():
+        for copy in copies(False):
+            copy.start()
+
     out_ref[...] = lax.dot_general(grad_ref[...], weight_ref[...], (((1,), (1,)), ((), ())),
                                    preferred_element_type=jnp.float32).astype(jnp.bfloat16)
 
-
-def project_and_join(core, grad, weight, mine, other, parts, heads):
+    @pl.when(step < limit)
+    def _():
+        for copy in copies(True):
+            copy.wait()
+
+    @pl.when(step >= limit)
+    def _():
+        for copy in copies(False):
+            copy.wait()
+
+
+def project_and_join(core, grad, weight, mine, other, split, parts, heads):
     rows, depth = grad.shape
     model = weight.shape[0]
-    half = mine.shape[1]
+    own, half = mine.shape
     tile = 256
-
-    def row_spec(cols):
-        return pl.BlockSpec((tile, cols), lambda t, core_ref: (t, 0))
-
-    return pl.pallas_call(
-        functools.partial(project_join_kernel, parts, heads),
+    limit = own // tile
+
+    half_spec = pl.BlockSpec((tile, half), lambda t, core_ref: (jnp.minimum(t, limit - 1), 0))
+    return pl.pallas_call(
+        functools.partial(project_join_kernel, parts, heads, limit),
         name='project_and_join',
         grid_spec=pltpu.PrefetchScalarGridSpec(
             num_scalar_prefetch=1, grid=(model // tile,),
             in_specs=[pl.BlockSpec((rows, depth), lambda t, core_ref: (0, 0), pipeline_mode=pl.Buffered(1)),
-                      row_spec(depth), row_spec(half), row_spec(half)],
-            out_specs=[pl.BlockSpec((rows, tile), lambda t, core_ref: (0, t)), row_spec(2 * half)]),
+                      pl.BlockSpec((tile, depth), lambda t, core_ref: (t, 0)), half_spec, half_spec,
+                      pl.BlockSpec((split.shape[0], tile, split.shape[2]),
+                                   lambda t, core_ref: (0, jnp.maximum(t - limit, 0), 0))],
+            out_specs=[pl.BlockSpec((rows, tile), lambda t, core_ref: (0, t)), pl.BlockSpec(memory_space=pl.ANY)],
+            scratch_shapes=[pltpu.SemaphoreType.DMA]),
         out_shape=[jax.ShapeDtypeStruct((rows, model), jnp.bfloat16),
                    jax.ShapeDtypeStruct((model, 2 * half), jnp.float32)],
         compiler_params=pltpu.CompilerParams(vmem_limit_bytes=62 * 1024 * 1024),
         cost_estimate=pl.CostEstimate(flops=2 * rows * depth * model,
                                       bytes_accessed=2 * depth * (rows + model) + 16 * model * half, transcendentals=0),
-    )(core, grad, weight, mine, other)
+    )(core, grad, weight, mine, other, split)
 
 
 def pick_columns_kernel(core_ref, query_ref, key_ref, value_ref, out_ref):
@@ -360,7 +406,10 @@
         *earlier, value = lax.optimization_barrier((*earlier, value))
         return (value, *earlier)
 
+    own_rows = model - SPLIT_ROWS
+    width = (group + 2) * dim
     grad_wqkv = None
+    grad_split = None
     grad_wout = None
     tokens = []
     last = len(CHUNKS) - 1
@@ -377,11 +426,16 @@
                 normed_all, attn = after(normed_all, attn)
             tokens[-1] = (attn, grad_qkv)
             qkv = project(normed_all)
-            grad_all, qkv, grad_wout = after(grad_all, qkv, grad_wout)
+            grad_all, qkv, grad_wout, grad_split = after(grad_all, qkv, grad_wout, grad_split)
             grad_attn = project_back(grad_all)
         attn, grad_qkv = attention(qkv, grad_attn, cos, sin, mine_heads, f'attention_{index}')
         tokens.append((attn, grad_qkv))
+        qkv_slice = lax.dynamic_slice_in_dim(grad_qkv, chip * width, width, axis=3)
+        part_split = jnp.einsum('tbsd,tbse->de', normed_all[..., own_rows:], qkv_slice, preferred_element_type=jnp.float32)
+        grad_split = part_split if grad_split is None else grad_split + part_split
         attn_slice = lax.dynamic_slice_in_dim(attn, chip * group * dim, group * dim, axis=3)
+        if index == last:
+            attn_slice, grad_split = after(attn_slice, grad_split)
         part_out = jnp.einsum('tbse,tbsd->ed', attn_slice, grad_all, preferred_element_type=jnp.float32)
         grad_wout = part_out if grad_wout is None else grad_wout + part_out
         if index == last:
@@ -390,10 +444,11 @@
                       zip(zip(*tokens), ('pick_attention', 'pick_gradient'))]
             others = [lax.ppermute(pair[1], 'sp', pairs) for pair in picked]
             grad_qkv, *others = after(grad_qkv, *others)
-        part_qkv = jnp.einsum('tbsd,tbse->de', normed_all, grad_qkv, preferred_element_type=jnp.float32)
+        part_qkv = jnp.einsum('tbsd,tbse->de', normed_all[..., :own_rows], grad_qkv, preferred_element_type=jnp.float32)
         grad_wqkv = part_qkv if grad_wqkv is None else grad_wqkv + part_qkv
 
     grad_wqkv_other = lax.ppermute(grad_wqkv, 'sp', pairs)
+    grad_split = lax.all_gather(grad_split, 'sp', axis=0)
     grad_wout = lax.all_gather(grad_wout, 'sp', axis=0, tiled=True)
     parts = (group * dim, dim, dim)
 
@@ -407,7 +462,8 @@
 
     grad_qkv = natural(1, parts, 'join_gradient')
     grad_qkv, out_hidden = after(grad_qkv, out_hidden)
-    grad_normed, grad_wqkv = project_and_join(core_ref, grad_qkv, w_qkv, grad_wqkv, grad_wqkv_other, parts, mine_heads)
+    grad_normed, grad_wqkv = project_and_join(core_ref, grad_qkv, w_qkv, grad_wqkv, grad_wqkv_other, grad_split,
+                                              parts, mine_heads)
     grad_normed = grad_normed.reshape(batch, sub, model).astype(jnp.float32)
     unit_hidden = hidden_wide * inv_rms
     grad_norm = jnp.sum(grad_normed * unit_hidden, axis=(0, 1))

time: 1360 us -> 1300 us (0.956)
  waiting for transfers between devices: 53.9 us -> 31.1 us
  Pallas kernels: 369 us -> 352 us
  matrix products: 786 us -> 771 us
    pallas_call x1, Pallas kernels: 108 us -> 91.2 us  [project_and_join(): pl.pallas_call(functools.partial(project_join_kernel, parts, heads, limit...]
    ppermute x1, waiting for transfers between devices: 20.9 us -> 4.69 us  [block_body(): grad_wqkv_other = lax.ppermute(grad_wqkv, 'sp', pairs)]
    dot_general x4 -> x8, matrix products: 263 us -> 248 us  [the longest x4 220 us: block_body(): jnp.einsum('tbsd,tbse->de', normed_all[..., :own_rows], grad_qkv, preferr...]
    unnamed x35 -> x41, local copies, waits for them, and re-layouts: 52.8 us -> 52.8 us
  transfers between devices with their start and end apart: 18 -> 19, of which waited for: 7 -> 6; matrix products, arithmetic and copies ran while one was open for 58% -> 59% of each run, Pallas kernels for 23% -> 23%
where the time goes in v4:
time: 1300 us
  matrix products  771 us (59%)
  Pallas kernels  352 us (27%)
  local copies, waits for them, and re-layouts  76.8 us (6%)
  other arithmetic  42.3 us (3%)
  waiting for transfers between devices  31.1 us (2%)
  between operations  14.7 us (1%)
    dot_general x4, matrix products, project(): jnp.einsum('tbsd,de->tbse', normed_all, w_own, preferred_element_type=jnp...  243 us
    dot_general x4, matrix products, block_body(): jnp.einsum('tbsd,tbse->de', normed_all[..., :own_rows], grad_qkv, preferr...  220 us
    pallas_call x4, Pallas kernels, attention(): pl.pallas_call(attention_kernel, name=name, grid=(count, heads), in_specs...  194 us
    dot_general x4, matrix products, project_back(): jnp.einsum('tbsd,ed->tbse', grad_all, wo_own, preferred_element_type=jnp....  172 us
    pallas_call x1, Pallas kernels, project_and_join(): pl.pallas_call(functools.partial(project_join_kernel, parts, heads, limit...  91.2 us
    dot_general x4, matrix products, block_body(): jnp.einsum('tbse,tbsd->ed', attn_slice, grad_all, preferred_element_type=...  66.1 us
    unnamed x41, local copies, waits for them, and re-layouts  52.8 us
    dot_general x1, matrix products, block_body(): jnp.einsum('bse,ed->bsd', attn_flat, w_out, preferred_element_type=jnp.fl...  41.8 us
  transfers between devices with their start and end apart: 19, of which 6 were waited for; matrix products, arithmetic and copies ran while one was open for 59% of the time, Pallas kernels for 23%

profile of v4, /device:TPU:0, one launch (start us, length us, event | category | flops | bytes accessed | tf_op | source)
XLA Modules:
  0.0 1297.8 jit_solution(16221133586073299320)
XLA Ops:
  7.2 2.3 slice.48
  9.6 5.1 fusion.28
  15.3 10.2 fusion.25
  27.8 3.1 slice.66
  31.0 3.1 slice.53
  34.2 5.5 fusion.114
  39.8 5.4 fusion.113
  48.4 2.9 collective-permute-start.1
  51.2 22.4 %pick_columns.1 = bf16[4096,3072]{1,0:T(8,128)(2,1)} custom-call(s32[1]{0:T(128)} %bitcast.core_ref, bf16[4096,6144]{1,0:T(8,128)(2,1)} %weight_ref.1, bf16[4096,6144]{1,0:T(8,128)(2,1)} %weight_ref.1, bf16[4096,6144]{1,0:T(8,128)(2,1)} %weight_ref.1), custom_call_target="tpu_custom_call" | custom-call | flops 402653184 | bytes 50331648 | tf_op jit(solution)/shard_map/pick_columns/pallas_call | solution.py:290
  75.1 8.0 pick_rows.1
  83.1 5.7 copy-done
  90.9 23.7 %convert_bitcast_fusion.grad_ref = bf16[8,2,64,2048]{3,2,1,0:T(8,128)(2,1)} fusion(bf16[8,2,64,4096]{3,2,1,0:T(8,128)(2,1)} %bitcast.141, bf16[2048,4096]{1,0:T(8,128)(2,1)} %copy-done), kind=kOutput, calls=%fused_computation.68 | convolution fusion | flops 17181966336 | bytes 29360128 | tf_op jit(solution)/shard_map/tbsd,ed->tbse/dot_general | solution.py:403
  114.7 33.0 %fusion.75.qkv_ref = bf16[8,2,64,3072]{3,2,1,0:T(8,128)(2,1)} fusion(bf16[8,2,64,4096]{3,2,1,0:T(8,128)(2,1)} %bitcast.162, bf16[4096,3072]{1,0:T(8,128)(2,1)} %pick_columns.1), kind=kOutput, calls=%fused_computation.66 | convolution fusion | flops 25772949504 | bytes 39845888 | tf_op jit(solution)/shard_map/tbsd,de->tbse/dot_general | solution.py:400
  147.7 25.8 %attention_0.1 = (bf16[8,2,64,2048]{3,2,1,0:T(8,128)(2,1)}, bf16[8,2,64,3072]{3,2,1,0:T(8,128)(2,1)}) custom-call(bf16[8,2,64,3072]{3,2,1,0:T(8,128)(2,1)} %fusion.75.qkv_ref, bf16[8,2,64,2048]{3,2,1,0:T(8,128)(2,1)} %convert_bitcast_fusion.grad_ref, f32[512,128]{1,0:T(8,128)} %get-tuple-element.98.cos_ref, f32[512,128]{1,0:T(8,128)} %get-tuple-element.99.sin_ref), custom_call_target="tpu_custom_call" | custom-call | flops 12884901888 | bytes 20971520 | tf_op jit(solution)/shard_map/attention_0/pallas_call | solution.py:148
  173.4 29.8 %convolution_bitcast_fusion = f32[3328,3072]{1,0:T(8,128)} fusion(bf16[8,2,64,3072]{3,2,1,0:T(8,128)(2,1)} %get-tuple-element.50.refs_0_.refs_4_, bf16[8,2,64,4096]{3,2,1,0:T(8,128)(2,1)} %bitcast.163), kind=kOutput, calls=%fused_computation.5 | convolution fusion | flops 20937965568 | bytes 54001664 | tf_op jit(solution)/shard_map/tbsd,tbse->de/dot_general | solution.py:447
  203.2 4.8 convolution_bitcast_fusion.1
  208.1 8.4 fusion.59
  216.5 61.3 %fusion.55.qkv_ref = bf16[8,4,64,3072]{3,2,1,0:T(8,128)(2,1)} fusion(bf16[8,4,64,4096]{3,2,1,0:T(8,128)(2,1)} %bitcast.157, bf16[4096,3072]{1,0:T(8,128)(2,1)} %pick_columns.1), kind=kOutput, calls=%fused_computation.60 | convolution fusion | flops 51545899008 | bytes 54525952 | tf_op jit(solution)/shard_map/tbsd,de->tbse/dot_general | solution.py:400
  277.8 6.3 all-gather.28.cloned.1.call-done
  284.1 42.7 %fusion.78.grad_ref = bf16[8,4,64,2048]{3,2,1,0:T(8,128)(2,1)} fusion(bf16[8,4,64,4096]{3,2,1,0:T(8,128)(2,1)} %bitcast.160, bf16[2048,4096]{1,0:T(8,128)(2,1)} %copy-done), kind=kOutput, calls=%fused_computation.67 | convolution fusion | flops 34363932672 | bytes 41943040 | tf_op jit(solution)/shard_map/tbsd,ed->tbse/dot_general | solution.py:403
  326.8 48.3 %attention_1.1 = (bf16[8,4,64,2048]{3,2,1,0:T(8,128)(2,1)}, bf16[8,4,64,3072]{3,2,1,0:T(8,128)(2,1)}) custom-call(bf16[8,4,64,3072]{3,2,1,0:T(8,128)(2,1)} %fusion.55.qkv_ref, bf16[8,4,64,2048]{3,2,1,0:T(8,128)(2,1)} %fusion.78.grad_ref, f32[512,128]{1,0:T(8,128)} %get-tuple-element.98.cos_ref, f32[512,128]{1,0:T(8,128)} %get-tuple-element.99.sin_ref), custom_call_target="tpu_custom_call" | custom-call | flops 25769803776 | bytes 41943040 | tf_op jit(solution)/shard_map/attention_1/pallas_call | solution.py:148
  375.1 19.0 %bitcast_add_fusion.5 = f32[512,4096]{1,0:T(8,128)} fusion(f32[512,4096]{1,0:T(8,128)} %fusion.59, bf16[8,4,64,4096]{3,2,1,0:T(8,128)(2,1)} %bitcast.161, bf16[8,4,64,2048]{3,2,1,0:T(8,128)(2,1)} %get-tuple-element.56.refs_1_.refs_5_, s32[]{:T(128)S(6)} %select_n.7), kind=kOutput, calls=%fused_computation.57 | convolution fusion | flops 8592031744 | bytes 35651588 | tf_op jit(solution)/shard_map/tbse,tbsd->ed/dot_general | solution.py:439
  394.1 7.0 bitcast_add_fusion.8
  401.1 74.6 %fusion.45.qkv_ref = bf16[8,5,64,3072]{3,2,1,0:T(8,128)(2,1)} fusion(bf16[8,5,64,4096]{3,2,1,0:T(8,128)(2,1)} %bitcast.146, bf16[4096,3072]{1,0:T(8,128)(2,1)} %pick_columns.1), kind=kOutput, calls=%fused_computation.53 | convolution fusion | flops 64432373760 | bytes 61865984 | tf_op jit(solution)/shard_map/tbsd,de->tbse/dot_general | solution.py:400
  475.7 15.5 %all-gather.32.cloned.1.call-done = bf16[40,64,4096]{2,1,0:T(8,128)(2,1)} async-done(((bf16[5,64,4096]{2,1,0:T(8,128)(2,1)}), bf16[40,64,4096]{2,1,0:T(8,128)(2,1)}) %all-gather.32.cloned.1.call-update) | async-done | bytes 20971536 | tf_op jit(solution)/shard_map/all_gather | solution.py:396
  491.2 52.8 %fusion.69.grad_ref = bf16[8,5,64,2048]{3,2,1,0:T(8,128)(2,1)} fusion(bf16[8,5,64,4096]{3,2,1,0:T(8,128)(2,1)} %bitcast.152, bf16[2048,4096]{1,0:T(8,128)(2,1)} %copy-done), kind=kOutput, calls=%fused_computation.64 | convolution fusion | flops 42954915840 | bytes 48234496 | tf_op jit(solution)/shard_map/tbsd,ed->tbse/dot_general | solution.py:403
  544.0 60.0 %attention_2.1 = (bf16[8,5,64,2048]{3,2,1,0:T(8,128)(2,1)}, bf16[8,5,64,3072]{3,2,1,0:T(8,128)(2,1)}) custom-call(bf16[8,5,64,3072]{3,2,1,0:T(8,128)(2,1)} %fusion.45.qkv_ref, bf16[8,5,64,2048]{3,2,1,0:T(8,128)(2,1)} %fusion.69.grad_ref, f32[512,128]{1,0:T(8,128)} %get-tuple-element.98.cos_ref, f32[512,128]{1,0:T(8,128)} %get-tuple-element.99.sin_ref), custom_call_target="tpu_custom_call" | custom-call | flops 32212254720 | bytes 52428800 | tf_op jit(solution)/shard_map/attention_2/pallas_call | solution.py:148
  603.9 8.0 bitcast_add_fusion.7
  611.9 19.7 %bitcast_add_fusion.4 = f32[512,4096]{1,0:T(8,128)} fusion(f32[512,4096]{1,0:T(8,128)} %bitcast_add_fusion.5, bf16[8,5,64,4096]{3,2,1,0:T(8,128)(2,1)} %bitcast.153, bf16[8,5,64,2048]{3,2,1,0:T(8,128)(2,1)} %get-tuple-element.64.refs_2_.refs_6_, s32[]{:T(128)S(6)} %select_n.7), kind=kOutput, calls=%fused_computation.56 | convolution fusion | flops 10739515392 | bytes 40370180 | tf_op jit(solution)/shard_map/tbse,tbsd->ed/dot_general | solution.py:439
  631.7 74.2 %fusion.48.qkv_ref = bf16[8,5,64,3072]{3,2,1,0:T(8,128)(2,1)} fusion(bf16[8,5,64,4096]{3,2,1,0:T(8,128)(2,1)} %bitcast.149, bf16[4096,3072]{1,0:T(8,128)(2,1)} %pick_columns.1), kind=kOutput, calls=%fused_computation.54 | convolution fusion | flops 64432373760 | bytes 61865984 | tf_op jit(solution)/shard_map/tbsd,de->tbse/dot_general | solution.py:400
  705.9 52.8 %fusion.72.grad_ref = bf16[8,5,64,2048]{3,2,1,0:T(8,128)(2,1)} fusion(bf16[8,5,64,4096]{3,2,1,0:T(8,128)(2,1)} %bitcast.154, bf16[2048,4096]{1,0:T(8,128)(2,1)} %copy-done), kind=kOutput, calls=%fused_computation.65 | convolution fusion | flops 42954915840 | bytes 48234496 | tf_op jit(solution)/shard_map/tbsd,ed->tbse/dot_general | solution.py:403
  758.7 59.9 %attention_3.1 = (bf16[8,5,64,2048]{3,2,1,0:T(8,128)(2,1)}, bf16[8,5,64,3072]{3,2,1,0:T(8,128)(2,1)}) custom-call(bf16[8,5,64,3072]{3,2,1,0:T(8,128)(2,1)} %fusion.48.qkv_ref, bf16[8,5,64,2048]{3,2,1,0:T(8,128)(2,1)} %fusion.72.grad_ref, f32[512,128]{1,0:T(8,128)} %get-tuple-element.98.cos_ref, f32[512,128]{1,0:T(8,128)} %get-tuple-element.99.sin_ref), custom_call_target="tpu_custom_call" | custom-call | flops 32212254720 | bytes 52428800 | tf_op jit(solution)/shard_map/attention_3/pallas_call | solution.py:148
  820.5 8.1 bitcast_add_fusion.6
  828.7 19.0 %bitcast_add_fusion.3 = f32[512,4096]{1,0:T(8,128)} fusion(f32[512,4096]{1,0:T(8,128)} %bitcast_add_fusion.4, bf16[8,5,64,4096]{3,2,1,0:T(8,128)(2,1)} %bitcast.155, bf16[8,5,64,512]{3,2,1,0:T(8,128)(2,1)S(1)} %constant_dynamic-slice_fusion), kind=kOutput, calls=%fused_computation.55 | convolution fusion | flops 10739515392 | bytes 40370176 | tf_op jit(solution)/shard_map/tbse,tbsd->ed/dot_general | solution.py:439
  848.3 52.1 %fusion.42 = f32[3328,3072,1,1]{1,0,3,2:T(8,128)} fusion(bf16[8,4,64,3072]{3,2,1,0:T(8,128)(2,1)} %get-tuple-element.60.refs_1_.refs_5_, bf16[8,4,64,4096]{3,2,1,0:T(8,128)(2,1)} %bitcast.159), kind=kOutput, calls=%fused_computation.50 | convolution fusion | flops 41875931136 | bytes 67108864 | tf_op jit(solution)/shard_map/tbsd,tbse->de/dot_general | solution.py:447
  900.4 7.7 pick_attention.1
  908.3 10.5 pick_gradient.1
  919.1 62.6 %fusion.20 = f32[3328,3072,1,1]{1,0,3,2:T(8,128)} fusion(bf16[8,5,64,3072]{3,2,1,0:T(8,128)(2,1)} %get-tuple-element.68.refs_2_.refs_6_, bf16[8,5,64,4096]{3,2,1,0:T(8,128)(2,1)} %bitcast.148), kind=kOutput, calls=%fused_computation.28 | convolution fusion | flops 52344913920 | bytes 73662464 | tf_op jit(solution)/shard_map/tbsd,tbse->de/dot_general | solution.py:447
  981.7 75.5 %bitcast_add_fusion.mine_ref = f32[3328,3072]{1,0:T(8,128)} fusion(f32[3328,3072,1,1]{1,0,3,2:T(8,128)} %fusion.20, f32[3328,3072]{1,0:T(8,128)} %convolution_bitcast_fusion, f32[3328,3072,1,1]{1,0,3,2:T(8,128)} %fusion.42, bf16[8,5,64,3072]{3,2,1,0:T(8,128)(2,1)} %get-tuple-element.82.refs_3_.refs_7_, bf16[8,5,64,4096]{3,2,1,0:T(8,128)(2,1)} %bitcast.151), kind=kOutput, calls=%fused_computation | convolution fusion | flops 52375584768 | bytes 196345856 | tf_op jit(solution)/shard_map/tbsd,tbse->de/dot_general | solution.py:447
  1057.5 2.3 copy-done.1
  1059.8 7.5 join_attention.1
  1067.3 10.8 join_gradient.1.grad_ref
  1078.1 41.8 %fusion.29 = bf16[16,64,4096]{2,1,0:T(8,128)(2,1)} fusion(bf16[16,64,4096]{2,1,0:T(8,128)(2,1)S(1)} %bitcast.135, bf16[16,64,4096]{2,1,0:T(8,128)(2,1)} %bitcast.145, bf16[4096,4096]{1,0:T(8,128)(2,1)} %in_ref.1), kind=kOutput, calls=%fused_computation.37 | convolution fusion | flops 34372321280 | bytes 58720256 | tf_op jit(solution)/shard_map/bse,ed->bsd/dot_general | solution.py:460
  1119.8 4.7 collective-permute-done.5.other_ref
  1124.5 91.2 %project_and_join.1 = (bf16[1024,4096]{1,0:T(8,128)(2,1)}, f32[4096,6144]{1,0:T(8,128)}) custom-call(s32[1]{0:T(128)} %bitcast.core_ref, bf16[1024,6144]{1,0:T(8,128)(2,1)} %join_gradient.1.grad_ref, bf16[4096,6144]{1,0:T(8,128)(2,1)} %weight_ref.1, f32[3328,3072]{1,0:T(8,128)} %bitcast_add_fusion.mine_ref, f32[3328,3072]{1,0:T(8,128)} %collective-permute-done.5.other_ref, ...), custom_call_target="tpu_custom_call" | custom-call | flops 51539607552 | bytes 264241152 | tf_op jit(solution)/shard_map/project_and_join/pallas_call | solution.py:258
  1215.8 13.0 %fusion.27 = (f32[4096]{0:T(1024)S(1)}, f32[16,64]{1,0:T(8,128)S(1)}) fusion(bf16[16,64,4096]{2,1,0:T(8,128)(2,1)} %param.7, f32[16,64]{1,0:T(8,128)S(1)} %copy-done.4, bf16[1024,4096]{1,0:T(8,128)(2,1)} %get-tuple-element.85, f32[4096]{0:T(1024)S(1)} %copy-done.2, bf16[16,64,4096]{2,1,0:T(8,128)(2,1)} %bitcast.138), kind=kLoop, calls=%fused_computation.35 | loop fusion | flops 37743616 | bytes 25206784 | tf_op jit(solution)/shard_map/reduce_sum | solution.py:469
  1235.5 10.5 fusion.24
  1246.6 44.1 %copy.200 = f32[4096,4096]{1,0:T(8,128)} copy(f32[4096,4096]{1,0:T(8,128)} %all-gather.20.cloned.1.call-done) | data formatting | bytes 134217728
  (103 shorter events, 20.5 us)
Async XLA Ops:
  7.2 83.8 %all-gather.22.cloned.1.call-start = ((), (), s32[]{:S(2)}) async-start(), calls=%async_computation.1 | async-start | bytes 9437184 | tf_op jit(solution)/shard_map/all_gather | solution.py:396
  9.5 105.1 %all-gather.24.cloned.1.call-start = ((), (), s32[]{:S(2)}) async-start(), calls=%async_computation.2 | async-start | bytes 9437184 | tf_op jit(solution)/shard_map/all_gather | solution.py:395
  14.7 0.6 copy-start.3
  27.7 188.8 %all-gather.26.cloned.1.call-start = ((), (), s32[]{:S(2)}) async-start(), calls=%async_computation.3 | async-start | bytes 18874368 | tf_op jit(solution)/shard_map/all_gather | solution.py:395
  30.9 253.1 %all-gather.28.cloned.1.call-start = ((), (), s32[]{:S(2)}) async-start(), calls=%async_computation.4 | async-start | bytes 18874368 | tf_op jit(solution)/shard_map/all_gather | solution.py:396
  34.1 12.0 copy-start.5
  34.2 13.1 %copy-start.6 = (f32[64]{0:T(128)S(1)}, f32[64]{0:T(128)}, u32[]{:S(2)}) copy-start(f32[64]{0:T(128)} %param.9) | copy-start | bytes 772
  34.2 366.9 %all-gather.30.cloned.1.call-start = ((), (), s32[]{:S(2)}) async-start(), calls=%async_computation.5 | async-start | bytes 23592960 | tf_op jit(solution)/shard_map/all_gather | solution.py:395
  39.8 451.4 %all-gather.32.cloned.1.call-start = ((), (), s32[]{:S(2)}) async-start(), calls=%async_computation.6 | async-start | bytes 23592960 | tf_op jit(solution)/shard_map/all_gather | solution.py:396
  45.3 558.6 %all-gather.34.cloned.1.call-start = ((), (), s32[]{:S(2)}) async-start(), calls=%async_computation.7 | async-start | bytes 23592960 | tf_op jit(solution)/shard_map/all_gather | solution.py:395
  46.0 659.8 %all-gather.36.cloned.1.call-start = ((), (), s32[]{:S(2)}) async-start(), calls=%async_computation.8 | async-start | bytes 23592960 | tf_op jit(solution)/shard_map/all_gather | solution.py:396
  46.4 1.7 collective-permute-start
  47.2 1072.6 %all-gather.38.cloned.1.call-start = ((), (), s32[]{:S(2)}) async-start(), calls=%async_computation.9 | async-start | bytes 21233664 | tf_op jit(solution)/shard_map/all_gather | solution.py:451
  48.4 25.2 %collective-permute-start.1 = (s32[512]{0:T(512)S(1)}, s32[512]{0:T(512)S(1)}, u32[]{:S(2)}, u32[]{:S(2)}) collective-permute-start(s32[512]{0:T(512)S(1)} %add_dynamic-update-slice_fusion), channel_id=1, source_target_pairs={{0,2},{1,3},{2,0},{3,1},{4,6},{5,7},{6,4},{7,5}} | collective-permute-start | bytes 6152 | tf_op jit(solution)/shard_map/ppermute | solution.py:362
  73.6 15.3 %collective-permute-start.2 = (s32[512]{0:T(512)S(1)}, s32[512]{0:T(512)S(1)}, u32[]{:S(2)}, u32[]{:S(2)}) collective-permute-start(s32[512]{0:T(512)S(1)} %add.86), channel_id=1, source_target_pairs={{0,4},{1,5},{2,6},{3,7},{4,0},{5,1},{6,2},{7,3}} | collective-permute-start | bytes 6152 | tf_op jit(solution)/shard_map/ppermute | solution.py:362
  83.1 5.7 copy-start
  147.7 60.4 %slice-start.8 = ((s8[8388608]{0:T(1024)(128)(4,1)}), s8[4194304]{0:T(1024)(128)(4,1)S(1)}, s32[]{:S(2)}) async-start(s8[8388608]{0:T(1024)(128)(4,1)} %bitcast.142), calls=%async_computation.18 | async-start | bytes 8388608
  173.4 34.6 %slice-start.9 = ((s8[8388608]{0:T(1024)(128)(4,1)}), s8[4194304]{0:T(1024)(128)(4,1)S(1)}, s32[]{:S(2)}) async-start(s8[8388608]{0:T(1024)(128)(4,1)} %bitcast.142), calls=%async_computation.19 | async-start | bytes 8388608
  375.1 19.0 %copy-start.7 = (f32[768,768]{1,0:T(8,128)S(1)}, f32[768,768]{1,0:T(8,128)}, u32[]{:S(2)}) copy-start(f32[768,768]{1,0:T(8,128)} %convolution_bitcast_fusion.1) | copy-start | bytes 7077892
  544.0 60.0 %copy-start.8 = (f32[768,768]{1,0:T(8,128)S(1)}, f32[768,768]{1,0:T(8,128)}, u32[]{:S(2)}) copy-start(f32[768,768]{1,0:T(8,128)} %bitcast_add_fusion.8) | copy-start | bytes 7077892
  758.7 61.9 %copy-start.9 = (f32[768,768]{1,0:T(8,128)S(1)}, f32[768,768]{1,0:T(8,128)}, u32[]{:S(2)}) copy-start(f32[768,768]{1,0:T(8,128)} %bitcast_add_fusion.7) | copy-start | bytes 7077892
  828.6 418.0 %all-gather.20.cloned.1.call-start = ((), (), s32[]{:S(2)}) async-start(), calls=%async_computation | async-start | bytes 75497472 | tf_op jit(solution)/shard_map/all_gather | solution.py:452
  908.0 73.6 %collective-permute-start.3 = (bf16[16,64,2048]{2,1,0:T(8,128)(2,1)}, bf16[16,64,2048]{2,1,0:T(8,128)(2,1)}, u32[]{:S(2)}, u32[]{:S(2)}) collective-permute-start(bf16[16,64,2048]{2,1,0:T(8,128)(2,1)} %get-tuple-element.73), channel_id=1, source_target_pairs={{0,1},{1,0},{2,3},{3,2},{4,5},{5,4},{6,7},{7,6}} | collective-permute-start | bytes 12582920 | tf_op jit(solution)/shard_map/ppermute | solution.py:445
  918.8 62.8 %collective-permute-start.4 = (bf16[16,64,3072]{2,1,0:T(8,128)(2,1)}, bf16[16,64,3072]{2,1,0:T(8,128)(2,1)}, u32[]{:S(2)}, u32[]{:S(2)}) collective-permute-start(bf16[16,64,3072]{2,1,0:T(8,128)(2,1)} %get-tuple-element.75), channel_id=1, source_target_pairs={{0,1},{1,0},{2,3},{3,2},{4,5},{5,4},{6,7},{7,6}} | collective-permute-start | bytes 18874376 | tf_op jit(solution)/shard_map/ppermute | solution.py:445
  1057.2 10.1 slice-start
  1057.2 67.3 %collective-permute-start.5 = (f32[3328,3072]{1,0:T(8,128)}, f32[3328,3072]{1,0:T(8,128)}, u32[]{:S(2)}, u32[]{:S(2)}) collective-permute-start(f32[3328,3072]{1,0:T(8,128)} %bitcast_add_fusion.mine_ref), channel_id=1, source_target_pairs={{0,1},{1,0},{2,3},{3,2},{4,5},{5,4},{6,7},{7,6}} | collective-permute-start | bytes 122683400 | tf_op jit(solution)/shard_map/ppermute | solution.py:450
  1057.4 2.3 copy-start.1
  1059.8 7.5 slice-start.1
  1067.3 10.8 slice-start.2
  1067.3 10.8 slice-start.3
  1124.5 91.3 %copy-start.2 = (f32[4096]{0:T(1024)S(1)}, f32[4096]{0:T(1024)}, u32[]{:S(2)}) copy-start(f32[4096]{0:T(1024)} %param.10) | copy-start | bytes 49156
  1124.5 91.3 %copy-start.4 = (f32[16,64]{1,0:T(8,128)S(1)}, f32[16,64]{1,0:T(8,128)}, u32[]{:S(2)}) copy-start(f32[16,64]{1,0:T(8,128)} %copy-done.3) | copy-start | bytes 12292
  1215.8 19.7 %slice-start.4 = ((s8[8388608]{0:T(1024)(128)(4,1)}), s8[4194304]{0:T(1024)(128)(4,1)S(1)}, s32[]{:S(2)}) async-start(s8[8388608]{0:T(1024)(128)(4,1)} %bitcast.136), calls=%async_computation.14 | async-start | bytes 8388608
  1215.8 19.7 %slice-start.6 = ((s8[8388608]{0:T(1024)(128)(4,1)}), s8[4194304]{0:T(1024)(128)(4,1)S(1)}, s32[]{:S(2)}) async-start(s8[8388608]{0:T(1024)(128)(4,1)} %bitcast.139), calls=%async_computation.16 | async-start | bytes 8388608
  1215.8 19.7 %slice-start.5 = ((s8[8388608]{0:T(1024)(128)(4,1)}), s8[4194304]{0:T(1024)(128)(4,1)S(1)}, s32[]{:S(2)}) async-start(s8[8388608]{0:T(1024)(128)(4,1)} %bitcast.136), calls=%async_computation.15 | async-start | bytes 8388608
  1215.8 19.7 %slice-start.7 = ((s8[8388608]{0:T(1024)(128)(4,1)}), s8[4194304]{0:T(1024)(128)(4,1)S(1)}, s32[]{:S(2)}) async-start(s8[8388608]{0:T(1024)(128)(4,1)} %bitcast.139), calls=%async_computation.17 | async-start | bytes 8388608
  1228.8 1.2 collective-permute-start.6
  1230.1 3.7 collective-permute-start.7
  1233.8 12.2 collective-permute-start.8
Sparse Core Ops, SparseCore 0:
  10.4 51.1 all-gather.21
  64.0 48.3 all-gather.23
  114.2 84.0 all-gather.25
  200.0 84.0 all-gather.27
  285.7 101.8 all-gather.29
  389.3 101.8 all-gather.31
  493.0 101.8 all-gather.33
  596.7 101.8 all-gather.35
  828.8 94.3 all-gather.37
  924.8 297.1 all-gather.19

commit v5 on v4

--- a/solution.py
+++ b/solution.py
@@ -25,14 +25,16 @@
     return jnp.concatenate([cos_half, cos_half], axis=-1), jnp.concatenate([-sin_half, sin_half], axis=-1)
 
 
-def attention_kernel(qkv_ref, grad_ref, cos_ref, sin_ref, out_ref, dqkv_ref, dkey_s, dvalue_s):
+def attention_kernel(group, qkv_ref, grad_ref, cos_ref, sin_ref, out_ref, dqkv_ref, dkey_s, dvalue_s):
     devs, _, sub, width = qkv_ref.shape
     dim = cos_ref.shape[1]
     seq = devs * sub
-    group = width // dim - 2
+    per_head = (group + 2) * dim
     block = 128
     per = block // sub
     scale = dim ** -0.5
+    heads_unit = 2
+    cols = heads_unit * block
 
     def rope(vals, cos, sin):
         wide = vals.astype(jnp.float32)
@@ -48,21 +50,23 @@
     def nn(lhs, rhs):
         return jnp.dot(lhs, rhs, preferred_element_type=jnp.float32)
 
-    key_raw = qkv_ref[:, 0, :, group * dim:(group + 1) * dim].reshape(seq, dim)
-    value = qkv_ref[:, 0, :, (group + 1) * dim:].reshape(seq, dim)
-    key = rope(key_raw, cos_ref[...], sin_ref[...])
-    key_t = key.T
-    value_t = value.T
-    heads_unit = 2
-    cols = heads_unit * block
     row_ids = lax.broadcasted_iota(jnp.int32, (block, cols), 0)
     col_ids = lax.broadcasted_iota(jnp.int32, (block, cols), 1)
     allowed = row_ids <= lax.rem(col_ids, block)
-    units = [(step, first) for step in reversed(range(seq // block)) for first in range(0, group, heads_unit)]
+    units = [(kv, step, first) for kv in range(width // per_head)
+             for step in reversed(range(seq // block)) for first in range(0, group, heads_unit)]
     state = {}
+    shared = {}
 
     def load(unit):
-        step, first = units[unit]
+        kv, step, first = units[unit]
+        base = kv * per_head
+        if kv not in shared:
+            key_raw = qkv_ref[:, 0, :, base + group * dim:base + (group + 1) * dim].reshape(seq, dim)
+            value = qkv_ref[:, 0, :, base + (group + 1) * dim:base + per_head].reshape(seq, dim)
+            key = rope(key_raw, cos_ref[...], sin_ref[...])
+            shared[kv] = key, value, key.T, value.T
+        key, value = shared[kv][:2]
         rows = pl.ds(step * block, block)
         cos = cos_ref[rows, :]
         sin = sin_ref[rows, :]
@@ -70,9 +74,9 @@
         queries = []
         grads = []
         for head in range(first, first + heads_unit):
-            lanes = pl.ds(head * dim, dim)
-            raw = qkv_ref[step * per:(step + 1) * per, 0, :, lanes].reshape(block, dim)
+            raw = qkv_ref[step * per:(step + 1) * per, 0, :, pl.ds(base + head * dim, dim)].reshape(block, dim)
             queries.append(rope(raw, cos, sin))
+            lanes = pl.ds((kv * group + head) * dim, dim)
             grads.append(grad_ref[step * per:(step + 1) * per, 0, :, lanes].reshape(block, dim))
         query = jnp.concatenate(queries, axis=0)
         grad = jnp.concatenate(grads, axis=0)
@@ -81,7 +85,7 @@
         state[unit] = (query, grad, scores, grad_probs)
 
     def soften(unit):
-        step, first = units[unit]
+        kv, step, first = units[unit]
         span = (step + 1) * block
         query, grad, scores, grad_probs = state[unit]
         last = jnp.where(allowed, scores[span - block:], -jnp.inf)
@@ -95,7 +99,9 @@
         state[unit] = (query, grad, probs.astype(jnp.bfloat16), grad_scores)
 
     def finish(unit):
-        step, first = units[unit]
+        kv, step, first = units[unit]
+        base = kv * per_head
+        key_t, value_t = shared[kv][2:]
         rows = pl.ds(step * block, block)
         cos = cos_ref[rows, :]
         sin = sin_ref[rows, :]
@@ -105,18 +111,25 @@
         grad_query = (nn(key_t[:, :span], grad_scores) * scale).astype(jnp.bfloat16).T
         part_value = nn(probs_low, grad)
         part_key = nn(grad_scores, query)
-        if unit == 0:
-            dvalue_s[...] = part_value
-            dkey_s[...] = part_key
+        if span == seq and first == 0:
+            dvalue_s[kv] = part_value
+            dkey_s[kv] = part_key
         else:
-            dvalue_s[:span, :] += part_value
-            dkey_s[:span, :] += part_key
+            dvalue_s[kv, :span, :] += part_value
+            dkey_s[kv, :span, :] += part_key
         for head in range(heads_unit):
-            lanes = pl.ds((first + head) * dim, dim)
             part = slice(head * block, (head + 1) * block)
+            lanes = pl.ds((kv * group + first + head) * dim, dim)
             out_ref[step * per:(step + 1) * per, 0, :, lanes] = attn[part].reshape(per, sub, dim)
             back = rope_back(grad_query[part], cos, sin)
+            lanes = pl.ds(base + (first + head) * dim, dim)
             dqkv_ref[step * per:(step + 1) * per, 0, :, lanes] = back.reshape(per, sub, dim)
+        if step == 0 and first + heads_unit == group:
+            grad_key = (dkey_s[kv] * scale).astype(jnp.bfloat16)
+            back = rope_back(grad_key, cos_ref[...], sin_ref[...])
+            dqkv_ref[:, 0, :, base + group * dim:base + (group + 1) * dim] = back.reshape(devs, sub, dim)
+            last = dvalue_s[kv].astype(jnp.bfloat16).reshape(devs, sub, dim)
+            dqkv_ref[:, 0, :, base + (group + 1) * dim:base + per_head] = last
 
     count = len(units)
     load(0)
@@ -128,13 +141,8 @@
         if unit > 0:
             finish(unit - 1)
 
-    grad_key = (dkey_s[...] * scale).astype(jnp.bfloat16)
-    back = rope_back(grad_key, cos_ref[...], sin_ref[...])
-    dqkv_ref[:, 0, :, group * dim:(group + 1) * dim] = back.reshape(devs, sub, dim)
-    dqkv_ref[:, 0, :, (group + 1) * dim:] = dvalue_s[...].astype(jnp.bfloat16).reshape(devs, sub, dim)
-
-
-def attention(qkv, grad, cos, sin, heads, name):
+
+def attention(qkv, grad, cos, sin, heads, name, kvs=2):
     devs, count, sub, width = qkv.shape
     dim = cos.shape[1]
     seq = devs * sub
@@ -142,18 +150,18 @@
     group = per_head // dim - 2
 
     def head_spec(cols):
-        return pl.BlockSpec((devs, 1, sub, cols), lambda b, a: (0, b, 0, a))
+        return pl.BlockSpec((devs, 1, sub, kvs * cols), lambda b, a: (0, b, 0, a))
 
     table_spec = pl.BlockSpec((seq, dim), lambda b, a: (0, 0))
     return pl.pallas_call(
-        attention_kernel,
+        functools.partial(attention_kernel, group),
         name=name,
-        grid=(count, heads),
+        grid=(count, heads // kvs),
         in_specs=[head_spec(per_head), head_spec(group * dim), table_spec, table_spec],
         out_specs=[head_spec(group * dim), head_spec(per_head)],
         out_shape=[jax.ShapeDtypeStruct((devs, count, sub, heads * cols), jnp.bfloat16)
                    for cols in (group * dim, per_head)],
-        scratch_shapes=[pltpu.VMEM((seq, dim), jnp.float32), pltpu.VMEM((seq, dim), jnp.float32)],
+        scratch_shapes=[pltpu.VMEM((kvs, seq, dim), jnp.float32), pltpu.VMEM((kvs, seq, dim), jnp.float32)],
         compiler_params=pltpu.CompilerParams(vmem_limit_bytes=56 * 1024 * 1024),
         cost_estimate=pl.CostEstimate(flops=count * heads * group * 6 * 2 * seq * seq * dim,
                                       bytes_accessed=4 * (qkv.size + grad.size),
@@ -274,6 +282,64 @@
     )(core, grad, weight, mine, other, split)
 
 
+def output_kernel(attn_ref, weight_ref, hidden_ref, half_ref, out_ref, full_ref, sem):
+    tile, cols = half_ref.shape
+    rows = pl.ds(pl.multiple_of(pl.program_id(0) * tile, tile), tile)
+    copy = pltpu.make_async_copy(half_ref, full_ref.at[rows, pl.ds(0, cols)], sem)
+    copy.start()
+    mixed = jnp.dot(attn_ref[...], weight_ref[...], preferred_element_type=jnp.float32)
+    out_ref[...] = (hidden_ref[...].astype(jnp.float32) + mixed).astype(jnp.bfloat16)
+    copy.wait()
+
+
+def output_and_copy(attn, weight, hidden, half):
+    rows, depth = attn.shape
+    model = weight.shape[1]
+    total, cols = half.shape
+    steps = 8
+    tile = model // steps
+    return pl.pallas_call(
+        output_kernel,
+        name='output_and_copy',
+        grid=(steps,),
+        in_specs=[pl.BlockSpec((rows, depth), lambda t: (0, 0), pipeline_mode=pl.Buffered(1)),
+                  pl.BlockSpec((depth, tile), lambda t: (0, t)), pl.BlockSpec((rows, tile), lambda t: (0, t)),
+                  pl.BlockSpec((total // steps, cols), lambda t: (t, 0))],
+        out_specs=[pl.BlockSpec((rows, tile), lambda t: (0, t)), pl.BlockSpec(memory_space=pl.ANY)],
+        out_shape=[jax.ShapeDtypeStruct((rows, model), jnp.bfloat16),
+                   jax.ShapeDtypeStruct((total, 2 * cols), jnp.float32)],
+        scratch_shapes=[pltpu.SemaphoreType.DMA],
+        compiler_params=pltpu.CompilerParams(vmem_limit_bytes=60 * 1024 * 1024),
+        cost_estimate=pl.CostEstimate(flops=2 * rows * depth * model,
+                                      bytes_accessed=2 * depth * (rows + model) + 8 * total * cols, transcendentals=0),
+    )(attn, weight, hidden, half)
+
+
+def second_half_kernel(left_ref, half_ref, full_ref, sem):
+    tile, cols = half_ref.shape
+    rows = pl.ds(pl.multiple_of(pl.program_id(0) * tile, tile), tile)
+    copy = pltpu.make_async_copy(half_ref, full_ref.at[rows, pl.ds(cols, cols)], sem)
+    copy.start()
+    copy.wait()
+
+
+def second_half(full, half):
+    total, cols = half.shape
+    steps = 8
+    return pl.pallas_call(
+        second_half_kernel,
+        name='second_half',
+        grid=(steps,),
+        in_specs=[pl.BlockSpec(memory_space=pl.ANY), pl.BlockSpec((total // steps, cols), lambda t: (t, 0))],
+        out_specs=pl.BlockSpec(memory_space=pl.ANY),
+        out_shape=jax.ShapeDtypeStruct(full.shape, full.dtype),
+        scratch_shapes=[pltpu.SemaphoreType.DMA],
+        input_output_aliases={0: 0},
+        compiler_params=pltpu.CompilerParams(vmem_limit_bytes=32 * 1024 * 1024),
+        cost_estimate=pl.CostEstimate(flops=32 * total * cols, bytes_accessed=8 * total * cols, transcendentals=0),
+    )(full, half)
+
+
 def pick_columns_kernel(core_ref, query_ref, key_ref, value_ref, out_ref):
     query = query_ref.shape[1]
     small = key_ref.shape[1]
@@ -410,7 +476,7 @@
     width = (group + 2) * dim
     grad_wqkv = None
     grad_split = None
-    grad_wout = None
+    grad_wout = [None, None]
     tokens = []
     last = len(CHUNKS) - 1
     for index, (normed_all, grad_all) in enumerate(gathered):
@@ -426,7 +492,7 @@
                 normed_all, attn = after(normed_all, attn)
             tokens[-1] = (attn, grad_qkv)
             qkv = project(normed_all)
-            grad_all, qkv, grad_wout, grad_split = after(grad_all, qkv, grad_wout, grad_split)
+            grad_all, qkv, *grad_wout, grad_split = after(grad_all, qkv, *grad_wout, grad_split)
             grad_attn = project_back(grad_all)
         attn, grad_qkv = attention(qkv, grad_attn, cos, sin, mine_heads, f'attention_{index}')
         tokens.append((attn, grad_qkv))
@@ -436,8 +502,10 @@
         attn_slice = lax.dynamic_slice_in_dim(attn, chip * group * dim, group * dim, axis=3)
         if index == last:
             attn_slice, grad_split = after(attn_slice, grad_split)
-        part_out = jnp.einsum('tbse,tbsd->ed', attn_slice, grad_all, preferred_element_type=jnp.float32)
-        grad_wout = part_out if grad_wout is None else grad_wout + part_out
+        for side in range(2):
+            lanes = slice(side * model // 2, (side + 1) * model // 2)
+            part_out = jnp.einsum('tbse,tbsd->ed', attn_slice, grad_all[..., lanes], preferred_element_type=jnp.float32)
+            grad_wout[side] = part_out if grad_wout[side] is None else grad_wout[side] + part_out
         if index == last:
             ends = jnp.stack([me, partner])
             picked = [pick_tokens(ends, list(arrays), name) for arrays, name in
@@ -449,16 +517,16 @@
 
     grad_wqkv_other = lax.ppermute(grad_wqkv, 'sp', pairs)
     grad_split = lax.all_gather(grad_split, 'sp', axis=0)
-    grad_wout = lax.all_gather(grad_wout, 'sp', axis=0, tiled=True)
+    grad_wout = [lax.all_gather(half, 'sp', axis=0, tiled=True) for half in grad_wout]
     parts = (group * dim, dim, dim)
 
     def natural(index, parts, name):
         rows = (batch * sub, -1)
         return join_columns(core_ref, picked[index][0].reshape(rows), others[index].reshape(rows), parts, mine_heads, name)
 
-    attn_flat = natural(0, parts[:1], 'join_attention').reshape(batch, sub, -1)
-    mixed_out = jnp.einsum('bse,ed->bsd', attn_flat, w_out, preferred_element_type=jnp.float32)
-    out_hidden = (hidden_wide + mixed_out).astype(jnp.bfloat16)
+    attn_flat = natural(0, parts[:1], 'join_attention')
+    out_hidden, grad_wout_full = output_and_copy(attn_flat, w_out, hidden.reshape(batch * sub, model), grad_wout[0])
+    out_hidden = out_hidden.reshape(batch, sub, model)
 
     grad_qkv = natural(1, parts, 'join_gradient')
     grad_qkv, out_hidden = after(grad_qkv, out_hidden)
@@ -471,6 +539,7 @@
     grad_inner = inv_rms * (grad_unit - unit_hidden * jnp.mean(grad_unit * unit_hidden, axis=-1, keepdims=True))
     grad_hidden = (grad_out.astype(jnp.float32) + grad_inner).astype(jnp.bfloat16)
 
+    grad_wout = second_half(grad_wout_full, grad_wout[1])
     return out_hidden, grad_hidden, exchange_sum(grad_norm, devs), grad_wqkv, grad_wout
 
 

time: 1300 us -> 1280 us (0.985)
  Pallas kernels: 352 us -> 415 us
  matrix products: 771 us -> 734 us
  local copies, waits for them, and re-layouts: 76.8 us -> 43.5 us
  waiting for transfers between devices: 31.1 us -> 14.2 us
    pallas_call x4 -> x6, Pallas kernels: 194 us -> 259 us  [the longest x4 188 us: attention(): pl.pallas_call(functools.partial(attention_kernel, group), name=name, gri...]
    unnamed x41 -> x52, local copies, waits for them, and re-layouts: 52.8 us -> 12.3 us
    dot_general x5 -> x8, matrix products: 108 us -> 73 us  [block_body(): jnp.einsum('tbse,tbsd->ed', attn_slice, grad_all[..., lanes], preferred_e...]
  transfers between devices with their start and end apart: 19 -> 20, of which waited for: 6 -> 4; matrix products, arithmetic and copies ran while one was open for 59% -> 57% of each run, Pallas kernels for 23% -> 28%
where the time goes in v5:
time: 1280 us; the launch traced here: 1270 us
  matrix products  734 us (57%)
  Pallas kernels  415 us (32%)
  other arithmetic  44.2 us (3%)
  local copies, waits for them, and re-layouts  43.5 us (3%)
  between operations  14.5 us (1%)
  waiting for transfers between devices  14.2 us (1%)
    dot_general x4, matrix products, project(): jnp.einsum('tbsd,de->tbse', normed_all, w_own, preferred_element_type=jnp...  244 us
    dot_general x4, matrix products, block_body(): jnp.einsum('tbsd,tbse->de', normed_all[..., :own_rows], grad_qkv, preferr...  219 us
    pallas_call x4, Pallas kernels, attention(): pl.pallas_call(functools.partial(attention_kernel, group), name=name, gri...  188 us
    dot_general x4, matrix products, project_back(): jnp.einsum('tbsd,ed->tbse', grad_all, wo_own, preferred_element_type=jnp....  169 us
    pallas_call x1, Pallas kernels, project_and_join(): pl.pallas_call(functools.partial(project_join_kernel, parts, heads, limit...  91.2 us
    dot_general x8, matrix products, block_body(): jnp.einsum('tbse,tbsd->ed', attn_slice, grad_all[..., lanes], preferred_e...  73 us
    pallas_call x1, Pallas kernels, output_and_copy(): pl.pallas_call(output_kernel, name='output_and_copy', grid=(steps,), in_s...  48.1 us
    dot_general x4, matrix products, block_body(): jnp.einsum('tbsd,tbse->de', normed_all[..., own_rows:], qkv_slice, prefer...  28.5 us
  transfers between devices with their start and end apart: 20, of which 4 were waited for; matrix products, arithmetic and copies ran while one was open for 57% of the time, Pallas kernels for 28%

profile of v5, /device:TPU:0, one launch (start us, length us, event | category | flops | bytes accessed | tf_op | source)
XLA Modules:
  0.0 1274.3 jit_solution(12740844159910754970)
XLA Ops:
  9.6 5.1 fusion.20
  14.7 10.5 fusion.18
  30.8 3.1 slice.79
  34.0 5.6 fusion.129
  39.7 5.4 fusion.128
  51.1 22.4 %pick_columns.1 = bf16[4096,3072]{1,0:T(8,128)(2,1)} custom-call(s32[1]{0:T(128)} %bitcast.core_ref, bf16[4096,6144]{1,0:T(8,128)(2,1)} %weight_ref.3, bf16[4096,6144]{1,0:T(8,128)(2,1)} %weight_ref.3, bf16[4096,6144]{1,0:T(8,128)(2,1)} %weight_ref.3), custom_call_target="tpu_custom_call" | custom-call | flops 402653184 | bytes 50331648 | tf_op jit(solution)/shard_map/pick_columns/pallas_call | solution.py:356
  75.0 8.0 pick_rows.1
  83.0 5.9 copy-done
  90.9 7.1 fusion.130
  98.0 4.0 copy-done.1
  102.1 20.9 %convert_bitcast_fusion.grad_ref = bf16[8,2,64,2048]{3,2,1,0:T(8,128)(2,1)} fusion(bf16[8,2,64,4096]{3,2,1,0:T(8,128)(2,1)} %bitcast.150, bf16[2048,4096]{1,0:T(8,128)(2,1)S(1)} %copy-done.1), kind=kOutput, calls=%fused_computation.74 | convolution fusion | flops 17181966336 | bytes 29360128 | tf_op jit(solution)/shard_map/tbsd,ed->tbse/dot_general | solution.py:469
  122.9 33.0 %fusion.64.qkv_ref = bf16[8,2,64,3072]{3,2,1,0:T(8,128)(2,1)} fusion(bf16[8,2,64,4096]{3,2,1,0:T(8,128)(2,1)} %bitcast.170, bf16[4096,3072]{1,0:T(8,128)(2,1)} %pick_columns.1), kind=kOutput, calls=%fused_computation.62 | convolution fusion | flops 25772949504 | bytes 39845888 | tf_op jit(solution)/shard_map/tbsd,de->tbse/dot_general | solution.py:466
  155.9 25.4 %attention_0.1 = (bf16[8,2,64,2048]{3,2,1,0:T(8,128)(2,1)}, bf16[8,2,64,3072]{3,2,1,0:T(8,128)(2,1)}) custom-call(bf16[8,2,64,3072]{3,2,1,0:T(8,128)(2,1)} %fusion.64.qkv_ref, bf16[8,2,64,2048]{3,2,1,0:T(8,128)(2,1)} %convert_bitcast_fusion.grad_ref, f32[512,128]{1,0:T(8,128)} %get-tuple-element.110.cos_ref, f32[512,128]{1,0:T(8,128)} %get-tuple-element.111.sin_ref), custom_call_target="tpu_custom_call" | custom-call | flops 12884901888 | bytes 20971520 | tf_op jit(solution)/shard_map/attention_0/pallas_call | solution.py:156
  181.3 5.7 fusion.85
  187.1 5.8 fusion.82
  192.8 28.5 %convolution_bitcast_fusion = f32[3328,3072]{1,0:T(8,128)} fusion(bf16[8,2,64,3072]{3,2,1,0:T(8,128)(2,1)S(1)} %bitcast.148, bf16[8,2,64,4096]{3,2,1,0:T(8,128)(2,1)} %bitcast.171), kind=kOutput, calls=%fused_computation.3 | convolution fusion | flops 20937965568 | bytes 54001664 | tf_op jit(solution)/shard_map/tbsd,tbse->de/dot_general | solution.py:515
  221.3 4.3 convolution_bitcast_fusion.1
  225.7 61.7 %fusion.53.qkv_ref = bf16[8,4,64,3072]{3,2,1,0:T(8,128)(2,1)} fusion(bf16[8,4,64,4096]{3,2,1,0:T(8,128)(2,1)} %bitcast.164, bf16[4096,3072]{1,0:T(8,128)(2,1)} %pick_columns.1), kind=kOutput, calls=%fused_computation.57 | convolution fusion | flops 51545899008 | bytes 54525952 | tf_op jit(solution)/shard_map/tbsd,de->tbse/dot_general | solution.py:466
  287.3 42.7 %fusion.67.grad_ref = bf16[8,4,64,2048]{3,2,1,0:T(8,128)(2,1)} fusion(bf16[8,4,64,4096]{3,2,1,0:T(8,128)(2,1)} %bitcast.167, bf16[2048,4096]{1,0:T(8,128)(2,1)} %copy-done), kind=kOutput, calls=%fused_computation.63 | convolution fusion | flops 34363932672 | bytes 41943040 | tf_op jit(solution)/shard_map/tbsd,ed->tbse/dot_general | solution.py:469
  330.0 47.0 %attention_1.1 = (bf16[8,4,64,2048]{3,2,1,0:T(8,128)(2,1)}, bf16[8,4,64,3072]{3,2,1,0:T(8,128)(2,1)}) custom-call(bf16[8,4,64,3072]{3,2,1,0:T(8,128)(2,1)} %fusion.53.qkv_ref, bf16[8,4,64,2048]{3,2,1,0:T(8,128)(2,1)} %fusion.67.grad_ref, f32[512,128]{1,0:T(8,128)} %get-tuple-element.110.cos_ref, f32[512,128]{1,0:T(8,128)} %get-tuple-element.111.sin_ref), custom_call_target="tpu_custom_call" | custom-call | flops 25769803776 | bytes 41943040 | tf_op jit(solution)/shard_map/attention_1/pallas_call | solution.py:156
  377.1 10.8 bitcast_add_fusion.7
  387.9 10.8 bitcast_add_fusion.8
  398.6 7.0 bitcast_add_fusion.11
  405.6 74.6 %fusion.43.qkv_ref = bf16[8,5,64,3072]{3,2,1,0:T(8,128)(2,1)} fusion(bf16[8,5,64,4096]{3,2,1,0:T(8,128)(2,1)} %bitcast.151, bf16[4096,3072]{1,0:T(8,128)(2,1)} %pick_columns.1), kind=kOutput, calls=%fused_computation.51 | convolution fusion | flops 64432373760 | bytes 61865984 | tf_op jit(solution)/shard_map/tbsd,de->tbse/dot_general | solution.py:466
  480.2 10.4 all-gather.35.cloned.1.call-done
  490.6 52.8 %fusion.58.grad_ref = bf16[8,5,64,2048]{3,2,1,0:T(8,128)(2,1)} fusion(bf16[8,5,64,4096]{3,2,1,0:T(8,128)(2,1)} %bitcast.160, bf16[2048,4096]{1,0:T(8,128)(2,1)} %copy-done), kind=kOutput, calls=%fused_computation.60 | convolution fusion | flops 42954915840 | bytes 48234496 | tf_op jit(solution)/shard_map/tbsd,ed->tbse/dot_general | solution.py:469
  543.4 57.8 %attention_2.1 = (bf16[8,5,64,2048]{3,2,1,0:T(8,128)(2,1)}, bf16[8,5,64,3072]{3,2,1,0:T(8,128)(2,1)}) custom-call(bf16[8,5,64,3072]{3,2,1,0:T(8,128)(2,1)} %fusion.43.qkv_ref, bf16[8,5,64,2048]{3,2,1,0:T(8,128)(2,1)} %fusion.58.grad_ref, f32[512,128]{1,0:T(8,128)} %get-tuple-element.110.cos_ref, f32[512,128]{1,0:T(8,128)} %get-tuple-element.111.sin_ref), custom_call_target="tpu_custom_call" | custom-call | flops 32212254720 | bytes 52428800 | tf_op jit(solution)/shard_map/attention_2/pallas_call | solution.py:156
  601.3 8.2 bitcast_add_fusion.10
  609.5 9.7 bitcast_add_fusion.5
  619.3 9.6 bitcast_add_fusion.6
  628.9 74.6 %fusion.46.qkv_ref = bf16[8,5,64,3072]{3,2,1,0:T(8,128)(2,1)} fusion(bf16[8,5,64,4096]{3,2,1,0:T(8,128)(2,1)} %bitcast.154, bf16[4096,3072]{1,0:T(8,128)(2,1)} %pick_columns.1), kind=kOutput, calls=%fused_computation.52 | convolution fusion | flops 64432373760 | bytes 61865984 | tf_op jit(solution)/shard_map/tbsd,de->tbse/dot_general | solution.py:466
  703.5 52.8 %fusion.61.grad_ref = bf16[8,5,64,2048]{3,2,1,0:T(8,128)(2,1)} fusion(bf16[8,5,64,4096]{3,2,1,0:T(8,128)(2,1)} %bitcast.157, bf16[2048,4096]{1,0:T(8,128)(2,1)} %copy-done), kind=kOutput, calls=%fused_computation.61 | convolution fusion | flops 42954915840 | bytes 48234496 | tf_op jit(solution)/shard_map/tbsd,ed->tbse/dot_general | solution.py:469
  756.3 57.7 %attention_3.1 = (bf16[8,5,64,2048]{3,2,1,0:T(8,128)(2,1)}, bf16[8,5,64,3072]{3,2,1,0:T(8,128)(2,1)}) custom-call(bf16[8,5,64,3072]{3,2,1,0:T(8,128)(2,1)} %fusion.46.qkv_ref, bf16[8,5,64,2048]{3,2,1,0:T(8,128)(2,1)} %fusion.61.grad_ref, f32[512,128]{1,0:T(8,128)} %get-tuple-element.110.cos_ref, f32[512,128]{1,0:T(8,128)} %get-tuple-element.111.sin_ref), custom_call_target="tpu_custom_call" | custom-call | flops 32212254720 | bytes 52428800 | tf_op jit(solution)/shard_map/attention_3/pallas_call | solution.py:156
  815.9 8.9 bitcast_add_fusion.9
  824.8 10.3 bitcast_add_fusion.4
  836.4 52.4 %fusion.32 = f32[3328,3072,1,1]{1,0,3,2:T(8,128)} fusion(bf16[8,4,64,3072]{3,2,1,0:T(8,128)(2,1)} %get-tuple-element.66.refs_1_.refs_5_, bf16[8,4,64,4096]{3,2,1,0:T(8,128)(2,1)} %bitcast.166), kind=kOutput, calls=%fused_computation.40 | convolution fusion | flops 41875931136 | bytes 67108864 | tf_op jit(solution)/shard_map/tbsd,tbse->de/dot_general | solution.py:515
  888.8 7.6 pick_attention.1
  896.5 10.5 pick_gradient.1
  907.4 62.7 %fusion.13 = f32[3328,3072,1,1]{1,0,3,2:T(8,128)} fusion(bf16[8,5,64,3072]{3,2,1,0:T(8,128)(2,1)} %get-tuple-element.75.refs_2_.refs_6_, bf16[8,5,64,4096]{3,2,1,0:T(8,128)(2,1)} %bitcast.153), kind=kOutput, calls=%fused_computation.21 | convolution fusion | flops 52344913920 | bytes 73662464 | tf_op jit(solution)/shard_map/tbsd,tbse->de/dot_general | solution.py:515
  970.0 10.3 bitcast_add_fusion.3
  980.3 75.5 %bitcast_add_fusion.mine_ref = f32[3328,3072]{1,0:T(8,128)} fusion(f32[3328,3072,1,1]{1,0,3,2:T(8,128)} %fusion.13, f32[3328,3072]{1,0:T(8,128)} %convolution_bitcast_fusion, f32[3328,3072,1,1]{1,0,3,2:T(8,128)} %fusion.32, bf16[8,5,64,3072]{3,2,1,0:T(8,128)(2,1)} %get-tuple-element.93.refs_3_.refs_7_, bf16[8,5,64,4096]{3,2,1,0:T(8,128)(2,1)} %bitcast.156), kind=kOutput, calls=%fused_computation | convolution fusion | flops 52375584768 | bytes 196345856 | tf_op jit(solution)/shard_map/tbsd,tbse->de/dot_general | solution.py:515
  1058.4 7.5 join_attention.1.attn_ref
  1065.9 9.0 join_gradient.1.grad_ref
  1074.8 48.1 %output_and_copy.1 = (bf16[1024,4096]{1,0:T(8,128)(2,1)}, f32[4096,4096]{1,0:T(8,128)}) custom-call(bf16[1024,4096]{1,0:T(8,128)(2,1)} %join_attention.1.attn_ref, bf16[4096,4096]{1,0:T(8,128)(2,1)} %weight_ref.2, bf16[1024,4096]{1,0:T(8,128)(2,1)} %bitcast.145, f32[4096,2048]{1,0:T(8,128)} %all-gather.21.cloned.1.call-done.half_ref), custom_call_target="tpu_custom_call" | custom-call | flops 34359738368 | bytes 109051904 | tf_op jit(solution)/shard_map/output_and_copy/pallas_call | solution.py:301
  1123.0 91.2 %project_and_join.1 = (bf16[1024,4096]{1,0:T(8,128)(2,1)}, f32[4096,6144]{1,0:T(8,128)}) custom-call(s32[1]{0:T(128)} %bitcast.core_ref, bf16[1024,6144]{1,0:T(8,128)(2,1)} %join_gradient.1.grad_ref, bf16[4096,6144]{1,0:T(8,128)(2,1)} %weight_ref.3, f32[3328,3072]{1,0:T(8,128)} %bitcast_add_fusion.mine_ref, f32[3328,3072]{1,0:T(8,128)} %collective-permute-done.5.other_ref, ...), custom_call_target="tpu_custom_call" | custom-call | flops 51539607552 | bytes 264241152 | tf_op jit(solution)/shard_map/project_and_join/pallas_call | solution.py:266
  1214.2 12.9 %fusion.21 = (f32[4096]{0:T(1024)S(1)}, f32[16,64]{1,0:T(8,128)S(1)}) fusion(bf16[16,64,4096]{2,1,0:T(8,128)(2,1)} %param.7, f32[16,64]{1,0:T(8,128)S(1)} %copy-done.12, bf16[1024,4096]{1,0:T(8,128)(2,1)} %get-tuple-element.95, f32[4096]{0:T(1024)S(1)} %copy-done.10, bf16[16,64,4096]{2,1,0:T(8,128)(2,1)} %bitcast.146), kind=kLoop, calls=%fused_computation.29 | loop fusion | flops 37743616 | bytes 25206784 | tf_op jit(solution)/shard_map/reduce_sum | solution.py:537
  1229.9 12.2 fusion.17
  1243.6 23.4 %second_half.1 = f32[4096,4096]{1,0:T(8,128)} custom-call(f32[4096,4096]{1,0:T(8,128)} %get-tuple-element.97.left_ref, f32[4096,2048]{1,0:T(8,128)} %all-gather.23.cloned.1.call-done.half_ref), custom_call_target="tpu_custom_call", output_to_operand_aliasing={{}: (0, {})} | custom-call | flops 268435456 | bytes 67108864 | tf_op jit(solution)/shard_map/second_half/pallas_call | solution.py:329
  (120 shorter events, 28.7 us)
Async XLA Ops:
  7.2 7.5 copy-start.9
  7.2 83.7 %all-gather.25.cloned.1.call-start = ((), (), s32[]{:S(2)}) async-start(), calls=%async_computation.2 | async-start | bytes 9437184 | tf_op jit(solution)/shard_map/all_gather | solution.py:462
  9.5 113.4 %all-gather.27.cloned.1.call-start = ((), (), s32[]{:S(2)}) async-start(), calls=%async_computation.3 | async-start | bytes 9437184 | tf_op jit(solution)/shard_map/all_gather | solution.py:461
  14.7 10.5 copy-start.11
  27.6 198.1 %all-gather.29.cloned.1.call-start = ((), (), s32[]{:S(2)}) async-start(), calls=%async_computation.4 | async-start | bytes 18874368 | tf_op jit(solution)/shard_map/all_gather | solution.py:461
  30.8 256.6 %all-gather.31.cloned.1.call-start = ((), (), s32[]{:S(2)}) async-start(), calls=%async_computation.5 | async-start | bytes 18874368 | tf_op jit(solution)/shard_map/all_gather | solution.py:462
  34.0 371.7 %all-gather.33.cloned.1.call-start = ((), (), s32[]{:S(2)}) async-start(), calls=%async_computation.6 | async-start | bytes 23592960 | tf_op jit(solution)/shard_map/all_gather | solution.py:461
  39.6 6.4 copy-start.13
  39.6 7.5 copy-start.14
  39.6 451.0 %all-gather.35.cloned.1.call-start = ((), (), s32[]{:S(2)}) async-start(), calls=%async_computation.7 | async-start | bytes 23592960 | tf_op jit(solution)/shard_map/all_gather | solution.py:462
  45.2 556.1 %all-gather.37.cloned.1.call-start = ((), (), s32[]{:S(2)}) async-start(), calls=%async_computation.8 | async-start | bytes 23592960 | tf_op jit(solution)/shard_map/all_gather | solution.py:461
  45.9 657.6 %all-gather.39.cloned.1.call-start = ((), (), s32[]{:S(2)}) async-start(), calls=%async_computation.9 | async-start | bytes 23592960 | tf_op jit(solution)/shard_map/all_gather | solution.py:462
  46.2 1.7 collective-permute-start
  47.1 1027.7 %all-gather.21.cloned.1.call-start = ((), (), s32[]{:S(2)}) async-start(), calls=%async_computation | async-start | bytes 37748736 | tf_op jit(solution)/shard_map/all_gather | solution.py:520
  48.2 25.2 %collective-permute-start.1 = (s32[512]{0:T(512)S(1)}, s32[512]{0:T(512)S(1)}, u32[]{:S(2)}, u32[]{:S(2)}) collective-permute-start(s32[512]{0:T(512)S(1)} %add_dynamic-update-slice_fusion), channel_id=1, source_target_pairs={{0,2},{1,3},{2,0},{3,1},{4,6},{5,7},{6,4},{7,5}} | collective-permute-start | bytes 6152 | tf_op jit(solution)/shard_map/ppermute | solution.py:428
  73.5 15.4 %collective-permute-start.2 = (s32[512]{0:T(512)S(1)}, s32[512]{0:T(512)S(1)}, u32[]{:S(2)}, u32[]{:S(2)}) collective-permute-start(s32[512]{0:T(512)S(1)} %add.92), channel_id=1, source_target_pairs={{0,4},{1,5},{2,6},{3,7},{4,0},{5,1},{6,2},{7,3}} | collective-permute-start | bytes 6152 | tf_op jit(solution)/shard_map/ppermute | solution.py:428
  83.0 5.9 copy-start
  90.9 11.1 copy-start.1
  155.9 25.4 %copy-start.6 = (bf16[8,2,64,2048]{3,2,1,0:T(8,128)(2,1)S(1)}, bf16[8,2,64,2048]{3,2,1,0:T(8,128)(2,1)}, u32[]{:S(2)}) copy-start(bf16[8,2,64,2048]{3,2,1,0:T(8,128)(2,1)} %get-tuple-element.105) | copy-start | bytes 12582916
  181.3 5.8 copy-start.5
  181.3 11.5 slice-start.2
  187.1 5.8 slice-start.3
  330.0 47.0 %copy-start.18 = (f32[512,2048]{1,0:T(8,128)S(1)}, f32[512,2048]{1,0:T(8,128)}, u32[]{:S(2)}) copy-start(f32[512,2048]{1,0:T(8,128)} %fusion.85) | copy-start | bytes 12582916
  377.0 10.8 copy-start.19
  387.9 10.8 copy-start.17
  543.4 57.9 %copy-start.20 = (f32[768,768]{1,0:T(8,128)S(1)}, f32[768,768]{1,0:T(8,128)}, u32[]{:S(2)}) copy-start(f32[768,768]{1,0:T(8,128)} %bitcast_add_fusion.11) | copy-start | bytes 7077892
  601.3 8.2 copy-start.4
  601.3 8.2 copy-start.16
  609.5 9.8 copy-start.15
  756.3 59.6 %copy-start.21 = (f32[768,768]{1,0:T(8,128)S(1)}, f32[768,768]{1,0:T(8,128)}, u32[]{:S(2)}) copy-start(f32[768,768]{1,0:T(8,128)} %bitcast_add_fusion.10) | copy-start | bytes 7077892
  815.9 9.0 copy-start.7
  835.1 287.8 %all-gather.41.cloned.1.call-start = ((), (), s32[]{:S(2)}) async-start(), calls=%async_computation.10 | async-start | bytes 21233664 | tf_op jit(solution)/shard_map/all_gather | solution.py:519
  835.7 407.8 %all-gather.23.cloned.1.call-start = ((), (), s32[]{:S(2)}) async-start(), calls=%async_computation.1 | async-start | bytes 37748736 | tf_op jit(solution)/shard_map/all_gather | solution.py:520
  896.3 84.0 %collective-permute-start.3 = (bf16[16,64,2048]{2,1,0:T(8,128)(2,1)}, bf16[16,64,2048]{2,1,0:T(8,128)(2,1)}, u32[]{:S(2)}, u32[]{:S(2)}) collective-permute-start(bf16[16,64,2048]{2,1,0:T(8,128)(2,1)} %get-tuple-element.80), channel_id=1, source_target_pairs={{0,1},{1,0},{2,3},{3,2},{4,5},{5,4},{6,7},{7,6}} | collective-permute-start | bytes 12582920 | tf_op jit(solution)/shard_map/ppermute | solution.py:513
  907.1 63.0 %copy-start.8 = (bf16[8,5,64,512]{3,2,1,0:T(8,128)(2,1)S(1)}, bf16[8,5,64,512]{3,2,1,0:T(8,128)(2,1)}, u32[]{:S(2)}) copy-start(bf16[8,5,64,512]{3,2,1,0:T(8,128)(2,1)} %copy-done.7) | copy-start | bytes 7864324
  907.1 73.3 %collective-permute-start.4 = (bf16[16,64,3072]{2,1,0:T(8,128)(2,1)}, bf16[16,64,3072]{2,1,0:T(8,128)(2,1)}, u32[]{:S(2)}, u32[]{:S(2)}) collective-permute-start(bf16[16,64,3072]{2,1,0:T(8,128)(2,1)} %get-tuple-element.82), channel_id=1, source_target_pairs={{0,1},{1,0},{2,3},{3,2},{4,5},{5,4},{6,7},{7,6}} | collective-permute-start | bytes 18874376 | tf_op jit(solution)/shard_map/ppermute | solution.py:513
  1055.9 10.0 slice-start
  1055.9 67.1 %collective-permute-start.5 = (f32[3328,3072]{1,0:T(8,128)}, f32[3328,3072]{1,0:T(8,128)}, u32[]{:S(2)}, u32[]{:S(2)}) collective-permute-start(f32[3328,3072]{1,0:T(8,128)} %bitcast_add_fusion.mine_ref), channel_id=1, source_target_pairs={{0,1},{1,0},{2,3},{3,2},{4,5},{5,4},{6,7},{7,6}} | collective-permute-start | bytes 122683400 | tf_op jit(solution)/shard_map/ppermute | solution.py:518
  1056.1 2.3 copy-start.2
  1058.4 7.5 slice-start.1
  1122.9 91.3 %copy-start.10 = (f32[4096]{0:T(1024)S(1)}, f32[4096]{0:T(1024)}, u32[]{:S(2)}) copy-start(f32[4096]{0:T(1024)} %param.10) | copy-start | bytes 49156
  1123.0 91.3 %copy-start.12 = (f32[16,64]{1,0:T(8,128)S(1)}, f32[16,64]{1,0:T(8,128)}, u32[]{:S(2)}) copy-start(f32[16,64]{1,0:T(8,128)} %copy-done.11) | copy-start | bytes 12292
  1214.2 15.7 %copy-start.3 = (bf16[1024,4096]{1,0:T(8,128)(2,1)S(1)}, bf16[1024,4096]{1,0:T(8,128)(2,1)}, u32[]{:S(2)}) copy-start(bf16[1024,4096]{1,0:T(8,128)(2,1)} %get-tuple-element.95) | copy-start | bytes 25165828
  1227.1 1.2 collective-permute-start.6
  1228.3 13.8 %collective-permute-start.7 = (f32[4096]{0:T(1024)S(1)}, f32[4096]{0:T(1024)S(1)}, u32[]{:S(2)}, u32[]{:S(2)}) collective-permute-start(f32[4096]{0:T(1024)S(1)} %add.108), channel_id=1, source_target_pairs={{0,2},{1,3},{2,0},{3,1},{4,6},{5,7},{6,4},{7,5}} | collective-permute-start | bytes 49160 | tf_op jit(solution)/shard_map/ppermute | solution.py:428
  1242.1 24.8 %collective-permute-start.8 = (f32[4096]{0:T(1024)S(1)}, f32[4096]{0:T(1024)S(1)}, u32[]{:S(2)}, u32[]{:S(2)}) collective-permute-start(f32[4096]{0:T(1024)S(1)} %add.109), channel_id=1, source_target_pairs={{0,4},{1,5},{2,6},{3,7},{4,0},{5,1},{6,2},{7,3}} | collective-permute-start | bytes 49160 | tf_op jit(solution)/shard_map/ppermute | solution.py:428
Sparse Core Ops, SparseCore 0:
  10.4 51.1 all-gather.24
  63.4 48.3 all-gather.26
  113.6 84.0 all-gather.28
  199.4 84.0 all-gather.30
  285.2 101.8 all-gather.32
  388.7 101.8 all-gather.34
  492.4 101.8 all-gather.36
  596.2 101.8 all-gather.38
  835.3 155.2 all-gather.20
  992.2 94.2 all-gather.40
  1088.3 155.1 all-gather.22
